TPU v7x, 8 devices: a whole 2x2x1 slice. The times are simulated.
8 devices in a mesh: dp: 2 (over z, y), sp: 4 (over x, core).
Axes of the slice: x: 2, y: 2, z: 1, core: 2. Of those that a mesh axis runs over, the one named last changes fastest.
Arguments:
- x: bfloat16 [32, 1024, 768], P('dp', 'sp'), parts along dimension 0
- g: bfloat16 [32, 1024, 768], P('dp', 'sp'), parts along dimension 0
- ln_g: float32 [768], replicated
- ln_b: float32 [768], replicated
- w_qkv: bfloat16 [768, 3, 12, 64], replicated
- b_qkv: float32 [3, 12, 64], replicated
- w_out: bfloat16 [12, 64, 768], replicated
- b_out: float32 [768], replicated
Outputs:
- output 1: bfloat16 [32, 1024, 768], P('dp', 'sp'), parts along dimension 0
- output 2: bfloat16 [32, 1024, 768], P('dp', 'sp'), parts along dimension 0
- output 3: float32 [1536], P('dp'), parts along dimension 0
- output 4: float32 [1536], P('dp'), parts along dimension 0
- output 5: float32 [1536, 3, 12, 64], P('dp'), parts along dimension 0
- output 6: float32 [6, 12, 64], P('dp'), parts along dimension 0
- output 7: float32 [24, 64, 768], P('dp'), parts along dimension 0
- output 8: float32 [1536], P('dp'), parts along dimension 0
There are 2 independent parts. A program takes and returns all parts, laid end to end along the dimension named above; an argument that names none is the same for every part.
All inputs are finite; a program needn't handle non-finite values.
Results may differ from a plain program's by a relative error of at most 0.00827913.
Values are sent between devices in bfloat16 or wider.
A program may use at most 1 GiB of HBM per device.

v0:
```python
import jax
import jax.numpy as jnp
from jax import lax
from jax.sharding import PartitionSpec as P

LN_EPS = 1e-5


def layer_norm(x_in):
    x_f = x_in.astype(jnp.float32)
    centred = x_f - jnp.mean(x_f, axis=-1, keepdims=True)
    inv_std = lax.rsqrt(jnp.mean(centred * centred, axis=-1, keepdims=True) + LN_EPS)
    return centred * inv_std, inv_std


def block_probs(q_rows, keys, row_start):
    scale = q_rows.shape[-1] ** -0.5
    scores = jnp.einsum('bqhe,bkhe->bhqk', q_rows, keys, preferred_element_type=jnp.float32) * scale
    row_pos = row_start + jnp.arange(q_rows.shape[1])
    col_pos = jnp.arange(keys.shape[1])
    scores = jnp.where(col_pos[None, :] <= row_pos[:, None], scores, -jnp.inf)
    return jax.nn.softmax(scores, axis=-1)


def attend(query, keys, values, q_offset, block_rows):
    def one_block(block_idx):
        row_start = block_idx * block_rows
        q_rows = lax.dynamic_slice_in_dim(query, row_start, block_rows, axis=1)
        attn_prob = block_probs(q_rows, keys, q_offset + row_start).astype(jnp.bfloat16)
        return jnp.einsum('bhqk,bkhe->bqhe', attn_prob, values, preferred_element_type=jnp.float32).astype(jnp.bfloat16)
    out_blocks = lax.map(one_block, jnp.arange(query.shape[1] // block_rows))
    return jnp.moveaxis(out_blocks, 0, 1).reshape(query.shape)


def attend_grad(query, keys, values, d_out, q_offset, block_rows):
    scale = query.shape[-1] ** -0.5
    def step(acc_pair, block_idx):
        key_grad, value_grad = acc_pair
        row_start = block_idx * block_rows
        q_rows = lax.dynamic_slice_in_dim(query, row_start, block_rows, axis=1)
        d_rows = lax.dynamic_slice_in_dim(d_out, row_start, block_rows, axis=1)
        attn_prob = block_probs(q_rows, keys, q_offset + row_start)
        d_prob = jnp.einsum('bqhe,bkhe->bhqk', d_rows, values, preferred_element_type=jnp.float32)
        row_dot = jnp.sum(attn_prob * d_prob, axis=-1, keepdims=True)
        d_score = (attn_prob * (d_prob - row_dot) * scale).astype(jnp.bfloat16)
        q_grad = jnp.einsum('bhqk,bkhe->bqhe', d_score, keys, preferred_element_type=jnp.float32).astype(jnp.bfloat16)
        key_grad = key_grad + jnp.einsum('bhqk,bqhe->bkhe', d_score, q_rows, preferred_element_type=jnp.float32)
        value_grad = value_grad + jnp.einsum('bhqk,bqhe->bkhe', attn_prob.astype(jnp.bfloat16), d_rows, preferred_element_type=jnp.float32)
        return (key_grad, value_grad), q_grad
    zeros = jnp.zeros(keys.shape, jnp.float32)
    (key_grad, value_grad), q_blocks = lax.scan(step, (zeros, zeros), jnp.arange(query.shape[1] // block_rows))
    return jnp.moveaxis(q_blocks, 0, 1).reshape(query.shape), key_grad, value_grad


def solution(mesh):
    tok_spec = P('dp', 'sp', None)
    rep_spec = P()
    part_spec = P('dp')

    def local_step(x, g, ln_g, ln_b, w_qkv, b_qkv, w_out, b_out):
        x_hat, inv_std = layer_norm(x)
        hidden = (x_hat * ln_g + ln_b).astype(jnp.bfloat16)
        proj_qkv = (jnp.einsum('bsd,dthe->bsthe', hidden, w_qkv, preferred_element_type=jnp.float32) + b_qkv).astype(jnp.bfloat16)
        head_qkv = lax.all_to_all(proj_qkv, 'sp', 3, 1, tiled=True)
        query = head_qkv[:, :, 0]
        keys = head_qkv[:, :, 1]
        values = head_qkv[:, :, 2]
        block_rows = min(query.shape[1], 256)
        head_out = attend(query, keys, values, 0, block_rows)
        attn_out = lax.all_to_all(head_out, 'sp', 1, 2, tiled=True)
        out_proj = jnp.einsum('bshe,hed->bsd', attn_out, w_out, preferred_element_type=jnp.float32) + b_out
        y = (x.astype(jnp.float32) + out_proj).astype(jnp.bfloat16)

        d_b_out = jnp.sum(g, axis=(0, 1), dtype=jnp.float32)
        d_w_out = jnp.einsum('bshe,bsd->hed', attn_out, g, preferred_element_type=jnp.float32)
        d_attn = jnp.einsum('bsd,hed->bshe', g, w_out, preferred_element_type=jnp.float32).astype(jnp.bfloat16)
        d_head_out = lax.all_to_all(d_attn, 'sp', 2, 1, tiled=True)
        d_query, key_grad, value_grad = attend_grad(query, keys, values, d_head_out, 0, block_rows)
        d_heads = jnp.stack([d_query, key_grad.astype(jnp.bfloat16), value_grad.astype(jnp.bfloat16)], axis=2)
        d_qkv = lax.all_to_all(d_heads, 'sp', 1, 3, tiled=True)
        d_b_qkv = jnp.sum(d_qkv, axis=(0, 1), dtype=jnp.float32)
        d_w_qkv = jnp.einsum('bsd,bsthe->dthe', hidden, d_qkv, preferred_element_type=jnp.float32)
        d_hidden = jnp.einsum('bsthe,dthe->bsd', d_qkv, w_qkv, preferred_element_type=jnp.float32)
        d_ln_g = jnp.sum(d_hidden * x_hat, axis=(0, 1))
        d_ln_b = jnp.sum(d_hidden, axis=(0, 1))
        d_norm = d_hidden * ln_g
        d_norm_in = inv_std * (d_norm - jnp.mean(d_norm, axis=-1, keepdims=True) - x_hat * jnp.mean(d_norm * x_hat, axis=-1, keepdims=True))
        d_x = (g.astype(jnp.float32) + d_norm_in).astype(jnp.bfloat16)
        grads = lax.psum((d_ln_g, d_ln_b, d_w_qkv, d_b_qkv, d_w_out, d_b_out), 'sp')
        return (y, d_x) + tuple(grads)

    return jax.shard_map(local_step, mesh=mesh, in_specs=(tok_spec, tok_spec) + (rep_spec,) * 6, out_specs=(tok_spec, tok_spec) + (part_spec,) * 6, check_vma=False)
```

profile of v0, /device:TPU:0, one launch (start us, length us, event | category | flops | bytes accessed | tf_op | source)
XLA Modules:
  0.0 2266.2 jit_solution(15781768029094937552)
XLA Ops:
  7.2 7.7 fusion.100
  32.7 21.3 add_convert_fusion
  53.9 17.0 copy.46
  70.9 24.1 %all-to-all-done.2 = bf16[16,256,12,64]{1,3,0,2:T(8,128)(2,1)} async-done(((bf16[16,256,12,64]{1,3,0,2:T(8,128)(2,1)}), bf16[16,256,12,64]{1,3,0,2:T(8,128)(2,1)}, u32[]{:S(2)}, u32[]{:S(2)}) %all-to-all-start.2) | async-done | bytes 6291488 | tf_op jit(solution)/shard_map/all_to_all | solution.py:77
  95.0 7.6 all-to-all-start
  102.7 11.6 copy.53
  114.3 11.0 all_to_all.63
  125.3 182.5 %all-to-all-done = bf16[16,256,3,12,64]{1,4,2,0,3:T(8,128)(2,1)} async-done(((bf16[16,256,3,12,64]{1,4,2,0,3:T(8,128)(2,1)}), bf16[16,256,3,12,64]{1,4,2,0,3:T(8,128)(2,1)}, u32[]{:S(2)}, u32[]{:S(2)}) %all-to-all-start) | async-done | bytes 18874400 | tf_op jit(solution)/shard_map/all_to_all | solution.py:64
  307.8 24.8 %copy.47 = bf16[16,4,256,3,3,64]{2,1,5,4,0,3:T(4,128)(2,1)} copy(bf16[16,4,256,3,3,64]{2,5,3,0,4,1:T(8,128)(2,1)} %bitcast.7) | data formatting | bytes 37748736 | tf_op jit(solution)/shard_map/all_to_all | solution.py:64
  332.6 30.7 %all_to_all.55 = bf16[16,1024,3,3,64]{1,4,3,0,2:T(8,128)(2,1)} reshape(bf16[16,4,256,3,3,64]{2,1,5,4,0,3:T(4,128)(2,1)} %copy.47) | data formatting | bytes 37748736 | tf_op jit(solution)/shard_map/all_to_all | solution.py:64
  363.3 15.4 slice_bitcast_fusion
  382.2 193.1 %while.25 = (s32[]{:T(128)}, bf16[4,16,256,3,64]{2,4,3,1,0:T(8,128)(2,1)}, s32[4]{0:T(128)S(1)}, bf16[16,1024,3,64]{1,3,2,0:T(8,128)(2,1)}, bf16[16,1024,3,64]{1...) while((s32[]{:T(128)}, ...), condition=%wide.region_5.6_spmd, body=%wide.region_2.5_spmd.sunk | while | flops 3297772800 | bytes 117033640 | solution.py:31
  384.8 24.7 %fusion.159 = (f32[16,3,256]{2,1,0:T(4,128)}, f32[16,3,256,1024]{3,2,1,0:T(8,128)}) fusion(pred[256,1024]{1,0:T(8,128)(4,1)} %iota_compare_fusion.4, bf16[16,1024,3,64]{1,3,2,0:T(8,128)(2,1)} %get-tuple-element.323, bf16[16,1024,3,64]{1,3,2,0:T(8,128)(2,1)} %get-tuple-element.322, s32[]{:T(128)S(6)} %select_n.41), kind=kOutput, calls=%fused_computation.114.clone.1 | convolution fusion | flops 1660945408 | bytes 58507268 | tf_op jit(solution)/shard_map/while/body/eval_jaxpr/sub | solution.py:22
  409.5 21.3 bitcast_dynamic-update-slice_fusion.4
  433.0 24.7 %fusion.159 = (f32[16,3,256]{2,1,0:T(4,128)}, f32[16,3,256,1024]{3,2,1,0:T(8,128)}) fusion(pred[256,1024]{1,0:T(8,128)(4,1)} %iota_compare_fusion.4, bf16[16,1024,3,64]{1,3,2,0:T(8,128)(2,1)} %get-tuple-element.323, bf16[16,1024,3,64]{1,3,2,0:T(8,128)(2,1)} %get-tuple-element.322, s32[]{:T(128)S(6)} %select_n.41), kind=kOutput, calls=%fused_computation.114.clone.1 | convolution fusion | flops 1660945408 | bytes 58507268 | tf_op jit(solution)/shard_map/while/body/eval_jaxpr/sub | solution.py:22
  457.7 21.3 bitcast_dynamic-update-slice_fusion.4
  481.1 24.7 %fusion.159 = (f32[16,3,256]{2,1,0:T(4,128)}, f32[16,3,256,1024]{3,2,1,0:T(8,128)}) fusion(pred[256,1024]{1,0:T(8,128)(4,1)} %iota_compare_fusion.4, bf16[16,1024,3,64]{1,3,2,0:T(8,128)(2,1)} %get-tuple-element.323, bf16[16,1024,3,64]{1,3,2,0:T(8,128)(2,1)} %get-tuple-element.322, s32[]{:T(128)S(6)} %select_n.41), kind=kOutput, calls=%fused_computation.114.clone.1 | convolution fusion | flops 1660945408 | bytes 58507268 | tf_op jit(solution)/shard_map/while/body/eval_jaxpr/sub | solution.py:22
  505.8 21.3 bitcast_dynamic-update-slice_fusion.4
  529.3 24.7 %fusion.159 = (f32[16,3,256]{2,1,0:T(4,128)}, f32[16,3,256,1024]{3,2,1,0:T(8,128)}) fusion(pred[256,1024]{1,0:T(8,128)(4,1)} %iota_compare_fusion.4, bf16[16,1024,3,64]{1,3,2,0:T(8,128)(2,1)} %get-tuple-element.323, bf16[16,1024,3,64]{1,3,2,0:T(8,128)(2,1)} %get-tuple-element.322, s32[]{:T(128)S(6)} %select_n.41), kind=kOutput, calls=%fused_computation.114.clone.1 | convolution fusion | flops 1660945408 | bytes 58507268 | tf_op jit(solution)/shard_map/while/body/eval_jaxpr/sub | solution.py:22
  554.0 21.3 bitcast_dynamic-update-slice_fusion.4
  575.3 15.7 copy.67
  591.0 12.8 reshape.71
  612.5 997.5 %while.26 = (s32[]{:T(128)}, f32[16,1024,3,64]{1,3,2,0:T(8,128)}, f32[16,1024,3,64]{1,3,2,0:T(8,128)}, bf16[4,16,256,3,64]{2,4,3,1,0:T(8,128)(2,1)}, s32[4]{0:T(...) while((s32[]{:T(128)}, f32[16,1024,3,64]{1,3,2,0:T(8,128)}, ...), condition=%wide.region_10.11_spmd.clone, body=%wide.region_6.0_spmd.clone.sunk | while | flops 8318381056 | bytes 631622656 | solution.py:51
  614.8 24.8 %fusion.171 = (f32[16,3,256]{2,1,0:T(4,128)}, f32[16,3,256,1024]{3,2,1,0:T(8,128)}) fusion(pred[256,1024]{1,0:T(8,128)(4,1)} %iota_compare_fusion.5, bf16[16,1024,3,64]{1,3,2,0:T(8,128)(2,1)} %get-tuple-element.361, bf16[16,1024,3,64]{1,3,2,0:T(8,128)(2,1)} %get-tuple-element.360, s32[]{:T(128)S(6)} %select_n.43), kind=kOutput, calls=%fused_computation.115.clone.1 | convolution fusion | flops 1660945408 | bytes 58507268 | tf_op jit(solution)/shard_map/while/body/eval_jaxpr/sub | solution.py:22
  639.6 22.4 fusion.170
  662.0 79.7 %bitcast_dynamic-update-slice_fusion.5 = bf16[4,16,256,3,64]{2,4,3,1,0:T(8,128)(2,1)} fusion(bf16[4,16,256,3,64]{2,4,3,1,0:T(8,128)(2,1)} %get-tuple-element.345, s32[]{:T(128)} %get-tuple-element.342, bf16[16,1024,3,64]{1,3,2,0:T(8,128)(2,1)} %get-tuple-element.361, f32[16,3,256,1024]{3,2,1,0:T(8,128)} %fusion.170, ...), kind=kOutput, calls=%fused_computation.41.clone.1 | convolution fusion | flops 1699492864 | bytes 209322496 | tf_op jit(solution)/shard_map/while/body/eval_jaxpr/bhqk,bkhe->bqhe/dot_general | solution.py:46
  741.7 23.1 %bitcast_add_fusion.6 = f32[16,1024,3,64]{1,3,2,0:T(8,128)} fusion(f32[16,1024,3,64]{1,3,2,0:T(8,128)} %get-tuple-element.344, pred[]{:T(512)S(6)} %compare.3, bf16[16,1024,3,64]{1,3,2,0:T(8,128)(2,1)} %get-tuple-element.362, s32[]{:T(128)S(6)} %select_n.43, f32[16,3,256,1024]{3,2,1,0:T(8,128)} %get-tuple-element.297, ...), kind=kOutput, calls=%fused_computation.37.clone.1 | convolution fusion | flops 1642070016 | bytes 77135880 | tf_op jit(solution)/shard_map/while/body/eval_jaxpr/bhqk,bqhe->bkhe/dot_general | solution.py:48
  764.8 87.6 %bitcast_add_fusion.5 = f32[16,1024,3,64]{1,3,2,0:T(8,128)} fusion(f32[16,1024,3,64]{1,3,2,0:T(8,128)} %get-tuple-element.343, pred[]{:T(512)S(6)} %compare.3, f32[16,3,256,1024]{3,2,1,0:T(8,128)} %fusion.170, bf16[16,1024,3,64]{1,3,2,0:T(8,128)(2,1)} %get-tuple-element.360, s32[]{:T(128)S(6)} %select_n.43, ...), kind=kOutput, calls=%fused_computation.38.clone.2 | convolution fusion | flops 1704997888 | bytes 228196352 | tf_op jit(solution)/shard_map/while/body/eval_jaxpr/bhqk,bqhe->bkhe/dot_general | solution.py:47
  854.6 24.8 %fusion.171 = (f32[16,3,256]{2,1,0:T(4,128)}, f32[16,3,256,1024]{3,2,1,0:T(8,128)}) fusion(pred[256,1024]{1,0:T(8,128)(4,1)} %iota_compare_fusion.5, bf16[16,1024,3,64]{1,3,2,0:T(8,128)(2,1)} %get-tuple-element.361, bf16[16,1024,3,64]{1,3,2,0:T(8,128)(2,1)} %get-tuple-element.360, s32[]{:T(128)S(6)} %select_n.43), kind=kOutput, calls=%fused_computation.115.clone.1 | convolution fusion | flops 1660945408 | bytes 58507268 | tf_op jit(solution)/shard_map/while/body/eval_jaxpr/sub | solution.py:22
  879.3 22.4 fusion.170
  901.8 79.7 %bitcast_dynamic-update-slice_fusion.5 = bf16[4,16,256,3,64]{2,4,3,1,0:T(8,128)(2,1)} fusion(bf16[4,16,256,3,64]{2,4,3,1,0:T(8,128)(2,1)} %get-tuple-element.345, s32[]{:T(128)} %get-tuple-element.342, bf16[16,1024,3,64]{1,3,2,0:T(8,128)(2,1)} %get-tuple-element.361, f32[16,3,256,1024]{3,2,1,0:T(8,128)} %fusion.170, ...), kind=kOutput, calls=%fused_computation.41.clone.1 | convolution fusion | flops 1699492864 | bytes 209322496 | tf_op jit(solution)/shard_map/while/body/eval_jaxpr/bhqk,bkhe->bqhe/dot_general | solution.py:46
  981.5 26.6 %bitcast_add_fusion.6 = f32[16,1024,3,64]{1,3,2,0:T(8,128)} fusion(f32[16,1024,3,64]{1,3,2,0:T(8,128)} %get-tuple-element.344, pred[]{:T(512)S(6)} %compare.3, bf16[16,1024,3,64]{1,3,2,0:T(8,128)(2,1)} %get-tuple-element.362, s32[]{:T(128)S(6)} %select_n.43, f32[16,3,256,1024]{3,2,1,0:T(8,128)} %get-tuple-element.297, ...), kind=kOutput, calls=%fused_computation.37.clone.1 | convolution fusion | flops 1642070016 | bytes 77135880 | tf_op jit(solution)/shard_map/while/body/eval_jaxpr/bhqk,bqhe->bkhe/dot_general | solution.py:48
  1008.1 94.7 %bitcast_add_fusion.5 = f32[16,1024,3,64]{1,3,2,0:T(8,128)} fusion(f32[16,1024,3,64]{1,3,2,0:T(8,128)} %get-tuple-element.343, pred[]{:T(512)S(6)} %compare.3, f32[16,3,256,1024]{3,2,1,0:T(8,128)} %fusion.170, bf16[16,1024,3,64]{1,3,2,0:T(8,128)(2,1)} %get-tuple-element.360, s32[]{:T(128)S(6)} %select_n.43, ...), kind=kOutput, calls=%fused_computation.38.clone.2 | convolution fusion | flops 1704997888 | bytes 228196352 | tf_op jit(solution)/shard_map/while/body/eval_jaxpr/bhqk,bqhe->bkhe/dot_general | solution.py:47
  1105.0 24.8 %fusion.171 = (f32[16,3,256]{2,1,0:T(4,128)}, f32[16,3,256,1024]{3,2,1,0:T(8,128)}) fusion(pred[256,1024]{1,0:T(8,128)(4,1)} %iota_compare_fusion.5, bf16[16,1024,3,64]{1,3,2,0:T(8,128)(2,1)} %get-tuple-element.361, bf16[16,1024,3,64]{1,3,2,0:T(8,128)(2,1)} %get-tuple-element.360, s32[]{:T(128)S(6)} %select_n.43), kind=kOutput, calls=%fused_computation.115.clone.1 | convolution fusion | flops 1660945408 | bytes 58507268 | tf_op jit(solution)/shard_map/while/body/eval_jaxpr/sub | solution.py:22
  1129.8 22.4 fusion.170
  1152.2 79.7 %bitcast_dynamic-update-slice_fusion.5 = bf16[4,16,256,3,64]{2,4,3,1,0:T(8,128)(2,1)} fusion(bf16[4,16,256,3,64]{2,4,3,1,0:T(8,128)(2,1)} %get-tuple-element.345, s32[]{:T(128)} %get-tuple-element.342, bf16[16,1024,3,64]{1,3,2,0:T(8,128)(2,1)} %get-tuple-element.361, f32[16,3,256,1024]{3,2,1,0:T(8,128)} %fusion.170, ...), kind=kOutput, calls=%fused_computation.41.clone.1 | convolution fusion | flops 1699492864 | bytes 209322496 | tf_op jit(solution)/shard_map/while/body/eval_jaxpr/bhqk,bkhe->bqhe/dot_general | solution.py:46
  1231.9 26.6 %bitcast_add_fusion.6 = f32[16,1024,3,64]{1,3,2,0:T(8,128)} fusion(f32[16,1024,3,64]{1,3,2,0:T(8,128)} %get-tuple-element.344, pred[]{:T(512)S(6)} %compare.3, bf16[16,1024,3,64]{1,3,2,0:T(8,128)(2,1)} %get-tuple-element.362, s32[]{:T(128)S(6)} %select_n.43, f32[16,3,256,1024]{3,2,1,0:T(8,128)} %get-tuple-element.297, ...), kind=kOutput, calls=%fused_computation.37.clone.1 | convolution fusion | flops 1642070016 | bytes 77135880 | tf_op jit(solution)/shard_map/while/body/eval_jaxpr/bhqk,bqhe->bkhe/dot_general | solution.py:48
  1258.6 100.5 %bitcast_add_fusion.5 = f32[16,1024,3,64]{1,3,2,0:T(8,128)} fusion(f32[16,1024,3,64]{1,3,2,0:T(8,128)} %get-tuple-element.343, pred[]{:T(512)S(6)} %compare.3, f32[16,3,256,1024]{3,2,1,0:T(8,128)} %fusion.170, bf16[16,1024,3,64]{1,3,2,0:T(8,128)(2,1)} %get-tuple-element.360, s32[]{:T(128)S(6)} %select_n.43, ...), kind=kOutput, calls=%fused_computation.38.clone.2 | convolution fusion | flops 1704997888 | bytes 228196352 | tf_op jit(solution)/shard_map/while/body/eval_jaxpr/bhqk,bqhe->bkhe/dot_general | solution.py:47
  1361.3 24.8 %fusion.171 = (f32[16,3,256]{2,1,0:T(4,128)}, f32[16,3,256,1024]{3,2,1,0:T(8,128)}) fusion(pred[256,1024]{1,0:T(8,128)(4,1)} %iota_compare_fusion.5, bf16[16,1024,3,64]{1,3,2,0:T(8,128)(2,1)} %get-tuple-element.361, bf16[16,1024,3,64]{1,3,2,0:T(8,128)(2,1)} %get-tuple-element.360, s32[]{:T(128)S(6)} %select_n.43), kind=kOutput, calls=%fused_computation.115.clone.1 | convolution fusion | flops 1660945408 | bytes 58507268 | tf_op jit(solution)/shard_map/while/body/eval_jaxpr/sub | solution.py:22
  1386.1 22.4 fusion.170
  1408.5 79.8 %bitcast_dynamic-update-slice_fusion.5 = bf16[4,16,256,3,64]{2,4,3,1,0:T(8,128)(2,1)} fusion(bf16[4,16,256,3,64]{2,4,3,1,0:T(8,128)(2,1)} %get-tuple-element.345, s32[]{:T(128)} %get-tuple-element.342, bf16[16,1024,3,64]{1,3,2,0:T(8,128)(2,1)} %get-tuple-element.361, f32[16,3,256,1024]{3,2,1,0:T(8,128)} %fusion.170, ...), kind=kOutput, calls=%fused_computation.41.clone.1 | convolution fusion | flops 1699492864 | bytes 209322496 | tf_op jit(solution)/shard_map/while/body/eval_jaxpr/bhqk,bkhe->bqhe/dot_general | solution.py:46
  1488.2 26.6 %bitcast_add_fusion.6 = f32[16,1024,3,64]{1,3,2,0:T(8,128)} fusion(f32[16,1024,3,64]{1,3,2,0:T(8,128)} %get-tuple-element.344, pred[]{:T(512)S(6)} %compare.3, bf16[16,1024,3,64]{1,3,2,0:T(8,128)(2,1)} %get-tuple-element.362, s32[]{:T(128)S(6)} %select_n.43, f32[16,3,256,1024]{3,2,1,0:T(8,128)} %get-tuple-element.297, ...), kind=kOutput, calls=%fused_computation.37.clone.1 | convolution fusion | flops 1642070016 | bytes 77135880 | tf_op jit(solution)/shard_map/while/body/eval_jaxpr/bhqk,bqhe->bkhe/dot_general | solution.py:48
  1514.9 94.9 %bitcast_add_fusion.5 = f32[16,1024,3,64]{1,3,2,0:T(8,128)} fusion(f32[16,1024,3,64]{1,3,2,0:T(8,128)} %get-tuple-element.343, pred[]{:T(512)S(6)} %compare.3, f32[16,3,256,1024]{3,2,1,0:T(8,128)} %fusion.170, bf16[16,1024,3,64]{1,3,2,0:T(8,128)(2,1)} %get-tuple-element.360, s32[]{:T(128)S(6)} %select_n.43, ...), kind=kOutput, calls=%fused_computation.38.clone.2 | convolution fusion | flops 1704997888 | bytes 228196352 | tf_op jit(solution)/shard_map/while/body/eval_jaxpr/bhqk,bqhe->bkhe/dot_general | solution.py:47
  1610.0 11.6 copy.54
  1621.6 11.0 stack_reshape.3
  1632.6 9.3 convert_bitcast_fusion
  1642.6 12.4 pad_maximum_fusion
  1655.0 44.4 %copy.55 = bf16[16,1024,3,3,64]{4,0,3,2,1:T(8,128)(2,1)} copy(bf16[16,1024,3,3,64]{1,4,3,0,2:T(8,128)(2,1)} %pad_maximum_fusion) | data formatting | bytes 37748736 | tf_op jit(solution)/shard_map/stack | solution.py:79
  1699.4 53.1 %reshape.73 = bf16[4,2,1179648]{2,1,0:T(2,128)(2,1)} reshape(bf16[1024,3,3,16,64]{4,3,2,1,0:T(8,128)(2,1)} %bitcast.141) | data formatting | bytes 37748736
  1752.5 7.4 all-to-all-start.3
  1759.9 12.8 reshape.72
  1772.7 15.1 copy.68
  1792.1 9.9 fusion.110
  1802.0 7.5 fusion.90
  1809.5 155.5 %all-to-all-done.3 = bf16[4,2,1179648]{2,1,0:T(2,128)(2,1)} async-done(((bf16[4,2,1179648]{2,1,0:T(2,128)(2,1)}), bf16[4,2,1179648]{2,1,0:T(2,128)(2,1)}, u32[]{:S(2)}, u32[]{:S(2)}) %all-to-all-start.3) | async-done | bytes 18874400 | tf_op jit(solution)/shard_map/all_to_all | solution.py:80
  1965.0 52.1 %reshape.74 = bf16[1024,3,3,16,64]{4,3,2,1,0:T(8,128)(2,1)} reshape(bf16[4,2,1179648]{2,1,0:T(2,128)(2,1)} %all-to-all-done.3) | data formatting | bytes 37748736
  2017.1 43.2 %copy.56 = bf16[16,4,256,3,3,64]{2,5,3,0,4,1:T(8,128)(2,1)} copy(bf16[16,4,256,3,3,64]{5,0,4,3,2,1:T(8,128)(2,1)} %bitcast.142) | data formatting | bytes 37748736 | tf_op jit(solution)/shard_map/all_to_all | solution.py:80
  2060.3 24.3 %fusion.105 = f32[768,3,12,64]{0,3,2,1:T(8,128)} fusion(bf16[16,256,3,12,64]{1,4,2,0,3:T(8,128)(2,1)} %bitcast.143, f32[768]{0:T(1024)} %param.15, f32[768]{0:T(1024)} %param.14, f32[16,256]{1,0:T(8,128)} %add_rsqrt_fusion, f32[16,256]{1,0:T(8,128)S(1)} %copy-done.5, bf16[16,256,768]{2,1,0:T(8,128)(2,1)} %param.12), kind=kOutput, calls=%fused_computation.105 | convolution fusion | flops 14514388992 | bytes 32282624 | tf_op jit(solution)/shard_map/bsd,bsthe->dthe/dot_general | solution.py:82
  2084.7 26.8 %fusion.87 = (f32[768]{0:T(1024)}, f32[16,256]{1,0:T(8,128)S(1)}, f32[16,256]{1,0:T(8,128)S(1)}, f32[768]{0:T(1024)}, f32[16,256,768,1,1]{2,1,4,0,3:T(8,128)}) fusion(bf16[16,256,768]{2,1,0:T(8,128)(2,1)} %param.12, f32[16,256]{1,0:T(8,128)} %add_rsqrt_fusion, f32[16,256]{1,0:T(8,128)S(1)} %copy-done.5, f32[768]{0:T(1024)} %param.14, ...), kind=kOutput, calls=%fused_computation.83 | convolution fusion | flops 14526961664 | bytes 41362432 | tf_op jit(solution)/shard_map/bsthe,dthe->bsd/dot_general | solution.py:83
  2111.6 9.8 convert_reduce_fusion
  2123.5 10.3 convert_reduce_fusion.2
  2133.9 13.4 all-reduce
  2148.6 101.9 %all-reduce.4.cloned.1.call-done = (f32[768,3,12,64]{0,3,2,1:T(8,128)}, f32[12,64,768]{2,1,0:T(8,128)}) async-done(((f32[768,3,12,64]{0,3,2,1:T(8,128)}, f32[12,64,768]{2,1,0:T(8,128)}), (f32[768,3,12,64]{0,3,2,1:T(8,128)}, f32[12,64,768]{2,1,0:T(8,128)})) %all-reduce.4.cloned.1.call-update) | async-done | bytes 9437200 | tf_op jit(solution)/shard_map/psum | solution.py:89
  2250.5 6.9 copy.102
  (91 shorter events, 52.0 us)
Async XLA Ops:
  7.2 25.5 %copy-start = (bf16[768,3,12,64]{0,3,2,1:T(8,128)(2,1)S(1)}, bf16[768,3,12,64]{0,3,2,1:T(8,128)(2,1)}, u32[]{:S(2)}) copy-start(bf16[768,3,12,64]{0,3,2,1:T(8,128)(2,1)} %param.16) | copy-start | bytes 10616836
  18.1 76.9 %all-to-all-start.2 = ((bf16[16,256,12,64]{1,3,0,2:T(8,128)(2,1)}), bf16[16,256,12,64]{1,3,0,2:T(8,128)(2,1)}, u32[]{:S(2)}, u32[]{:S(2)}) async-start(bf16[16,256,12,64]{1,3,0,2:T(8,128)(2,1)} %copy.52), calls=%async_computation.2 | async-start | bytes 12582912 | tf_op jit(solution)/shard_map/all_to_all | solution.py:77
  27.3 26.6 %copy-start.4 = (f32[16,256]{1,0:T(8,128)}, f32[16,256]{1,0:T(8,128)S(1)}, u32[]{:S(2)}) copy-start(f32[16,256]{1,0:T(8,128)S(1)} %broadcast_multiply_fusion.2) | copy-start | bytes 49156
  95.0 212.8 %all-to-all-start = ((bf16[16,256,3,12,64]{1,4,2,0,3:T(8,128)(2,1)}), bf16[16,256,3,12,64]{1,4,2,0,3:T(8,128)(2,1)}, u32[]{:S(2)}, u32[]{:S(2)}) async-start(bf16[16,256,3,12,64]{1,4,2,0,3:T(8,128)(2,1)} %copy.46), calls=%async_computation | async-start | bytes 37748736 | tf_op jit(solution)/shard_map/all_to_all | solution.py:64
  603.8 1148.6 %all-to-all-start.1 = ((bf16[4,2,393216]{2,1,0:T(2,128)(2,1)}), bf16[4,2,393216]{2,1,0:T(2,128)(2,1)}, u32[]{:S(2)}, u32[]{:S(2)}) async-start(bf16[4,2,393216]{2,1,0:T(2,128)(2,1)} %reshape.71), calls=%async_computation.1 | async-start | bytes 12582912 | tf_op jit(solution)/shard_map/all_to_all | solution.py:70
  612.6 27.0 %copy-start.10 = (s32[4]{0:T(128)}, s32[4]{0:T(128)S(1)}, u32[]{:S(2)}) copy-start(s32[4]{0:T(128)S(1)} %get-tuple-element.359) | copy-start | bytes 52 | tf_op jit(solution)/shard_map/while
  764.8 87.6 %copy-start.11 = (s32[4]{0:T(128)S(1)}, s32[4]{0:T(128)}, u32[]{:S(2)}) copy-start(s32[4]{0:T(128)} %copy-done.10) | copy-start | bytes 52 | tf_op jit(solution)/shard_map/while
  852.4 27.0 %copy-start.10 = (s32[4]{0:T(128)}, s32[4]{0:T(128)S(1)}, u32[]{:S(2)}) copy-start(s32[4]{0:T(128)S(1)} %get-tuple-element.359) | copy-start | bytes 52 | tf_op jit(solution)/shard_map/while
  1008.1 94.7 %copy-start.11 = (s32[4]{0:T(128)S(1)}, s32[4]{0:T(128)}, u32[]{:S(2)}) copy-start(s32[4]{0:T(128)} %copy-done.10) | copy-start | bytes 52 | tf_op jit(solution)/shard_map/while
  1102.8 27.0 %copy-start.10 = (s32[4]{0:T(128)}, s32[4]{0:T(128)S(1)}, u32[]{:S(2)}) copy-start(s32[4]{0:T(128)S(1)} %get-tuple-element.359) | copy-start | bytes 52 | tf_op jit(solution)/shard_map/while
  1258.6 100.5 %copy-start.11 = (s32[4]{0:T(128)S(1)}, s32[4]{0:T(128)}, u32[]{:S(2)}) copy-start(s32[4]{0:T(128)} %copy-done.10) | copy-start | bytes 52 | tf_op jit(solution)/shard_map/while
  1359.1 27.0 %copy-start.10 = (s32[4]{0:T(128)}, s32[4]{0:T(128)S(1)}, u32[]{:S(2)}) copy-start(s32[4]{0:T(128)S(1)} %get-tuple-element.359) | copy-start | bytes 52 | tf_op jit(solution)/shard_map/while
  1514.9 94.9 %copy-start.11 = (s32[4]{0:T(128)S(1)}, s32[4]{0:T(128)}, u32[]{:S(2)}) copy-start(s32[4]{0:T(128)} %copy-done.10) | copy-start | bytes 52 | tf_op jit(solution)/shard_map/while
  1632.6 10.0 copy-start.1
  1752.5 212.6 %all-to-all-start.3 = ((bf16[4,2,1179648]{2,1,0:T(2,128)(2,1)}), bf16[4,2,1179648]{2,1,0:T(2,128)(2,1)}, u32[]{:S(2)}, u32[]{:S(2)}) async-start(bf16[4,2,1179648]{2,1,0:T(2,128)(2,1)} %reshape.73), calls=%async_computation.3 | async-start | bytes 37748736 | tf_op jit(solution)/shard_map/all_to_all | solution.py:80
  1759.8 490.7 %all-reduce.4.cloned.1.call-start = ((), (), s32[]{:S(2)}) async-start(), calls=%async_computation.4 | async-start | bytes 18874368 | tf_op jit(solution)/shard_map/psum | solution.py:89
  1787.8 14.2 slice-start
  1792.0 9.9 slice-start.1
  1792.0 9.9 copy-start.8
  1792.1 9.9 copy-start.9
  2017.1 43.3 %copy-start.5 = (f32[16,256]{1,0:T(8,128)S(1)}, f32[16,256]{1,0:T(8,128)}, u32[]{:S(2)}) copy-start(f32[16,256]{1,0:T(8,128)} %copy-done.4) | copy-start | bytes 49156
  2111.5 9.8 slice-start.2
  2111.5 11.4 copy-start.2
  2111.5 11.4 copy-start.6
  2111.5 11.4 copy-start.7
  2111.5 12.0 slice-start.3
  2250.5 6.9 copy-start.3
Sparse Core Ops, SparseCore 0:
  2084.8 165.6 all-reduce.3
where the time goes:
time: 2270 us
  matrix products  1270 us (56%)
  waiting for transfers between devices  464 us (20%)
  local copies, waits for them, and re-layouts  414 us (18%)
  other arithmetic  58.2 us (3%)
  starting transfers between devices  25.7 us (1%)
    dot_general x4, matrix products, step(): jnp.einsum('bhqk,bqhe->bkhe', d_score, q_rows, preferred_element_type=jnp...  378 us
    dot_general x4, matrix products, step(): jnp.einsum('bhqk,bkhe->bqhe', d_score, keys, preferred_element_type=jnp.f...  319 us
    sub x8, matrix products, block_probs(): return jax.nn.softmax(scores, axis=-1)  198 us
    all_to_all x1, waiting for transfers between devices, local_step(): head_qkv = lax.all_to_all(proj_qkv, 'sp', 3, 1, tiled=True)  182 us
    all_to_all x1, waiting for transfers between devices, local_step(): d_qkv = lax.all_to_all(d_heads, 'sp', 1, 3, tiled=True)  156 us
    unnamed x35, local copies, waits for them, and re-layouts  143 us
    dot_general x4, matrix products, step(): jnp.einsum('bhqk,bqhe->bkhe', attn_prob.astype(jnp.bfloat16), d_rows, pre...  103 us
    psum x1, waiting for transfers between devices, local_step(): grads = lax.psum((d_ln_g, d_ln_b, d_w_qkv, d_b_qkv, d_w_out, d_b_out), 'sp')  102 us
  transfers between devices with their start and end apart: 5, of which 4 were waited for; matrix products, arithmetic and copies ran while one was open for 57% of the time, Pallas kernels for 0%

commit v1 on v0

v1 whole, which is shorter than its diff:
```python
import functools

import jax
import jax.numpy as jnp
from jax import lax
from jax.experimental import pallas as pl
from jax.experimental.pallas import tpu as pltpu
from jax.sharding import PartitionSpec as P


LN_EPS = 1e-5
F32 = jnp.float32
BF16 = jnp.bfloat16
CHUNKS = 4
UP = [(0, 2), (1, 3)]
DOWN = [(2, 0), (3, 1)]
SWAP_CHIP = [(0, 2), (1, 3), (2, 0), (3, 1)]
SWAP_CORE = [(0, 1), (1, 0), (2, 3), (3, 2)]


UNREAD = pl.BlockSpec(memory_space=pltpu.HBM)


def dot_nn(a, b):
    return lax.dot_general(a, b, (((1,), (0,)), ((), ())), preferred_element_type=F32)


def dot_nt(a, b):
    return lax.dot_general(a, b, (((1,), (1,)), ((), ())), preferred_element_type=F32)


def params(n):
    return pltpu.CompilerParams(dimension_semantics=("arbitrary",) * n, vmem_limit_bytes=56 * 1024 * 1024)


def normed(x_f):
    centred = x_f - jnp.mean(x_f, axis=-1, keepdims=True)
    inv_std = lax.rsqrt(jnp.mean(centred * centred, axis=-1, keepdims=True) + LN_EPS)
    return centred * inv_std, inv_std


def front_kernel(core_ref, x_ref, xr_ref, g_ref, gr_ref, lng_ref, lnb_ref, w_ref, b_ref, wo_ref,
                 h_ref, q_ref, k_ref, v_ref, da_ref, xb_ref, gb_ref):
    dim = x_ref.shape[2]
    run = x_ref.shape[1]
    mine = pl.ds(pl.multiple_of(core_ref[0] * run, run), run)
    theirs = pl.ds(pl.multiple_of((1 - core_ref[0]) * run, run), run)
    xb_ref[0, mine, :] = x_ref[0]
    xb_ref[0, theirs, :] = xr_ref[0]
    gb_ref[0, mine, :] = g_ref[0]
    gb_ref[0, theirs, :] = gr_ref[0]
    da_ref[0] = dot_nt(gb_ref[0], wo_ref[...]).astype(BF16)
    x_hat, _ = normed(xb_ref[0].astype(F32))
    h_ref[0] = (x_hat * lng_ref[...] + lnb_ref[...]).astype(BF16)
    for t, out in enumerate((q_ref, k_ref, v_ref)):
        cols = slice(t * dim, (t + 1) * dim)
        out[0] = (dot_nt(h_ref[0], w_ref[cols, :]) + b_ref[:, cols]).astype(BF16)


def front(core, x, x_r, g, g_r, ln_g, ln_b, w_t, b_qkv, w_o, lo):
    batch, run, dim = x.shape
    n, seq = x_r.shape[0], 2 * run
    whole = lambda shape: pl.BlockSpec(shape, lambda b, c: (0,) * len(shape))
    own = pl.BlockSpec((1, run, dim), lambda b, c: (c[0] * (batch // 2) + lo + b, 0, 0))
    got = pl.BlockSpec((1, run, dim), lambda b, c: (b, 0, 0))
    tok = pl.BlockSpec((1, seq, dim), lambda b, c: (b, 0, 0))
    out = jax.ShapeDtypeStruct((n, seq, dim), BF16)
    return pl.pallas_call(
        front_kernel,
        grid_spec=pltpu.PrefetchScalarGridSpec(
            num_scalar_prefetch=1,
            grid=(n,),
            in_specs=[own, got, own, got, whole((1, dim)), whole((1, dim)), whole((3 * dim, dim)), whole((1, 3 * dim)), whole((dim, dim))],
            out_specs=[tok] * 7,
        ),
        out_shape=[out] * 7,
        compiler_params=params(1),
        cost_estimate=pl.CostEstimate(flops=8 * n * seq * dim * dim, bytes_accessed=18 * n * seq * dim, transcendentals=0),
        name="front",
    )(core, x, x_r, g, g_r, ln_g, ln_b, w_t, b_qkv, w_o)


def kv_kernel(role_ref, h_ref, w_ref, b_ref, k_ref, v_ref):
    dim = h_ref.shape[2]

    @pl.when(role_ref[0] == 1)
    def _():
        for t, out in enumerate((k_ref, v_ref)):
            cols = slice((t + 1) * dim, (t + 2) * dim)
            out[0] = (dot_nt(h_ref[0], w_ref[cols, :]) + b_ref[:, cols]).astype(BF16)


def other_kv(role, h_o, w_t, b_qkv):
    n, seq, dim = h_o.shape
    tok = pl.BlockSpec((1, seq, dim), lambda b, r: (b * r[0], 0, 0))
    out = jax.ShapeDtypeStruct((n, seq, dim), BF16)
    return pl.pallas_call(
        kv_kernel,
        grid_spec=pltpu.PrefetchScalarGridSpec(
            num_scalar_prefetch=1,
            grid=(n,),
            in_specs=[tok, pl.BlockSpec((3 * dim, dim), lambda b, r: (0, 0)), pl.BlockSpec((1, 3 * dim), lambda b, r: (0, 0))],
            out_specs=[tok] * 2,
        ),
        out_shape=[out] * 2,
        compiler_params=params(1),
        cost_estimate=pl.CostEstimate(flops=4 * n * seq * dim * dim, bytes_accessed=6 * n * seq * dim, transcendentals=0),
        name="other_kv",
    )(role, h_o, w_t, b_qkv)


def attn_kernel(role_ref, q_ref, k_ref, v_ref, g_ref, ko_ref, vo_ref, a_ref, dq_ref, dk_ref, dv_ref, st_ref, *, head, scale):
    seq = q_ref.shape[1]
    blk = seq // 2
    width = q_ref.shape[2]
    lane = lax.broadcasted_iota(jnp.int32, (blk, width), 1)
    causal = lax.broadcasted_iota(jnp.int32, (blk, blk), 0) <= lax.broadcasted_iota(jnp.int32, (blk, blk), 1)

    def run(rect):
        k_t, v_t = k_ref[0].T, v_ref[0].T
        if rect:
            ko_t, vo_t = ko_ref[0].T, vo_ref[0].T
        for qi in range(2):
            rows = slice(qi * blk, (qi + 1) * blk)
            q2 = q_ref[0, rows, :] * jnp.asarray(scale, BF16)
            g2 = g_ref[0, rows, :]
            o_parts, dq_parts = [], []
            dk_parts = [None] * (qi + 1)
            dv_parts = [None] * (qi + 1)
            for h in range(width // head):
                mine = (lane >= h * head) & (lane < (h + 1) * head)
                hrow = slice(h * head, (h + 1) * head)
                qm = jnp.where(mine, q2, jnp.zeros_like(q2))
                gm = jnp.where(mine, g2, jnp.zeros_like(g2))
                pieces = []
                for ki in range(qi + 1):
                    kr = slice(ki * blk, (ki + 1) * blk)
                    pieces.append((ki, k_ref[0, kr, :], v_ref[0, kr, :], k_t[hrow, kr], v_t[hrow, kr]))
                if rect:
                    for ki in range(2):
                        kr = slice(ki * blk, (ki + 1) * blk)
                        pieces.append((None, ko_ref[0, kr, :], vo_ref[0, kr, :], ko_t[hrow, kr], vo_t[hrow, kr]))
                s = []
                for ki, k_i, _, _, _ in pieces:
                    s_i = dot_nt(k_i, qm)
                    if ki == qi:
                        s_i = jnp.where(causal, s_i, -jnp.inf)
                    s.append(s_i)
                m = functools.reduce(jnp.maximum, [jnp.max(s_i, axis=0, keepdims=True) for s_i in s])
                e = [jnp.exp(s_i - m) for s_i in s]
                dp = [dot_nt(v_i, gm) for _, _, v_i, _, _ in pieces]
                l = functools.reduce(jnp.add, [jnp.sum(e_i, axis=0, keepdims=True) for e_i in e])
                c = functools.reduce(jnp.add, [jnp.sum(e_i * d_i, axis=0, keepdims=True) for e_i, d_i in zip(e, dp)])
                inv_l = 1.0 / l
                c = c * inv_l
                st_ref[0, 0, 2 * h, rows] = (m + jnp.log(l))[0]
                st_ref[0, 0, 2 * h + 1, rows] = c[0]
                o_h = dq_h = None
                for (ki, _, _, kt_i, vt_i), e_i, d_i in zip(pieces, e, dp):
                    p_i = e_i * inv_l
                    pb = p_i.astype(BF16)
                    ds = (p_i * (d_i - c)).astype(BF16)
                    o_i = dot_nn(vt_i, pb)
                    dq_i = dot_nn(kt_i, ds)
                    o_h = o_i if o_h is None else o_h + o_i
                    dq_h = dq_i if dq_h is None else dq_h + dq_i
                    if ki is not None:
                        dv_i = dot_nn(pb, gm)
                        dk_i = dot_nn(ds, qm)
                        dv_parts[ki] = dv_i if dv_parts[ki] is None else dv_parts[ki] + dv_i
                        dk_parts[ki] = dk_i if dk_parts[ki] is None else dk_parts[ki] + dk_i
                o_parts.append(o_h)
                dq_parts.append(dq_h)
            a_ref[0, rows, :] = jnp.concatenate(o_parts, axis=0).T.astype(BF16)
            dq_ref[0, rows, :] = (jnp.concatenate(dq_parts, axis=0).T * scale).astype(BF16)
            for ki in range(qi + 1):
                kr = slice(ki * blk, (ki + 1) * blk)
                if ki == qi:
                    dk_ref[0, kr, :] = dk_parts[ki]
                    dv_ref[0, kr, :] = dv_parts[ki]
                else:
                    dk_ref[0, kr, :] += dk_parts[ki]
                    dv_ref[0, kr, :] += dv_parts[ki]

    pl.when(role_ref[0] == 0)(lambda: run(False))
    pl.when(role_ref[0] == 1)(lambda: run(True))


def attend(role, q, k, v, da, k_o, v_o, head):
    n, seq, dim = q.shape
    width = 128
    pairs = dim // width
    tok = pl.BlockSpec((1, seq, width), lambda b, p, r: (b, 0, p))
    far = pl.BlockSpec((1, seq, width), lambda b, p, r: (b * r[0], 0, p * r[0]))
    low = jax.ShapeDtypeStruct((n, seq, dim), BF16)
    acc = jax.ShapeDtypeStruct((n, seq, dim), F32)
    return pl.pallas_call(
        functools.partial(attn_kernel, head=head, scale=head ** -0.5),
        grid_spec=pltpu.PrefetchScalarGridSpec(
            num_scalar_prefetch=1,
            grid=(n, pairs),
            in_specs=[tok] * 4 + [far] * 2,
            out_specs=[tok] * 4 + [pl.BlockSpec((1, 1, 4, seq), lambda b, p, r: (b, p, 0, 0))],
        ),
        out_shape=[low, low, acc, acc, jax.ShapeDtypeStruct((n, pairs, 4, seq), F32)],
        compiler_params=params(2),
        cost_estimate=pl.CostEstimate(flops=32 * n * seq * seq * dim, bytes_accessed=24 * n * seq * dim, transcendentals=0),
        name="attend",
    )(role, q, k, v, da, k_o, v_o)


def late_kernel(role_ref, q_ref, g_ref, st_ref, k_ref, v_ref, dka_ref, dva_ref, *rest, head, scale):
    dk_ref, dv_ref = rest[-2:]
    seq = q_ref.shape[1]
    blk = seq // 2
    width = q_ref.shape[2]
    lane = lax.broadcasted_iota(jnp.int32, (blk, width), 1)

    @pl.when(role_ref[0] == 1)
    def _():
        dk_ref[0] = dka_ref[0].astype(BF16)
        dv_ref[0] = dva_ref[0].astype(BF16)

    @pl.when(role_ref[0] == 0)
    def _():
        for ki in range(2):
            kr = slice(ki * blk, (ki + 1) * blk)
            k_i, v_i = k_ref[0, kr, :], v_ref[0, kr, :]
            dk, dv = dka_ref[0, kr, :], dva_ref[0, kr, :]
            for qi in range(2):
                rows = slice(qi * blk, (qi + 1) * blk)
                q2 = q_ref[0, rows, :] * jnp.asarray(scale, BF16)
                g2 = g_ref[0, rows, :]
                for h in range(width // head):
                    mine = (lane >= h * head) & (lane < (h + 1) * head)
                    qm = jnp.where(mine, q2, jnp.zeros_like(q2))
                    gm = jnp.where(mine, g2, jnp.zeros_like(g2))
                    lse = st_ref[0, 0, 2 * h, rows].reshape(1, blk)
                    c = st_ref[0, 0, 2 * h + 1, rows].reshape(1, blk)
                    p = jnp.exp(dot_nt(k_i, qm) - lse)
                    ds = (p * (dot_nt(v_i, gm) - c)).astype(BF16)
                    dv = dv + dot_nn(p.astype(BF16), gm)
                    dk = dk + dot_nn(ds, qm)
            dk_ref[0, kr, :] = dk.astype(BF16)
            dv_ref[0, kr, :] = dv.astype(BF16)


def late(role, q_o, da_o, stats, k, v, dk_acc, dv_acc, head, after):
    n, seq, dim = k.shape
    width = 128
    pairs = dim // width
    tok = pl.BlockSpec((1, seq, width), lambda b, p, r: (b, 0, p))
    far = pl.BlockSpec((1, seq, width), lambda b, p, r: (b * (1 - r[0]), 0, p * (1 - r[0])))
    low = jax.ShapeDtypeStruct((n, seq, dim), BF16)
    return pl.pallas_call(
        functools.partial(late_kernel, head=head, scale=head ** -0.5),
        grid_spec=pltpu.PrefetchScalarGridSpec(
            num_scalar_prefetch=1,
            grid=(n, pairs),
            in_specs=[far, far, pl.BlockSpec((1, 1, 4, seq), lambda b, p, r: (b, p, 0, 0)), far, far, tok, tok] + [UNREAD] * len(after),
            out_specs=[tok] * 2,
        ),
        out_shape=[low] * 2,
        compiler_params=params(2),
        cost_estimate=pl.CostEstimate(flops=16 * n * seq * seq * dim, bytes_accessed=20 * n * seq * dim, transcendentals=0),
        name="late",
    )(role, q_o, da_o, stats, k, v, dk_acc, dv_acc, *after)


def split_rows(core_ref, full_ref, own_ref, send_ref):
    run = own_ref.shape[1]
    own_ref[0] = full_ref[pl.ds(pl.multiple_of(core_ref[0] * run, run), run), :]
    send_ref[0] = full_ref[pl.ds(pl.multiple_of((1 - core_ref[0]) * run, run), run), :]


def post_kernel(core_ref, a_ref, x_ref, wo_ref, bo_ref, own_ref, send_ref, full_ref):
    out = dot_nn(a_ref[0], wo_ref[...]) + bo_ref[...]
    full_ref[...] = (x_ref[0].astype(F32) + out).astype(BF16)
    split_rows(core_ref, full_ref, own_ref, send_ref)


def post(core, a, x, w_o, b_o):
    n, seq, dim = a.shape
    run = seq // 2
    tok = pl.BlockSpec((1, seq, dim), lambda b, c: (b, 0, 0))
    part = pl.BlockSpec((1, run, dim), lambda b, c: (b, 0, 0))
    whole = lambda shape: pl.BlockSpec(shape, lambda b, c: (0,) * len(shape))
    return pl.pallas_call(
        post_kernel,
        grid_spec=pltpu.PrefetchScalarGridSpec(
            num_scalar_prefetch=1,
            grid=(n,),
            in_specs=[tok, tok, whole((dim, dim)), whole((1, dim))],
            out_specs=[part] * 2,
            scratch_shapes=[pltpu.VMEM((seq, dim), BF16)],
        ),
        out_shape=[jax.ShapeDtypeStruct((n, run, dim), BF16)] * 2,
        compiler_params=params(1),
        cost_estimate=pl.CostEstimate(flops=2 * n * seq * dim * dim, bytes_accessed=6 * n * seq * dim, transcendentals=0),
        name="post",
    )(core, a, x, w_o, b_o)


def back_kernel(core_ref, dq_ref, dk_ref, dv_ref, x_ref, g_ref, lng_ref, w_ref, prev_ref, *rest):
    own_ref, send_ref, acc_ref, full_ref = rest[-4:]
    dim = x_ref.shape[2]

    @pl.when(pl.program_id(0) == 0)
    def _():
        acc_ref[...] = prev_ref[...]

    dh = dot_nn(dq_ref[0], w_ref[0:dim, :]) + dot_nn(dk_ref[0], w_ref[dim:2 * dim, :]) + dot_nn(dv_ref[0], w_ref[2 * dim:3 * dim, :])
    x_hat, inv_std = normed(x_ref[0].astype(F32))
    g = g_ref[0].astype(F32)
    u = dh * lng_ref[...]
    dx = inv_std * (u - jnp.mean(u, axis=-1, keepdims=True) - x_hat * jnp.mean(u * x_hat, axis=-1, keepdims=True))
    full_ref[...] = (g + dx).astype(BF16)
    split_rows(core_ref, full_ref, own_ref, send_ref)
    acc_ref[0:1, :] += jnp.sum(dh * x_hat, axis=0, keepdims=True)
    acc_ref[1:2, :] += jnp.sum(dh, axis=0, keepdims=True)
    for t, ref in enumerate((dq_ref, dk_ref, dv_ref)):
        acc_ref[2 + t:3 + t, :] += jnp.sum(ref[0].astype(F32), axis=0, keepdims=True)
    acc_ref[5:6, :] += jnp.sum(g, axis=0, keepdims=True)


def back(core, dq, dk, dv, x, g, ln_g, w_t, prev, after):
    n, seq, dim = dq.shape
    run = seq // 2
    tok = pl.BlockSpec((1, seq, dim), lambda b, c: (b, 0, 0))
    part = pl.BlockSpec((1, run, dim), lambda b, c: (b, 0, 0))
    whole = lambda shape: pl.BlockSpec(shape, lambda b, c: (0,) * len(shape))
    return pl.pallas_call(
        back_kernel,
        grid_spec=pltpu.PrefetchScalarGridSpec(
            num_scalar_prefetch=1,
            grid=(n,),
            in_specs=[tok] * 5 + [whole((1, dim)), whole((3 * dim, dim)), whole((8, dim))] + [UNREAD] * len(after),
            out_specs=[part, part, whole((8, dim))],
            scratch_shapes=[pltpu.VMEM((seq, dim), BF16)],
        ),
        out_shape=[jax.ShapeDtypeStruct((n, run, dim), BF16)] * 2 + [jax.ShapeDtypeStruct((8, dim), F32)],
        compiler_params=params(1),
        cost_estimate=pl.CostEstimate(flops=6 * n * seq * dim * dim, bytes_accessed=12 * n * seq * dim, transcendentals=0),
        name="back",
    )(core, dq, dk, dv, x, g, ln_g, w_t, prev, *after)


def tok_dot(a, b):
    return lax.dot_general(a, b, (((0, 1), (0, 1)), ((), ())), preferred_element_type=F32)


def solution(mesh):
    tok_spec = P('dp', 'sp', None)
    part_spec = P('dp')

    def local_step(x, g, ln_g, ln_b, w_qkv, b_qkv, w_out, b_out):
        batch, run, dim = x.shape
        _, _, heads, head = w_qkv.shape
        index = lax.axis_index('sp')
        chip, core = lax.div(index, 2), lax.rem(index, 2)
        role, side = chip.reshape(1), core.reshape(1)
        ln_g2, ln_b2, b_o = ln_g.reshape(1, dim), ln_b.reshape(1, dim), b_out.reshape(1, dim)
        w_t = jnp.transpose(w_qkv, (1, 2, 3, 0)).reshape(3 * dim, dim)
        w_o = w_out.reshape(dim, dim)
        b_all = b_qkv.reshape(1, 3 * dim)
        half_b = batch // 2
        n = half_b // CHUNKS
        half_d = dim // 2

        def send(z, perm):
            return lax.ppermute(z, 'sp', perm)

        def handed(z, i):
            return send(lax.dynamic_slice_in_dim(z, (1 - core) * half_b + i * n, n, 0), SWAP_CORE)

        def gathered(own, got):
            buf = jnp.zeros((batch, run, dim), BF16)
            for i in range(CHUNKS):
                buf = lax.dynamic_update_slice_in_dim(buf, own[i], core * half_b + i * n, 0)
            for i in range(CHUNKS):
                buf = lax.dynamic_update_slice_in_dim(buf, got[i], (1 - core) * half_b + i * n, 0)
            return buf

        got = [(handed(g, i), handed(x, i)) for i in range(CHUNKS)]
        own, far = [], []
        for i in range(CHUNKS):
            h, q, k, v, da, xb, gb = front(side, x, got[i][1], g, got[i][0], ln_g2, ln_b2, w_t, b_all, w_o, i * n)
            own.append((h, q, k, v, da, xb, gb))
            far.append((send(h, UP), send(da, DOWN), send(q, DOWN)))

        att, y_own, y_send, dw_o, dw_q = [], [], [], None, None
        for i in range(CHUNKS):
            h, q, k, v, da, xb, gb = own[i]
            k_o, v_o = other_kv(role, far[i][0], w_t, b_all)
            a, dq, dk_acc, dv_acc, stats = attend(role, q, k, v, da, k_o, v_o, head)
            att.append((dq, dk_acc, dv_acc, send(stats, DOWN)))
            mine, theirs = post(side, a, xb, w_o, b_o)
            y_own.append(mine)
            y_send.append(theirs)
            do, dwq = tok_dot(a, gb), tok_dot(dq, h)
            dw_o = do if dw_o is None else dw_o + do
            dw_q = dwq if dw_q is None else dw_q + dwq

        def halves_added(w):
            theirs = send(lax.dynamic_slice_in_dim(w, (1 - core) * half_d, half_d, 0), SWAP_CORE)
            return lax.dynamic_slice_in_dim(w, core * half_d, half_d, 0) + theirs

        part_o, part_q = halves_added(dw_o), halves_added(dw_q)
        sum_o = part_o + send(part_o, SWAP_CHIP)
        sum_q = part_q + send(part_q, SWAP_CHIP)
        y = gathered(y_own, [send(z, SWAP_CORE) for z in y_send])

        dx_own, dx_send, dw_k, dw_v = [], [], None, None
        acc = jnp.zeros((8, dim), F32)
        after = [part_o, part_q] + y_send
        for i in range(CHUNKS):
            h, q, k, v, da, xb, gb = own[i]
            dq, dk_acc, dv_acc, stats_o = att[i]
            dk, dv = late(role, far[i][2], far[i][1], stats_o, k, v, dk_acc, dv_acc, head, after)
            dwk, dwv = tok_dot(dk, h), tok_dot(dv, h)
            dw_k = dwk if dw_k is None else dw_k + dwk
            dw_v = dwv if dw_v is None else dw_v + dwv
            if i == CHUNKS - 1:
                part_k, part_v = halves_added(dw_k), halves_added(dw_v)
                after = [part_k, part_v]
            else:
                after = [dwk, dwv]
            mine, theirs, acc = back(side, dq, dk, dv, xb, gb, ln_g2, w_t, acc, after)
            after = [acc]
            dx_own.append(mine)
            dx_send.append(theirs)
        sum_k = part_k + send(part_k, SWAP_CHIP)
        sum_v = part_v + send(part_v, SWAP_CHIP)
        d_x = gathered(dx_own, [send(z, SWAP_CORE) for z in dx_send])
        acc = acc + send(acc, SWAP_CORE)
        acc = acc + send(acc, SWAP_CHIP)

        d_w_out = jnp.zeros((dim, dim), F32)
        d_w_out = lax.dynamic_update_slice(d_w_out, sum_o, (core * half_d, 0))
        d_w_out = lax.dynamic_update_slice(d_w_out, send(sum_o, SWAP_CORE), ((1 - core) * half_d, 0))
        dw = jnp.zeros((3 * dim, dim), F32)
        for t, w in enumerate((sum_q, sum_k, sum_v)):
            dw = lax.dynamic_update_slice(dw, w, (t * dim + core * half_d, 0))
            dw = lax.dynamic_update_slice(dw, send(w, SWAP_CORE), (t * dim + (1 - core) * half_d, 0))
        d_w_qkv = jnp.transpose(dw.reshape(3, heads, head, dim), (3, 0, 1, 2))
        return y, d_x, acc[0], acc[1], d_w_qkv, acc[2:5].reshape(3, heads, head), d_w_out.reshape(heads, head, dim), acc[5]


    return jax.shard_map(local_step, mesh=mesh, in_specs=(tok_spec, tok_spec) + (P(),) * 6, out_specs=(tok_spec, tok_spec) + (part_spec,) * 6, check_vma=False)
```

time: 2270 us -> 720 us (0.32)
  matrix products: 1270 us -> 47.7 us
  local copies, waits for them, and re-layouts: 414 us -> 54.7 us
  Pallas kernels: 0 us -> 336 us
  waiting for transfers between devices: 464 us -> 219 us
  other arithmetic: 58.2 us -> 11.9 us
    dot_general x26 -> x16, matrix products: 1070 us -> 47.7 us  [tok_dot(): lax.dot_general(a, b, (((0, 1), (0, 1)), ((), ())), preferred_element_typ...]
    all_to_all x4 -> x0, waiting for transfers between devices: 362 us -> none  [the longest x1 182 us: local_step(): head_qkv = lax.all_to_all(proj_qkv, 'sp', 3, 1, tiled=True)]
    pallas_call x0 -> x24, Pallas kernels: none -> 336 us  [the longest x4 118 us: attend(): pl.pallas_call(functools.partial(attn_kernel, head=head, scale=head ** (-...]
    ppermute x0 -> x46, waiting for transfers between devices: none -> 219 us  [send(): return lax.ppermute(z, 'sp', perm)]
    sub x8 -> x0, matrix products: 198 us -> none  [block_probs(): return jax.nn.softmax(scores, axis=-1)]
    all_to_all x7 -> x0, local copies, waits for them, and re-layouts: 141 us -> none  [the longest x2 55.4 us: local_step(): head_qkv = lax.all_to_all(proj_qkv, 'sp', 3, 1, tiled=True)]
    unnamed x35 -> x138, local copies, waits for them, and re-layouts: 143 us -> 18.9 us
    psum x1 -> x0, waiting for transfers between devices: 102 us -> none  [local_step(): grads = lax.psum((d_ln_g, d_ln_b, d_w_qkv, d_b_qkv, d_w_out, d_b_out), 'sp')]
  transfers between devices with their start and end apart: 5 -> 46, of which waited for: 4 -> 8; matrix products, arithmetic and copies ran while one was open for 57% -> 12% of each run, Pallas kernels for 0% -> 47%
where the time goes in v1:
time: 720 us; the launch traced here: 711 us
  Pallas kernels  336 us (47%)
  waiting for transfers between devices  219 us (30%)
  local copies, waits for them, and re-layouts  54.7 us (8%)
  matrix products  47.7 us (7%)
  starting transfers between devices  38.4 us (5%)
  other arithmetic  11.9 us (2%)
    ppermute x46, waiting for transfers between devices, send(): return lax.ppermute(z, 'sp', perm)  219 us
    pallas_call x4, Pallas kernels, attend(): pl.pallas_call(functools.partial(attn_kernel, head=head, scale=head ** (-...  118 us
    pallas_call x4, Pallas kernels, late(): pl.pallas_call(functools.partial(late_kernel, head=head, scale=head ** (-...  107 us
    dot_general x16, matrix products, tok_dot(): lax.dot_general(a, b, (((0, 1), (0, 1)), ((), ())), preferred_element_typ...  47.7 us
    pallas_call x4, Pallas kernels, back(): pl.pallas_call(back_kernel, grid_spec=pltpu.PrefetchScalarGridSpec(num_sc...  41.9 us
    pallas_call x4, Pallas kernels, front(): pl.pallas_call(front_kernel, grid_spec=pltpu.PrefetchScalarGridSpec(num_s...  39 us
    ppermute x46, starting transfers between devices, send(): return lax.ppermute(z, 'sp', perm)  38.4 us
    unnamed x138, local copies, waits for them, and re-layouts  18.9 us
  transfers between devices with their start and end apart: 46, of which 8 were waited for; matrix products, arithmetic and copies ran while one was open for 12% of the time, Pallas kernels for 47%

profile of v1, /device:TPU:0, one launch (start us, length us, event | category | flops | bytes accessed | tf_op | source)
XLA Modules:
  0.0 710.5 jit_solution(8835603249262352694)
XLA Ops:
  0.7 3.7 constant_dynamic-slice_fusion.5
  5.5 1.7 constant_dynamic-slice_fusion.4
  11.8 9.8 %front.6 = (bf16[2,512,768]{2,1,0:T(8,128)(2,1)}, bf16[2,512,768]{2,1,0:T(8,128)(2,1)}, bf16[2,512,768]{2,1,0:T(8,128)(2,1)}, bf16[2,512,768]{2,1,0:T(8,128)(2,1...) custom-call(s32[1]{0:T(128)} %bitcast.core_ref, ...), custom_call_target="tpu_custom_call" | custom-call | flops 4831838208 | bytes 14155776 | tf_op jit(solution)/shard_map/front/pallas_call | solution.py:68
  21.6 5.5 collective-permute-start.8
  28.3 9.8 %front.4 = (bf16[2,512,768]{2,1,0:T(8,128)(2,1)}, bf16[2,512,768]{2,1,0:T(8,128)(2,1)}, bf16[2,512,768]{2,1,0:T(8,128)(2,1)}, bf16[2,512,768]{2,1,0:T(8,128)(2,1...) custom-call(s32[1]{0:T(128)} %bitcast.core_ref, ...), custom_call_target="tpu_custom_call" | custom-call | flops 4831838208 | bytes 14155776 | tf_op jit(solution)/shard_map/front/pallas_call | solution.py:68
  40.4 9.7 %front.5 = (bf16[2,512,768]{2,1,0:T(8,128)(2,1)}, bf16[2,512,768]{2,1,0:T(8,128)(2,1)}, bf16[2,512,768]{2,1,0:T(8,128)(2,1)}, bf16[2,512,768]{2,1,0:T(8,128)(2,1...) custom-call(s32[1]{0:T(128)} %bitcast.core_ref, ...), custom_call_target="tpu_custom_call" | custom-call | flops 4831838208 | bytes 14155776 | tf_op jit(solution)/shard_map/front/pallas_call | solution.py:68
  53.3 9.7 %front.7 = (bf16[2,512,768]{2,1,0:T(8,128)(2,1)}, bf16[2,512,768]{2,1,0:T(8,128)(2,1)}, bf16[2,512,768]{2,1,0:T(8,128)(2,1)}, bf16[2,512,768]{2,1,0:T(8,128)(2,1...) custom-call(s32[1]{0:T(128)} %bitcast.core_ref, ...), custom_call_target="tpu_custom_call" | custom-call | flops 4831838208 | bytes 14155776 | tf_op jit(solution)/shard_map/front/pallas_call | solution.py:68
  63.0 2.4 collective-permute-start.11
  66.8 1.5 collective-permute-start.17
  68.3 3.4 other_kv.6
  71.7 29.3 %attend.6 = (bf16[2,512,768]{2,1,0:T(8,128)(2,1)}, bf16[2,512,768]{2,1,0:T(8,128)(2,1)}, f32[2,512,768]{2,1,0:T(8,128)}, f32[2,512,768]{2,1,0:T(8,128)}, f32[2,6,4,512]{3,2,1,0:T(4,128)}) custom-call(s32[1]{0:T(128)} %bitcast.1.role_ref, bf16[2,512,768]{2,1,0:T(8,128)(2,1)} %get-tuple-element.112.q_ref, bf16[2,512,768]{2,1,0:T(8,128)(2,1)} %get-tuple-element.113.k_ref, ...), custom_call_target="tpu_custom_call" | custom-call | flops 12884901888 | bytes 18874368 | tf_op jit(solution)/shard_map/attend/pallas_call | solution.py:197
  101.1 2.8 fusion.2
  103.9 24.6 %collective-permute-done.5.h_ref = bf16[2,512,768]{2,1,0:T(8,128)(2,1)S(1)} collective-permute-done((bf16[2,512,768]{2,1,0:T(8,128)(2,1)}, bf16[2,512,768]{2,1,0:T(8,128)(2,1)S(1)}, u32[]{:S(2)}, u32[]{:S(2)}) %collective-permute-start.5) | collective-permute-done | bytes 1572896 | tf_op jit(solution)/shard_map/ppermute | solution.py:371
  129.6 3.4 other_kv.5
  133.0 29.6 %attend.5 = (bf16[2,512,768]{2,1,0:T(8,128)(2,1)}, bf16[2,512,768]{2,1,0:T(8,128)(2,1)}, f32[2,512,768]{2,1,0:T(8,128)}, f32[2,512,768]{2,1,0:T(8,128)}, f32[2,6,4,512]{3,2,1,0:T(4,128)}) custom-call(s32[1]{0:T(128)} %bitcast.1.role_ref, bf16[2,512,768]{2,1,0:T(8,128)(2,1)} %get-tuple-element.102.q_ref, bf16[2,512,768]{2,1,0:T(8,128)(2,1)} %get-tuple-element.103.k_ref, ...), custom_call_target="tpu_custom_call" | custom-call | flops 12884901888 | bytes 18874368 | tf_op jit(solution)/shard_map/attend/pallas_call | solution.py:197
  162.6 2.8 fusion.1
  166.6 3.5 other_kv.4
  170.1 29.4 %attend.4 = (bf16[2,512,768]{2,1,0:T(8,128)(2,1)}, bf16[2,512,768]{2,1,0:T(8,128)(2,1)}, f32[2,512,768]{2,1,0:T(8,128)}, f32[2,512,768]{2,1,0:T(8,128)}, f32[2,6,4,512]{3,2,1,0:T(4,128)}) custom-call(s32[1]{0:T(128)} %bitcast.1.role_ref, bf16[2,512,768]{2,1,0:T(8,128)(2,1)} %get-tuple-element.92.q_ref, bf16[2,512,768]{2,1,0:T(8,128)(2,1)} %get-tuple-element.93.k_ref, ...), custom_call_target="tpu_custom_call" | custom-call | flops 12884901888 | bytes 18874368 | tf_op jit(solution)/shard_map/attend/pallas_call | solution.py:197
  199.5 4.3 fusion
  203.7 3.5 other_kv.7
  207.2 29.4 %attend.7 = (bf16[2,512,768]{2,1,0:T(8,128)(2,1)}, bf16[2,512,768]{2,1,0:T(8,128)(2,1)}, f32[2,512,768]{2,1,0:T(8,128)}, f32[2,512,768]{2,1,0:T(8,128)}, f32[2,6,4,512]{3,2,1,0:T(4,128)}) custom-call(s32[1]{0:T(128)} %bitcast.1.role_ref, bf16[2,512,768]{2,1,0:T(8,128)(2,1)} %get-tuple-element.122.q_ref, bf16[2,512,768]{2,1,0:T(8,128)(2,1)} %get-tuple-element.123.k_ref, ...), custom_call_target="tpu_custom_call" | custom-call | flops 12884901888 | bytes 18874368 | tf_op jit(solution)/shard_map/attend/pallas_call | solution.py:197
  236.6 4.2 bitcast_add_fusion.5
  247.9 1.5 bitcast_add_fusion.2
  253.8 4.3 post.4
  258.2 4.4 post.5
  262.5 4.4 post.6
  266.9 4.3 post.7
  272.7 2.5 dynamic-slice_add_fusion.3.rest_0_
  275.2 1.6 collective-permute-start.18
  276.8 2.5 dynamic-slice_add_fusion.2.rest_1_
  281.9 105.5 %collective-permute-done.18.st_ref = f32[2,6,4,512]{3,2,1,0:T(4,128)S(1)} collective-permute-done((f32[2,6,4,512]{3,2,1,0:T(4,128)S(1)}, f32[2,6,4,512]{3,2,1,0:T(4,128)S(1)}, u32[]{:S(2)}, u32[]{:S(2)}) %collective-permute-start.18) | collective-permute-done | bytes 98336 | tf_op jit(solution)/shard_map/ppermute | solution.py:371
  388.7 26.7 %late.4 = (bf16[2,512,768]{2,1,0:T(8,128)(2,1)}, bf16[2,512,768]{2,1,0:T(8,128)(2,1)}) custom-call(s32[1]{0:T(128)} %bitcast.1.role_ref, bf16[2,512,768]{2,1,0:T(8,128)(2,1)} %collective-permute-done.16.q_ref, bf16[2,512,768]{2,1,0:T(8,128)(2,1)} %collective-permute-done.17.g_ref, f32[2,6,4,512]{3,2,1,0:T(4,128)} %copy-done.68, ...), custom_call_target="tpu_custom_call" | custom-call | flops 6442450944 | bytes 15728640 | tf_op jit(solution)/shard_map/late/pallas_call | solution.py:255
  415.4 4.4 convolution_bitcast_fusion.5.rest_0_
  419.8 2.8 convolution_bitcast_fusion.4.rest_1_
  423.3 10.5 %back.4 = (bf16[2,256,768]{2,1,0:T(8,128)(2,1)}, bf16[2,256,768]{2,1,0:T(8,128)(2,1)}, f32[8,768]{1,0:T(8,128)}) custom-call(s32[1]{0:T(128)} %bitcast.core_ref, bf16[2,512,768]{2,1,0:T(8,128)(2,1)} %get-tuple-element.136.dq_ref, bf16[2,512,768]{2,1,0:T(8,128)(2,1)} %get-tuple-element.147.dk_ref, bf16[2,512,768]{2,1,0:T(8,128)(2,1)} %get-tuple-element.148.dv_ref, ...), custom_call_target="tpu_custom_call" | custom-call | flops 3623878656 | bytes 9437184 | tf_op jit(solution)/shard_map/back/pallas_call | solution.py:332
  436.4 20.5 %collective-permute-done.23.st_ref = f32[2,6,4,512]{3,2,1,0:T(4,128)S(1)} collective-permute-done((f32[2,6,4,512]{3,2,1,0:T(4,128)S(1)}, f32[2,6,4,512]{3,2,1,0:T(4,128)S(1)}, u32[]{:S(2)}, u32[]{:S(2)}) %collective-permute-start.23) | collective-permute-done | bytes 98336 | tf_op jit(solution)/shard_map/ppermute | solution.py:371
  458.2 26.6 %late.5 = (bf16[2,512,768]{2,1,0:T(8,128)(2,1)}, bf16[2,512,768]{2,1,0:T(8,128)(2,1)}) custom-call(s32[1]{0:T(128)} %bitcast.1.role_ref, bf16[2,512,768]{2,1,0:T(8,128)(2,1)} %collective-permute-done.21.q_ref, bf16[2,512,768]{2,1,0:T(8,128)(2,1)} %collective-permute-done.22.g_ref, f32[2,6,4,512]{3,2,1,0:T(4,128)} %copy-done.66, ...), custom_call_target="tpu_custom_call" | custom-call | flops 6442450944 | bytes 15728640 | tf_op jit(solution)/shard_map/late/pallas_call | solution.py:255
  484.8 4.4 convolution_bitcast_fusion.3.rest_0_
  489.2 2.8 convolution_bitcast_fusion.2.rest_1_
  492.1 10.5 %back.5 = (bf16[2,256,768]{2,1,0:T(8,128)(2,1)}, bf16[2,256,768]{2,1,0:T(8,128)(2,1)}, f32[8,768]{1,0:T(8,128)}) custom-call(s32[1]{0:T(128)} %bitcast.core_ref, bf16[2,512,768]{2,1,0:T(8,128)(2,1)} %get-tuple-element.144.dq_ref, bf16[2,512,768]{2,1,0:T(8,128)(2,1)} %get-tuple-element.154.dk_ref, bf16[2,512,768]{2,1,0:T(8,128)(2,1)} %get-tuple-element.155.dv_ref, ...), custom_call_target="tpu_custom_call" | custom-call | flops 3623878656 | bytes 9437184 | tf_op jit(solution)/shard_map/back/pallas_call | solution.py:332
  503.9 2.7 collective-permute-start.38
  506.6 20.0 %collective-permute-done.26.st_ref = f32[2,6,4,512]{3,2,1,0:T(4,128)} collective-permute-done((f32[2,6,4,512]{3,2,1,0:T(4,128)}, f32[2,6,4,512]{3,2,1,0:T(4,128)}, u32[]{:S(2)}, u32[]{:S(2)}) %collective-permute-start.26) | collective-permute-done | bytes 98336 | tf_op jit(solution)/shard_map/ppermute | solution.py:371
  526.5 26.6 %late.6 = (bf16[2,512,768]{2,1,0:T(8,128)(2,1)}, bf16[2,512,768]{2,1,0:T(8,128)(2,1)}) custom-call(s32[1]{0:T(128)} %bitcast.1.role_ref, bf16[2,512,768]{2,1,0:T(8,128)(2,1)} %collective-permute-done.24.q_ref, bf16[2,512,768]{2,1,0:T(8,128)(2,1)} %collective-permute-done.25.g_ref, f32[2,6,4,512]{3,2,1,0:T(4,128)} %collective-permute-done.26.st_ref, ...), custom_call_target="tpu_custom_call" | custom-call | flops 6442450944 | bytes 15728640 | tf_op jit(solution)/shard_map/late/pallas_call | solution.py:255
  553.2 4.4 convolution_bitcast_fusion.1.rest_0_
  557.6 2.9 convolution_bitcast_fusion.rest_1_
  560.5 10.4 %back.6 = (bf16[2,256,768]{2,1,0:T(8,128)(2,1)}, bf16[2,256,768]{2,1,0:T(8,128)(2,1)}, f32[8,768]{1,0:T(8,128)}) custom-call(s32[1]{0:T(128)} %bitcast.core_ref, bf16[2,512,768]{2,1,0:T(8,128)(2,1)} %get-tuple-element.145.dq_ref, bf16[2,512,768]{2,1,0:T(8,128)(2,1)} %get-tuple-element.161.dk_ref, bf16[2,512,768]{2,1,0:T(8,128)(2,1)} %get-tuple-element.162.dv_ref, ...), custom_call_target="tpu_custom_call" | custom-call | flops 3623878656 | bytes 9437184 | tf_op jit(solution)/shard_map/back/pallas_call | solution.py:332
  571.7 26.7 %late.7 = (bf16[2,512,768]{2,1,0:T(8,128)(2,1)}, bf16[2,512,768]{2,1,0:T(8,128)(2,1)}) custom-call(s32[1]{0:T(128)} %bitcast.1.role_ref, bf16[2,512,768]{2,1,0:T(8,128)(2,1)} %collective-permute-done.27.q_ref, bf16[2,512,768]{2,1,0:T(8,128)(2,1)} %collective-permute-done.28.g_ref, f32[2,6,4,512]{3,2,1,0:T(4,128)} %copy-done.67, ...), custom_call_target="tpu_custom_call" | custom-call | flops 6442450944 | bytes 15728640 | tf_op jit(solution)/shard_map/late/pallas_call | solution.py:255
  598.4 4.1 bitcast_add_fusion.1
  604.6 1.7 constant_dynamic-update-slice_fusion.7
  606.9 2.0 dynamic-slice_add_fusion.1.rest_0_
  609.0 1.7 bitcast_add_fusion
  618.0 19.8 %collective-permute-done.40 = f32[384,768]{1,0:T(8,128)S(1)} collective-permute-done((f32[384,768]{1,0:T(8,128)S(1)}, f32[384,768]{1,0:T(8,128)S(1)}, u32[]{:S(2)}, u32[]{:S(2)}) %collective-permute-start.40) | collective-permute-done | bytes 1179680 | tf_op jit(solution)/shard_map/ppermute | solution.py:371
  641.0 3.3 broadcast.4.clone.1
  644.3 2.0 copy-done.16
  647.3 15.8 %collective-permute-done.44 = f32[384,768]{1,0:T(8,128)S(1)} collective-permute-done((f32[384,768]{1,0:T(8,128)S(1)}, f32[384,768]{1,0:T(8,128)S(1)}, u32[]{:S(2)}, u32[]{:S(2)}) %collective-permute-start.44) | collective-permute-done | bytes 1179680 | tf_op jit(solution)/shard_map/ppermute | solution.py:371
  663.4 10.4 %back.7 = (bf16[2,256,768]{2,1,0:T(8,128)(2,1)}, bf16[2,256,768]{2,1,0:T(8,128)(2,1)}, f32[8,768]{1,0:T(8,128)}) custom-call(s32[1]{0:T(128)} %bitcast.core_ref, bf16[2,512,768]{2,1,0:T(8,128)(2,1)} %get-tuple-element.146.dq_ref, bf16[2,512,768]{2,1,0:T(8,128)(2,1)} %get-tuple-element.168.dk_ref, bf16[2,512,768]{2,1,0:T(8,128)(2,1)} %get-tuple-element.169.dv_ref, ...), custom_call_target="tpu_custom_call" | custom-call | flops 3623878656 | bytes 9437184 | tf_op jit(solution)/shard_map/back/pallas_call | solution.py:332
  674.4 2.4 constant_dynamic-update-slice_fusion.4
  676.7 10.6 %collective-permute-done.42 = f32[384,768]{1,0:T(8,128)S(1)} collective-permute-done((f32[384,768]{1,0:T(8,128)S(1)}, f32[384,768]{1,0:T(8,128)S(1)}, u32[]{:S(2)}, u32[]{:S(2)}) %collective-permute-start.42) | collective-permute-done | bytes 1179680 | tf_op jit(solution)/shard_map/ppermute | solution.py:371
  687.3 1.6 constant_dynamic-update-slice_fusion.3
  692.2 2.1 constant_dynamic-update-slice_fusion.11
  694.7 2.1 constant_dynamic-update-slice_fusion.10
  698.0 2.6 collective-permute-done.37
  703.4 2.1 constant_dynamic-update-slice_fusion.8
  706.9 3.2 constant_dynamic-update-slice_fusion.2
  (254 shorter events, 63.0 us)
Async XLA Ops:
  4.4 5.4 copy-start.45
  4.4 6.1 collective-permute-start.6
  7.2 4.6 collective-permute-start.7
  8.1 19.1 %collective-permute-start = (bf16[2,256,768]{2,1,0:T(8,128)(2,1)}, bf16[2,256,768]{2,1,0:T(8,128)(2,1)S(1)}, u32[]{:S(2)}, u32[]{:S(2)}) collective-permute-start(bf16[2,256,768]{2,1,0:T(8,128)(2,1)} %get-tuple-element.194), channel_id=1, source_target_pairs={{0,1},{1,0},{2,3},{3,2},{4,5},{5,4},{6,7},{7,6}} | collective-permute-start | bytes 2359304 | tf_op jit(solution)/shard_map/ppermute | solution.py:371
  8.1 19.3 %collective-permute-start.1 = (bf16[2,256,768]{2,1,0:T(8,128)(2,1)}, bf16[2,256,768]{2,1,0:T(8,128)(2,1)S(1)}, u32[]{:S(2)}, u32[]{:S(2)}) collective-permute-start(bf16[2,256,768]{2,1,0:T(8,128)(2,1)} %get-tuple-element.190), channel_id=1, source_target_pairs={{0,1},{1,0},{2,3},{3,2},{4,5},{5,4},{6,7},{7,6}} | collective-permute-start | bytes 2359304 | tf_op jit(solution)/shard_map/ppermute | solution.py:371
  8.6 29.5 %collective-permute-start.3 = (bf16[2,256,768]{2,1,0:T(8,128)(2,1)}, bf16[2,256,768]{2,1,0:T(8,128)(2,1)S(1)}, u32[]{:S(2)}, u32[]{:S(2)}) collective-permute-start(bf16[2,256,768]{2,1,0:T(8,128)(2,1)} %get-tuple-element.193), channel_id=1, source_target_pairs={{0,1},{1,0},{2,3},{3,2},{4,5},{5,4},{6,7},{7,6}} | collective-permute-start | bytes 2359304 | tf_op jit(solution)/shard_map/ppermute | solution.py:371
  11.3 28.2 %collective-permute-start.4 = (bf16[2,256,768]{2,1,0:T(8,128)(2,1)}, bf16[2,256,768]{2,1,0:T(8,128)(2,1)S(1)}, u32[]{:S(2)}, u32[]{:S(2)}) collective-permute-start(bf16[2,256,768]{2,1,0:T(8,128)(2,1)} %get-tuple-element.189), channel_id=1, source_target_pairs={{0,1},{1,0},{2,3},{3,2},{4,5},{5,4},{6,7},{7,6}} | collective-permute-start | bytes 2359304 | tf_op jit(solution)/shard_map/ppermute | solution.py:371
  21.6 45.1 %collective-permute-start.8 = (bf16[2,512,768]{2,1,0:T(8,128)(2,1)}, bf16[2,512,768]{2,1,0:T(8,128)(2,1)}, u32[]{:S(2)}, u32[]{:S(2)}) collective-permute-start(bf16[2,512,768]{2,1,0:T(8,128)(2,1)} %get-tuple-element.116), channel_id=1, source_target_pairs={{0,2},{1,3},{4,6},{5,7}} | collective-permute-start | bytes 4718600 | tf_op jit(solution)/shard_map/ppermute | solution.py:371
  27.1 24.4 %collective-permute-start.9 = (bf16[2,256,768]{2,1,0:T(8,128)(2,1)}, bf16[2,256,768]{2,1,0:T(8,128)(2,1)S(1)}, u32[]{:S(2)}, u32[]{:S(2)}) collective-permute-start(bf16[2,256,768]{2,1,0:T(8,128)(2,1)} %get-tuple-element.191), channel_id=1, source_target_pairs={{0,1},{1,0},{2,3},{3,2},{4,5},{5,4},{6,7},{7,6}} | collective-permute-start | bytes 2359304 | tf_op jit(solution)/shard_map/ppermute | solution.py:371
  27.4 24.1 %collective-permute-start.10 = (bf16[2,256,768]{2,1,0:T(8,128)(2,1)}, bf16[2,256,768]{2,1,0:T(8,128)(2,1)S(1)}, u32[]{:S(2)}, u32[]{:S(2)}) collective-permute-start(bf16[2,256,768]{2,1,0:T(8,128)(2,1)} %get-tuple-element.187), channel_id=1, source_target_pairs={{0,1},{1,0},{2,3},{3,2},{4,5},{5,4},{6,7},{7,6}} | collective-permute-start | bytes 2359304 | tf_op jit(solution)/shard_map/ppermute | solution.py:371
  38.1 127.4 %collective-permute-start.2 = (bf16[2,512,768]{2,1,0:T(8,128)(2,1)}, bf16[2,512,768]{2,1,0:T(8,128)(2,1)S(1)}, u32[]{:S(2)}, u32[]{:S(2)}) collective-permute-start(bf16[2,512,768]{2,1,0:T(8,128)(2,1)} %get-tuple-element.96), channel_id=1, source_target_pairs={{0,2},{1,3},{4,6},{5,7}} | collective-permute-start | bytes 4718600 | tf_op jit(solution)/shard_map/ppermute | solution.py:371
  50.1 78.4 %collective-permute-start.5 = (bf16[2,512,768]{2,1,0:T(8,128)(2,1)}, bf16[2,512,768]{2,1,0:T(8,128)(2,1)S(1)}, u32[]{:S(2)}, u32[]{:S(2)}) collective-permute-start(bf16[2,512,768]{2,1,0:T(8,128)(2,1)} %get-tuple-element.106), channel_id=1, source_target_pairs={{0,2},{1,3},{4,6},{5,7}} | collective-permute-start | bytes 4718600 | tf_op jit(solution)/shard_map/ppermute | solution.py:371
  63.0 140.7 %collective-permute-start.11 = (bf16[2,512,768]{2,1,0:T(8,128)(2,1)}, bf16[2,512,768]{2,1,0:T(8,128)(2,1)}, u32[]{:S(2)}, u32[]{:S(2)}) collective-permute-start(bf16[2,512,768]{2,1,0:T(8,128)(2,1)} %get-tuple-element.126), channel_id=1, source_target_pairs={{0,2},{1,3},{4,6},{5,7}} | collective-permute-start | bytes 4718600 | tf_op jit(solution)/shard_map/ppermute | solution.py:371
  65.5 213.9 %collective-permute-start.16 = (bf16[2,512,768]{2,1,0:T(8,128)(2,1)}, bf16[2,512,768]{2,1,0:T(8,128)(2,1)}, u32[]{:S(2)}, u32[]{:S(2)}) collective-permute-start(bf16[2,512,768]{2,1,0:T(8,128)(2,1)} %get-tuple-element.92.q_ref), channel_id=1, source_target_pairs={{2,0},{3,1},{6,4},{7,5}} | collective-permute-start | bytes 4718600 | tf_op jit(solution)/shard_map/ppermute | solution.py:371
  66.8 213.9 %collective-permute-start.17 = (bf16[2,512,768]{2,1,0:T(8,128)(2,1)}, bf16[2,512,768]{2,1,0:T(8,128)(2,1)}, u32[]{:S(2)}, u32[]{:S(2)}) collective-permute-start(bf16[2,512,768]{2,1,0:T(8,128)(2,1)} %get-tuple-element.95.g_ref), channel_id=1, source_target_pairs={{2,0},{3,1},{6,4},{7,5}} | collective-permute-start | bytes 4718600 | tf_op jit(solution)/shard_map/ppermute | solution.py:371
  71.7 29.4 %copy-start.20 = (bf16[2,512,768]{2,1,0:T(8,128)(2,1)S(1)}, bf16[2,512,768]{2,1,0:T(8,128)(2,1)}, u32[]{:S(2)}) copy-start(bf16[2,512,768]{2,1,0:T(8,128)(2,1)} %get-tuple-element.142.g_ref) | copy-start | bytes 4718596
  133.0 29.6 %copy-start.21 = (bf16[2,512,768]{2,1,0:T(8,128)(2,1)S(1)}, bf16[2,512,768]{2,1,0:T(8,128)(2,1)}, u32[]{:S(2)}) copy-start(bf16[2,512,768]{2,1,0:T(8,128)(2,1)} %get-tuple-element.141.g_ref) | copy-start | bytes 4718596
  170.1 29.4 %copy-start.23 = (bf16[2,512,768]{2,1,0:T(8,128)(2,1)S(1)}, bf16[2,512,768]{2,1,0:T(8,128)(2,1)}, u32[]{:S(2)}) copy-start(bf16[2,512,768]{2,1,0:T(8,128)(2,1)} %get-tuple-element.140.g_ref) | copy-start | bytes 4718596
  241.0 30.3 %collective-permute-start.19 = (f32[384,768]{1,0:T(8,128)S(1)}, f32[384,768]{1,0:T(8,128)}, u32[]{:S(2)}, u32[]{:S(2)}) collective-permute-start(f32[384,768]{1,0:T(8,128)S(1)} %constant_dynamic-slice_fusion.3), channel_id=1, source_target_pairs={{0,1},{1,0},{2,3},{3,2},{4,5},{5,4},{6,7},{7,6}} | collective-permute-start | bytes 3538952 | tf_op jit(solution)/shard_map/ppermute | solution.py:371
  252.0 23.2 %collective-permute-start.20 = (f32[384,768]{1,0:T(8,128)}, f32[384,768]{1,0:T(8,128)}, u32[]{:S(2)}, u32[]{:S(2)}) collective-permute-start(f32[384,768]{1,0:T(8,128)} %constant_dynamic-slice_fusion.2), channel_id=1, source_target_pairs={{0,1},{1,0},{2,3},{3,2},{4,5},{5,4},{6,7},{7,6}} | collective-permute-start | bytes 3538952 | tf_op jit(solution)/shard_map/ppermute | solution.py:371
  252.5 181.3 %collective-permute-start.21 = (bf16[2,512,768]{2,1,0:T(8,128)(2,1)}, bf16[2,512,768]{2,1,0:T(8,128)(2,1)}, u32[]{:S(2)}, u32[]{:S(2)}) collective-permute-start(bf16[2,512,768]{2,1,0:T(8,128)(2,1)} %get-tuple-element.102.q_ref), channel_id=1, source_target_pairs={{2,0},{3,1},{6,4},{7,5}} | collective-permute-start | bytes 4718600 | tf_op jit(solution)/shard_map/ppermute | solution.py:371
  271.3 5.5 copy-start.2
  271.3 163.8 %collective-permute-start.22 = (bf16[2,512,768]{2,1,0:T(8,128)(2,1)}, bf16[2,512,768]{2,1,0:T(8,128)(2,1)}, u32[]{:S(2)}, u32[]{:S(2)}) collective-permute-start(bf16[2,512,768]{2,1,0:T(8,128)(2,1)} %get-tuple-element.105.g_ref), channel_id=1, source_target_pairs={{2,0},{3,1},{6,4},{7,5}} | collective-permute-start | bytes 4718600 | tf_op jit(solution)/shard_map/ppermute | solution.py:371
  275.2 5.4 copy-start.52
  275.2 112.2 %copy-start.64 = (f32[2,6,4,512]{3,2,1,0:T(4,128)S(1)}, f32[2,6,4,512]{3,2,1,0:T(4,128)}, u32[]{:S(2)}) copy-start(f32[2,6,4,512]{3,2,1,0:T(4,128)} %get-tuple-element.150) | copy-start | bytes 294916
  275.2 112.2 %collective-permute-start.18 = (f32[2,6,4,512]{3,2,1,0:T(4,128)S(1)}, f32[2,6,4,512]{3,2,1,0:T(4,128)S(1)}, u32[]{:S(2)}, u32[]{:S(2)}) collective-permute-start(f32[2,6,4,512]{3,2,1,0:T(4,128)S(1)} %copy-done.65), channel_id=1, source_target_pairs={{2,0},{3,1},{6,4},{7,5}} | collective-permute-start | bytes 294920 | tf_op jit(solution)/shard_map/ppermute | solution.py:371
  279.3 223.2 %collective-permute-start.24 = (bf16[2,512,768]{2,1,0:T(8,128)(2,1)S(1)}, bf16[2,512,768]{2,1,0:T(8,128)(2,1)}, u32[]{:S(2)}, u32[]{:S(2)}) collective-permute-start(bf16[2,512,768]{2,1,0:T(8,128)(2,1)S(1)} %copy-done.53), channel_id=1, source_target_pairs={{2,0},{3,1},{6,4},{7,5}} | collective-permute-start | bytes 4718600 | tf_op jit(solution)/shard_map/ppermute | solution.py:371
  280.6 223.2 %collective-permute-start.25 = (bf16[2,512,768]{2,1,0:T(8,128)(2,1)S(1)}, bf16[2,512,768]{2,1,0:T(8,128)(2,1)}, u32[]{:S(2)}, u32[]{:S(2)}) collective-permute-start(bf16[2,512,768]{2,1,0:T(8,128)(2,1)S(1)} %copy-done.52), channel_id=1, source_target_pairs={{2,0},{3,1},{6,4},{7,5}} | collective-permute-start | bytes 4718600 | tf_op jit(solution)/shard_map/ppermute | solution.py:371
  387.4 69.5 %collective-permute-start.23 = (f32[2,6,4,512]{3,2,1,0:T(4,128)S(1)}, f32[2,6,4,512]{3,2,1,0:T(4,128)S(1)}, u32[]{:S(2)}, u32[]{:S(2)}) collective-permute-start(f32[2,6,4,512]{3,2,1,0:T(4,128)S(1)} %copy-done.64), channel_id=1, source_target_pairs={{2,0},{3,1},{6,4},{7,5}} | collective-permute-start | bytes 294920 | tf_op jit(solution)/shard_map/ppermute | solution.py:371
  388.7 26.7 %copy-start.58 = (bf16[2,512,768]{2,1,0:T(8,128)(2,1)S(1)}, bf16[2,512,768]{2,1,0:T(8,128)(2,1)}, u32[]{:S(2)}) copy-start(bf16[2,512,768]{2,1,0:T(8,128)(2,1)} %get-tuple-element.96) | copy-start | bytes 4718596
  423.3 11.8 %copy-start.54 = (bf16[2,512,768]{2,1,0:T(8,128)(2,1)S(1)}, bf16[2,512,768]{2,1,0:T(8,128)(2,1)}, u32[]{:S(2)}) copy-start(bf16[2,512,768]{2,1,0:T(8,128)(2,1)} %get-tuple-element.125.g_ref) | copy-start | bytes 4718596
  433.8 137.2 %collective-permute-start.27 = (bf16[2,512,768]{2,1,0:T(8,128)(2,1)}, bf16[2,512,768]{2,1,0:T(8,128)(2,1)}, u32[]{:S(2)}, u32[]{:S(2)}) collective-permute-start(bf16[2,512,768]{2,1,0:T(8,128)(2,1)} %get-tuple-element.122.q_ref), channel_id=1, source_target_pairs={{2,0},{3,1},{6,4},{7,5}} | collective-permute-start | bytes 4718600 | tf_op jit(solution)/shard_map/ppermute | solution.py:371
  435.1 135.9 %collective-permute-start.28 = (bf16[2,512,768]{2,1,0:T(8,128)(2,1)S(1)}, bf16[2,512,768]{2,1,0:T(8,128)(2,1)}, u32[]{:S(2)}, u32[]{:S(2)}) collective-permute-start(bf16[2,512,768]{2,1,0:T(8,128)(2,1)S(1)} %copy-done.54), channel_id=1, source_target_pairs={{2,0},{3,1},{6,4},{7,5}} | collective-permute-start | bytes 4718600 | tf_op jit(solution)/shard_map/ppermute | solution.py:371
  456.9 69.6 %collective-permute-start.26 = (f32[2,6,4,512]{3,2,1,0:T(4,128)}, f32[2,6,4,512]{3,2,1,0:T(4,128)}, u32[]{:S(2)}, u32[]{:S(2)}) collective-permute-start(f32[2,6,4,512]{3,2,1,0:T(4,128)} %get-tuple-element.157), channel_id=1, source_target_pairs={{2,0},{3,1},{6,4},{7,5}} | collective-permute-start | bytes 294920 | tf_op jit(solution)/shard_map/ppermute | solution.py:371
  458.2 26.6 %copy-start.56 = (bf16[2,512,768]{2,1,0:T(8,128)(2,1)S(1)}, bf16[2,512,768]{2,1,0:T(8,128)(2,1)}, u32[]{:S(2)}) copy-start(bf16[2,512,768]{2,1,0:T(8,128)(2,1)} %get-tuple-element.106) | copy-start | bytes 4718596
  492.1 10.5 %copy-start.63 = (f32[2,6,4,512]{3,2,1,0:T(4,128)S(1)}, f32[2,6,4,512]{3,2,1,0:T(4,128)}, u32[]{:S(2)}) copy-start(f32[2,6,4,512]{3,2,1,0:T(4,128)} %get-tuple-element.164) | copy-start | bytes 294916
  492.1 11.8 %copy-start.18 = (f32[384,768]{1,0:T(8,128)S(1)}, f32[384,768]{1,0:T(8,128)}, u32[]{:S(2)}) copy-start(f32[384,768]{1,0:T(8,128)} %dynamic-slice_add_fusion.2.rest_1_) | copy-start | bytes 3538948
  502.6 68.4 %collective-permute-start.29 = (f32[2,6,4,512]{3,2,1,0:T(4,128)S(1)}, f32[2,6,4,512]{3,2,1,0:T(4,128)S(1)}, u32[]{:S(2)}, u32[]{:S(2)}) collective-permute-start(f32[2,6,4,512]{3,2,1,0:T(4,128)S(1)} %copy-done.63), channel_id=1, source_target_pairs={{2,0},{3,1},{6,4},{7,5}} | collective-permute-start | bytes 294920 | tf_op jit(solution)/shard_map/ppermute | solution.py:371
  503.9 100.2 %collective-permute-start.38 = (f32[384,768]{1,0:T(8,128)S(1)}, f32[384,768]{1,0:T(8,128)}, u32[]{:S(2)}, u32[]{:S(2)}) collective-permute-start(f32[384,768]{1,0:T(8,128)S(1)} %copy-done.18), channel_id=1, source_target_pairs={{0,2},{1,3},{2,0},{3,1},{4,6},{5,7},{6,4},{7,5}} | collective-permute-start | bytes 3538952 | tf_op jit(solution)/shard_map/ppermute | solution.py:371
  526.5 26.6 %copy-start.51 = (bf16[2,512,768]{2,1,0:T(8,128)(2,1)S(1)}, bf16[2,512,768]{2,1,0:T(8,128)(2,1)}, u32[]{:S(2)}) copy-start(bf16[2,512,768]{2,1,0:T(8,128)(2,1)} %get-tuple-element.116) | copy-start | bytes 4718596
  571.6 26.7 %copy-start.6 = (f32[768,768]{1,0:T(8,128)S(1)}, f32[768,768]{1,0:T(8,128)}, u32[]{:S(2)}) copy-start(f32[768,768]{1,0:T(8,128)} %convolution_bitcast_fusion.5.rest_0_) | copy-start | bytes 7077892
  571.7 26.7 %copy-start.7 = (f32[768,768]{1,0:T(8,128)S(1)}, f32[768,768]{1,0:T(8,128)}, u32[]{:S(2)}) copy-start(f32[768,768]{1,0:T(8,128)} %convolution_bitcast_fusion.3.rest_0_) | copy-start | bytes 7077892
  603.6 3.3 collective-permute-start.30
  603.6 11.3 %collective-permute-start.12 = (bf16[2,256,768]{2,1,0:T(8,128)(2,1)}, bf16[2,256,768]{2,1,0:T(8,128)(2,1)S(1)}, u32[]{:S(2)}, u32[]{:S(2)}) collective-permute-start(bf16[2,256,768]{2,1,0:T(8,128)(2,1)} %get-tuple-element.132.rest_2_), channel_id=1, source_target_pairs={{0,1},{1,0},{2,3},{3,2},{4,5},{5,4},{6,7},{7,6}} | collective-permute-start | bytes 2359304 | tf_op jit(solution)/shard_map/ppermute | solution.py:371
  604.1 11.0 %collective-permute-start.13 = (bf16[2,256,768]{2,1,0:T(8,128)(2,1)}, bf16[2,256,768]{2,1,0:T(8,128)(2,1)S(1)}, u32[]{:S(2)}, u32[]{:S(2)}) collective-permute-start(bf16[2,256,768]{2,1,0:T(8,128)(2,1)} %get-tuple-element.133.rest_3_), channel_id=1, source_target_pairs={{0,1},{1,0},{2,3},{3,2},{4,5},{5,4},{6,7},{7,6}} | collective-permute-start | bytes 2359304 | tf_op jit(solution)/shard_map/ppermute | solution.py:371
  606.4 11.3 %collective-permute-start.39 = (f32[384,768]{1,0:T(8,128)S(1)}, f32[384,768]{1,0:T(8,128)S(1)}, u32[]{:S(2)}, u32[]{:S(2)}) collective-permute-start(f32[384,768]{1,0:T(8,128)S(1)} %get-tuple-element.186), channel_id=1, source_target_pairs={{0,1},{1,0},{2,3},{3,2},{4,5},{5,4},{6,7},{7,6}} | collective-permute-start | bytes 3538952 | tf_op jit(solution)/shard_map/ppermute | solution.py:371
  608.9 28.9 %copy-start.12 = (f32[384,768]{1,0:T(8,128)}, f32[384,768]{1,0:T(8,128)S(1)}, u32[]{:S(2)}) copy-start(f32[384,768]{1,0:T(8,128)S(1)} %dynamic-slice_add_fusion.1.rest_0_) | copy-start | bytes 3538948
  608.9 28.9 %collective-permute-start.40 = (f32[384,768]{1,0:T(8,128)S(1)}, f32[384,768]{1,0:T(8,128)S(1)}, u32[]{:S(2)}, u32[]{:S(2)}) collective-permute-start(f32[384,768]{1,0:T(8,128)S(1)} %dynamic-slice_add_fusion.1.rest_0_), channel_id=1, source_target_pairs={{0,2},{1,3},{2,0},{3,1},{4,6},{5,7},{6,4},{7,5}} | collective-permute-start | bytes 3538952 | tf_op jit(solution)/shard_map/ppermute | solution.py:371
  610.8 28.3 %collective-permute-start.31 = (f32[384,768]{1,0:T(8,128)S(1)}, f32[384,768]{1,0:T(8,128)S(1)}, u32[]{:S(2)}, u32[]{:S(2)}) collective-permute-start(f32[384,768]{1,0:T(8,128)S(1)} %constant_dynamic-slice_fusion), channel_id=1, source_target_pairs={{0,1},{1,0},{2,3},{3,2},{4,5},{5,4},{6,7},{7,6}} | collective-permute-start | bytes 3538952 | tf_op jit(solution)/shard_map/ppermute | solution.py:371
  615.0 24.2 %collective-permute-start.14 = (bf16[2,256,768]{2,1,0:T(8,128)(2,1)S(1)}, bf16[2,256,768]{2,1,0:T(8,128)(2,1)S(1)}, u32[]{:S(2)}, u32[]{:S(2)}) collective-permute-start(bf16[2,256,768]{2,1,0:T(8,128)(2,1)S(1)} %copy-done.62), channel_id=1, source_target_pairs={{0,1},{1,0},{2,3},{3,2},{4,5},{5,4},{6,7},{7,6}} | collective-permute-start | bytes 2359304 | tf_op jit(solution)/shard_map/ppermute | solution.py:371
  616.1 46.9 %collective-permute-start.44 = (f32[384,768]{1,0:T(8,128)S(1)}, f32[384,768]{1,0:T(8,128)S(1)}, u32[]{:S(2)}, u32[]{:S(2)}) collective-permute-start(f32[384,768]{1,0:T(8,128)S(1)} %copy-done.17), channel_id=1, source_target_pairs={{0,2},{1,3},{2,0},{3,1},{4,6},{5,7},{6,4},{7,5}} | collective-permute-start | bytes 3538952 | tf_op jit(solution)/shard_map/ppermute | solution.py:371
  617.7 21.7 %collective-permute-start.15 = (bf16[2,256,768]{2,1,0:T(8,128)(2,1)S(1)}, bf16[2,256,768]{2,1,0:T(8,128)(2,1)S(1)}, u32[]{:S(2)}, u32[]{:S(2)}) collective-permute-start(bf16[2,256,768]{2,1,0:T(8,128)(2,1)S(1)} %copy-done.61), channel_id=1, source_target_pairs={{0,1},{1,0},{2,3},{3,2},{4,5},{5,4},{6,7},{7,6}} | collective-permute-start | bytes 2359304 | tf_op jit(solution)/shard_map/ppermute | solution.py:371
  639.0 34.8 %collective-permute-start.41 = (f32[384,768]{1,0:T(8,128)}, f32[384,768]{1,0:T(8,128)}, u32[]{:S(2)}, u32[]{:S(2)}) collective-permute-start(f32[384,768]{1,0:T(8,128)} %get-tuple-element.184), channel_id=1, source_target_pairs={{0,1},{1,0},{2,3},{3,2},{4,5},{5,4},{6,7},{7,6}} | collective-permute-start | bytes 3538952 | tf_op jit(solution)/shard_map/ppermute | solution.py:371
  639.2 48.1 %collective-permute-start.42 = (f32[384,768]{1,0:T(8,128)S(1)}, f32[384,768]{1,0:T(8,128)S(1)}, u32[]{:S(2)}, u32[]{:S(2)}) collective-permute-start(f32[384,768]{1,0:T(8,128)S(1)} %dynamic-slice_add_fusion.rest_1_), channel_id=1, source_target_pairs={{0,2},{1,3},{2,0},{3,1},{4,6},{5,7},{6,4},{7,5}} | collective-permute-start | bytes 3538952 | tf_op jit(solution)/shard_map/ppermute | solution.py:371
  640.4 5.9 copy-start.16
  640.4 48.4 %collective-permute-start.32 = (bf16[2,256,768]{2,1,0:T(8,128)(2,1)}, bf16[2,256,768]{2,1,0:T(8,128)(2,1)}, u32[]{:S(2)}, u32[]{:S(2)}) collective-permute-start(bf16[2,256,768]{2,1,0:T(8,128)(2,1)} %get-tuple-element.171), channel_id=1, source_target_pairs={{0,1},{1,0},{2,3},{3,2},{4,5},{5,4},{6,7},{7,6}} | collective-permute-start | bytes 2359304 | tf_op jit(solution)/shard_map/ppermute | solution.py:371
  640.7 53.5 %collective-permute-start.33 = (bf16[2,256,768]{2,1,0:T(8,128)(2,1)}, bf16[2,256,768]{2,1,0:T(8,128)(2,1)}, u32[]{:S(2)}, u32[]{:S(2)}) collective-permute-start(bf16[2,256,768]{2,1,0:T(8,128)(2,1)} %get-tuple-element.172), channel_id=1, source_target_pairs={{0,1},{1,0},{2,3},{3,2},{4,5},{5,4},{6,7},{7,6}} | collective-permute-start | bytes 2359304 | tf_op jit(solution)/shard_map/ppermute | solution.py:371
  663.0 34.1 %collective-permute-start.34 = (bf16[2,256,768]{2,1,0:T(8,128)(2,1)}, bf16[2,256,768]{2,1,0:T(8,128)(2,1)S(1)}, u32[]{:S(2)}, u32[]{:S(2)}) collective-permute-start(bf16[2,256,768]{2,1,0:T(8,128)(2,1)} %get-tuple-element.173), channel_id=1, source_target_pairs={{0,1},{1,0},{2,3},{3,2},{4,5},{5,4},{6,7},{7,6}} | collective-permute-start | bytes 2359304 | tf_op jit(solution)/shard_map/ppermute | solution.py:371
  673.8 13.5 %copy-start.14 = (f32[384,768]{1,0:T(8,128)S(1)}, f32[384,768]{1,0:T(8,128)}, u32[]{:S(2)}) copy-start(f32[384,768]{1,0:T(8,128)} %copy-done.13) | copy-start | bytes 3538948
  673.8 29.6 %collective-permute-start.35 = (bf16[2,256,768]{2,1,0:T(8,128)(2,1)}, bf16[2,256,768]{2,1,0:T(8,128)(2,1)}, u32[]{:S(2)}, u32[]{:S(2)}) collective-permute-start(bf16[2,256,768]{2,1,0:T(8,128)(2,1)} %get-tuple-element.174), channel_id=1, source_target_pairs={{0,1},{1,0},{2,3},{3,2},{4,5},{5,4},{6,7},{7,6}} | collective-permute-start | bytes 2359304 | tf_op jit(solution)/shard_map/ppermute | solution.py:371
  687.3 18.2 %collective-permute-start.45 = (f32[384,768]{1,0:T(8,128)S(1)}, f32[384,768]{1,0:T(8,128)}, u32[]{:S(2)}, u32[]{:S(2)}) collective-permute-start(f32[384,768]{1,0:T(8,128)S(1)} %get-tuple-element.180), channel_id=1, source_target_pairs={{0,1},{1,0},{2,3},{3,2},{4,5},{5,4},{6,7},{7,6}} | collective-permute-start | bytes 3538952 | tf_op jit(solution)/shard_map/ppermute | solution.py:371
  688.9 18.0 %collective-permute-start.43 = (f32[384,768]{1,0:T(8,128)}, f32[384,768]{1,0:T(8,128)}, u32[]{:S(2)}, u32[]{:S(2)}) collective-permute-start(f32[384,768]{1,0:T(8,128)} %get-tuple-element.182), channel_id=1, source_target_pairs={{0,1},{1,0},{2,3},{3,2},{4,5},{5,4},{6,7},{7,6}} | collective-permute-start | bytes 3538952 | tf_op jit(solution)/shard_map/ppermute | solution.py:371
  694.3 2.5 collective-permute-start.36
  696.8 3.8 collective-permute-start.37
  (51 other events, 120.8 us)

commit v2 on v1

v2 whole, which is shorter than its diff:
```python
import functools

import jax
import jax.numpy as jnp
from jax import lax
from jax.experimental import pallas as pl
from jax.experimental.pallas import tpu as pltpu
from jax.sharding import PartitionSpec as P


LN_EPS = 1e-5
F32 = jnp.float32
BF16 = jnp.bfloat16
CHUNKS = 4
UP = [(0, 2), (1, 3)]
DOWN = [(2, 0), (3, 1)]
SWAP_CHIP = [(0, 2), (1, 3), (2, 0), (3, 1)]
SWAP_CORE = [(0, 1), (1, 0), (2, 3), (3, 2)]


UNREAD = pl.BlockSpec(memory_space=pltpu.HBM)


def dot_nn(a, b):
    return lax.dot_general(a, b, (((1,), (0,)), ((), ())), preferred_element_type=F32)


def dot_nt(a, b):
    return lax.dot_general(a, b, (((1,), (1,)), ((), ())), preferred_element_type=F32)


def params(n):
    return pltpu.CompilerParams(dimension_semantics=("arbitrary",) * n, vmem_limit_bytes=56 * 1024 * 1024)


def normed(x_f):
    centred = x_f - jnp.mean(x_f, axis=-1, keepdims=True)
    inv_std = lax.rsqrt(jnp.mean(centred * centred, axis=-1, keepdims=True) + LN_EPS)
    return centred * inv_std, inv_std


def front_kernel(core_ref, x_ref, xr_ref, g_ref, gr_ref, lng_ref, lnb_ref, w_ref, b_ref, wo_ref,
                 h_ref, qd_ref, k_ref, v_ref, xb_ref, gb_ref):
    dim = x_ref.shape[2]
    run = x_ref.shape[1]
    mine = pl.ds(pl.multiple_of(core_ref[0] * run, run), run)
    theirs = pl.ds(pl.multiple_of((1 - core_ref[0]) * run, run), run)
    xb_ref[0, mine, :] = x_ref[0]
    xb_ref[0, theirs, :] = xr_ref[0]
    gb_ref[0, mine, :] = g_ref[0]
    gb_ref[0, theirs, :] = gr_ref[0]
    qd_ref[0, 0] = dot_nt(gb_ref[0], wo_ref[...]).astype(BF16)
    x_hat, _ = normed(xb_ref[0].astype(F32))
    h_ref[0] = (x_hat * lng_ref[...] + lnb_ref[...]).astype(BF16)
    for t in range(3):
        cols = slice(t * dim, (t + 1) * dim)
        val = (dot_nt(h_ref[0], w_ref[cols, :]) + b_ref[:, cols]).astype(BF16)
        if t == 0:
            qd_ref[1, 0] = val
        else:
            (k_ref if t == 1 else v_ref)[0] = val


def front(core, x, x_r, g, g_r, ln_g, ln_b, w_t, b_qkv, w_o, lo):
    batch, run, dim = x.shape
    n, seq = x_r.shape[0], 2 * run
    whole = lambda shape: pl.BlockSpec(shape, lambda b, c: (0,) * len(shape))
    own = pl.BlockSpec((1, run, dim), lambda b, c: (c[0] * (batch // 2) + lo + b, 0, 0))
    got = pl.BlockSpec((1, run, dim), lambda b, c: (b, 0, 0))
    tok = pl.BlockSpec((1, seq, dim), lambda b, c: (b, 0, 0))
    out = jax.ShapeDtypeStruct((n, seq, dim), BF16)
    return pl.pallas_call(
        front_kernel,
        grid_spec=pltpu.PrefetchScalarGridSpec(
            num_scalar_prefetch=1,
            grid=(n,),
            in_specs=[own, got, own, got, whole((1, dim)), whole((1, dim)), whole((3 * dim, dim)), whole((1, 3 * dim)), whole((dim, dim))],
            out_specs=[tok, pl.BlockSpec((2, 1, seq, dim), lambda b, c: (0, b, 0, 0)), tok, tok, tok, tok],
        ),
        out_shape=[out, jax.ShapeDtypeStruct((2, n, seq, dim), BF16), out, out, out, out],
        compiler_params=params(1),
        cost_estimate=pl.CostEstimate(flops=8 * n * seq * dim * dim, bytes_accessed=18 * n * seq * dim, transcendentals=0),
        name="front",
    )(core, x, x_r, g, g_r, ln_g, ln_b, w_t, b_qkv, w_o)


def kv_kernel(role_ref, h_ref, w_ref, b_ref, k_ref, v_ref):
    dim = h_ref.shape[2]

    @pl.when(role_ref[0] == 1)
    def _():
        for t, out in enumerate((k_ref, v_ref)):
            cols = slice((t + 1) * dim, (t + 2) * dim)
            out[0] = (dot_nt(h_ref[0], w_ref[cols, :]) + b_ref[:, cols]).astype(BF16)


def other_kv(role, h_o, w_t, b_qkv):
    n, seq, dim = h_o.shape
    tok = pl.BlockSpec((1, seq, dim), lambda b, r: (b * r[0], 0, 0))
    out = jax.ShapeDtypeStruct((n, seq, dim), BF16)
    return pl.pallas_call(
        kv_kernel,
        grid_spec=pltpu.PrefetchScalarGridSpec(
            num_scalar_prefetch=1,
            grid=(n,),
            in_specs=[tok, pl.BlockSpec((3 * dim, dim), lambda b, r: (0, 0)), pl.BlockSpec((1, 3 * dim), lambda b, r: (0, 0))],
            out_specs=[tok] * 2,
        ),
        out_shape=[out] * 2,
        compiler_params=params(1),
        cost_estimate=pl.CostEstimate(flops=4 * n * seq * dim * dim, bytes_accessed=6 * n * seq * dim, transcendentals=0),
        name="other_kv",
    )(role, h_o, w_t, b_qkv)


def head_only(z, h, head):
    lane = lax.broadcasted_iota(jnp.int32, z.shape, 1)
    return jnp.where((lane >= h * head) & (lane < (h + 1) * head), z, jnp.zeros_like(z))


def attn_kernel(role_ref, q_ref, g_ref, k_ref, v_ref, ko_ref, vo_ref, *rest, head, scale):
    a_ref, dq_ref, dk_ref, dv_ref, dkb_ref, dvb_ref, st_ref = rest[-7:]
    seq, width = k_ref.shape[1:]
    blk = seq // 2
    causal = lax.broadcasted_iota(jnp.int32, (blk, blk), 0) <= lax.broadcasted_iota(jnp.int32, (blk, blk), 1)

    def run(rect):
        k_t, v_t = k_ref[0].T, v_ref[0].T
        if rect:
            ko_t, vo_t = ko_ref[0].T, vo_ref[0].T
        for qi in range(2):
            rows = slice(qi * blk, (qi + 1) * blk)
            near = (qi + 1) * blk
            q2 = q_ref[0, 0, rows, :] * jnp.asarray(scale, BF16)
            g2 = g_ref[0, 0, rows, :]
            o_parts, dq_parts, p_near, ds_near, q_only, g_only = [], [], [], [], [], []
            for h in range(width // head):
                hrow = slice(h * head, (h + 1) * head)
                qm, gm = head_only(q2, h, head), head_only(g2, h, head)

                def products(mine, far, z):
                    near_z = dot_nt(mine[0, :near, :], z)
                    parts = [near_z] if qi == 0 else [near_z[:blk], near_z[blk:]]
                    return parts + ([dot_nt(far[0], z)] if rect else [])

                s = products(k_ref, ko_ref, qm)
                s[qi] = jnp.where(causal, s[qi], -jnp.inf)
                m = functools.reduce(jnp.maximum, [jnp.max(s_i, axis=0, keepdims=True) for s_i in s])
                e = [jnp.exp(s_i - m) for s_i in s]
                dp = products(v_ref, vo_ref, gm)
                l = functools.reduce(jnp.add, [jnp.sum(e_i, axis=0, keepdims=True) for e_i in e])
                c = functools.reduce(jnp.add, [jnp.sum(e_i * d_i, axis=0, keepdims=True) for e_i, d_i in zip(e, dp)])
                inv_l = 1.0 / l
                c = c * inv_l
                st_ref[0, 0, 2 * h, rows] = (m + jnp.log(l))[0]
                st_ref[0, 0, 2 * h + 1, rows] = c[0]
                p = [e_i * inv_l for e_i in e]
                ds = [(p_i * (d_i - c)).astype(BF16) for p_i, d_i in zip(p, dp)]
                p = [p_i.astype(BF16) for p_i in p]
                kt_h, vt_h = k_t[hrow, :near], v_t[hrow, :near]
                if rect:
                    kt_h = jnp.concatenate([kt_h, ko_t[hrow]], axis=1)
                    vt_h = jnp.concatenate([vt_h, vo_t[hrow]], axis=1)
                o_parts.append(dot_nn(vt_h, jnp.concatenate(p, axis=0)))
                dq_parts.append(dot_nn(kt_h, jnp.concatenate(ds, axis=0)))
                p_near.append(jnp.concatenate(p[:qi + 1], axis=0))
                ds_near.append(jnp.concatenate(ds[:qi + 1], axis=0))
                q_only.append(qm)
                g_only.append(gm)
            a_ref[0, rows, :] = jnp.concatenate(o_parts, axis=0).T.astype(BF16)
            dq_ref[0, rows, :] = (jnp.concatenate(dq_parts, axis=0).T * scale).astype(BF16)
            for acc_ref, parts, other in ((dk_ref, ds_near, q_only), (dv_ref, p_near, g_only)):
                val = dot_nn(jnp.concatenate(parts, axis=1), jnp.concatenate(other, axis=0))
                if qi == 0:
                    acc_ref[0, :blk, :] = val
                else:
                    acc_ref[0, :blk, :] += val[:blk]
                    acc_ref[0, blk:, :] = val[blk:]
        if rect:
            dkb_ref[0] = dk_ref[0].astype(BF16)
            dvb_ref[0] = dv_ref[0].astype(BF16)

    pl.when(role_ref[0] == 0)(lambda: run(False))
    pl.when(role_ref[0] == 1)(lambda: run(True))


def attend(role, qd, k, v, lo, k_o, v_o, head, after):
    n, seq, dim = k_o.shape
    width = 128
    pairs = dim // width
    pick = lambda t: pl.BlockSpec((1, 1, seq, width), lambda b, p, r: (t, b + lo, 0, p))
    tok_in = pl.BlockSpec((1, seq, width), lambda b, p, r: (b + lo, 0, p))
    tok = pl.BlockSpec((1, seq, width), lambda b, p, r: (b, 0, p))
    high = pl.BlockSpec((1, seq, width), lambda b, p, r: (b * r[0], 0, p * r[0]))
    low = pl.BlockSpec((1, seq, width), lambda b, p, r: (b * (1 - r[0]), 0, p * (1 - r[0])))
    narrow = jax.ShapeDtypeStruct((n, seq, dim), BF16)
    acc = jax.ShapeDtypeStruct((n, seq, dim), F32)
    return pl.pallas_call(
        functools.partial(attn_kernel, head=head, scale=head ** -0.5),
        grid_spec=pltpu.PrefetchScalarGridSpec(
            num_scalar_prefetch=1,
            grid=(n, pairs),
            in_specs=[pick(1), pick(0), tok_in, tok_in, high, high] + [UNREAD] * len(after),
            out_specs=[tok, tok, low, low, high, high, pl.BlockSpec((1, 1, 4, seq), lambda b, p, r: (b, p, 0, 0))],
        ),
        out_shape=[narrow, narrow, acc, acc, narrow, narrow, jax.ShapeDtypeStruct((n, pairs, 4, seq), F32)],
        compiler_params=params(2),
        cost_estimate=pl.CostEstimate(flops=32 * n * seq * seq * dim, bytes_accessed=24 * n * seq * dim, transcendentals=0),
        name="attend",
    )(role, qd, qd, k, v, k_o, v_o, *after)


def late_kernel(role_ref, q_ref, g_ref, st_ref, k_ref, v_ref, dka_ref, dva_ref, dkb_ref, dvb_ref, *rest, head, scale):
    dk_ref, dv_ref = rest[-2:]
    seq, width = k_ref.shape[1:]
    blk = seq // 2

    @pl.when(role_ref[0] == 1)
    def _():
        dk_ref[0] = dkb_ref[0]
        dv_ref[0] = dvb_ref[0]

    @pl.when(role_ref[0] == 0)
    def _():
        dk, dv = dka_ref[0], dva_ref[0]
        for qi in range(2):
            rows = slice(qi * blk, (qi + 1) * blk)
            q2 = q_ref[0, 0, rows, :] * jnp.asarray(scale, BF16)
            g2 = g_ref[0, 0, rows, :]
            ps, dss, q_only, g_only = [], [], [], []
            for h in range(width // head):
                qm, gm = head_only(q2, h, head), head_only(g2, h, head)
                lse = st_ref[0, 0, 2 * h, rows].reshape(1, blk)
                c = st_ref[0, 0, 2 * h + 1, rows].reshape(1, blk)
                p = jnp.exp(dot_nt(k_ref[0], qm) - lse)
                dss.append((p * (dot_nt(v_ref[0], gm) - c)).astype(BF16))
                ps.append(p.astype(BF16))
                q_only.append(qm)
                g_only.append(gm)
            dv = dv + dot_nn(jnp.concatenate(ps, axis=1), jnp.concatenate(g_only, axis=0))
            dk = dk + dot_nn(jnp.concatenate(dss, axis=1), jnp.concatenate(q_only, axis=0))
        dk_ref[0] = dk.astype(BF16)
        dv_ref[0] = dv.astype(BF16)


def late(role, qd_o, stats, k, v, lo, dk_acc, dv_acc, dk_b, dv_b, head, after):
    n, seq, dim = dk_acc.shape
    width = 128
    pairs = dim // width
    pick = lambda t: pl.BlockSpec((1, 1, seq, width), lambda b, p, r: (t, b * (1 - r[0]), 0, p * (1 - r[0])))
    low_in = pl.BlockSpec((1, seq, width), lambda b, p, r: (lo + b * (1 - r[0]), 0, p * (1 - r[0])))
    low = pl.BlockSpec((1, seq, width), lambda b, p, r: (b * (1 - r[0]), 0, p * (1 - r[0])))
    first = pl.BlockSpec((1, seq, width), lambda b, p, r: (0, 0, 0))
    narrow = jax.ShapeDtypeStruct((n, seq, dim), BF16)
    return pl.pallas_call(
        functools.partial(late_kernel, head=head, scale=head ** -0.5),
        grid_spec=pltpu.PrefetchScalarGridSpec(
            num_scalar_prefetch=1,
            grid=(n, pairs),
            in_specs=[pick(1), pick(0), pl.BlockSpec((1, 1, 4, seq), lambda b, p, r: (b, p, 0, 0)), low_in, low_in, low, low, first, first] + [UNREAD] * len(after),
            out_specs=[low] * 2,
        ),
        out_shape=[narrow] * 2,
        input_output_aliases={8: 0, 9: 1},
        compiler_params=params(2),
        cost_estimate=pl.CostEstimate(flops=16 * n * seq * seq * dim, bytes_accessed=20 * n * seq * dim, transcendentals=0),
        name="late",
    )(role, qd_o, qd_o, stats, k, v, dk_acc, dv_acc, dk_b, dv_b, *after)


def split_rows(core_ref, full_ref, own_ref, send_ref):
    run = own_ref.shape[1]
    own_ref[0] = full_ref[pl.ds(pl.multiple_of(core_ref[0] * run, run), run), :]
    send_ref[0] = full_ref[pl.ds(pl.multiple_of((1 - core_ref[0]) * run, run), run), :]


def post_kernel(core_ref, a_ref, x_ref, wo_ref, bo_ref, *rest):
    own_ref, send_ref, full_ref = rest[-3:]
    out = dot_nn(a_ref[0], wo_ref[...]) + bo_ref[...]
    full_ref[...] = (x_ref[0].astype(F32) + out).astype(BF16)
    split_rows(core_ref, full_ref, own_ref, send_ref)


def row_outputs(batch, run, dim, first):
    own = pl.BlockSpec((1, run, dim), lambda b, c: (c[0] * (batch // 2) + first + b, 0, 0))
    other = pl.BlockSpec((1, run, dim), lambda b, c: (first + b, 0, 0))
    return [own, other], [jax.ShapeDtypeStruct((batch, run, dim), BF16), jax.ShapeDtypeStruct((batch // 2, run, dim), BF16)]


def post(core, a, x, lo, w_o, b_o, batch, first, prev):
    n, seq, dim = a.shape
    run = seq // 2
    tok = pl.BlockSpec((1, seq, dim), lambda b, c: (b, 0, 0))
    tok_in = pl.BlockSpec((1, seq, dim), lambda b, c: (b + lo, 0, 0))
    whole = lambda shape: pl.BlockSpec(shape, lambda b, c: (0,) * len(shape))
    specs, shapes = row_outputs(batch, run, dim, first)
    return pl.pallas_call(
        post_kernel,
        grid_spec=pltpu.PrefetchScalarGridSpec(
            num_scalar_prefetch=1,
            grid=(n,),
            in_specs=[tok, tok_in, whole((dim, dim)), whole((1, dim))] + [UNREAD] * len(prev),
            out_specs=specs,
            scratch_shapes=[pltpu.VMEM((seq, dim), BF16)],
        ),
        out_shape=shapes,
        input_output_aliases={5 + i: i for i in range(len(prev))},
        compiler_params=params(1),
        cost_estimate=pl.CostEstimate(flops=2 * n * seq * dim * dim, bytes_accessed=6 * n * seq * dim, transcendentals=0),
        name="post",
    )(core, a, x, w_o, b_o, *prev)


def back_kernel(core_ref, dq_ref, dk_ref, dv_ref, x_ref, g_ref, lng_ref, w_ref, prev_ref, *rest):
    own_ref, send_ref, acc_ref, full_ref = rest[-4:]
    dim = x_ref.shape[2]

    @pl.when(pl.program_id(0) == 0)
    def _():
        acc_ref[...] = prev_ref[...]

    dh = dot_nn(dq_ref[0], w_ref[0:dim, :]) + dot_nn(dk_ref[0], w_ref[dim:2 * dim, :]) + dot_nn(dv_ref[0], w_ref[2 * dim:3 * dim, :])
    x_hat, inv_std = normed(x_ref[0].astype(F32))
    g = g_ref[0].astype(F32)
    u = dh * lng_ref[...]
    dx = inv_std * (u - jnp.mean(u, axis=-1, keepdims=True) - x_hat * jnp.mean(u * x_hat, axis=-1, keepdims=True))
    full_ref[...] = (g + dx).astype(BF16)
    split_rows(core_ref, full_ref, own_ref, send_ref)
    acc_ref[0:1, :] += jnp.sum(dh * x_hat, axis=0, keepdims=True)
    acc_ref[1:2, :] += jnp.sum(dh, axis=0, keepdims=True)
    for t, ref in enumerate((dq_ref, dk_ref, dv_ref)):
        acc_ref[2 + t:3 + t, :] += jnp.sum(ref[0].astype(F32), axis=0, keepdims=True)
    acc_ref[5:6, :] += jnp.sum(g, axis=0, keepdims=True)


def back(core, dq, dk, dv, x, g, lo, ln_g, w_t, acc, batch, first, prev, after):
    n, seq, dim = dq.shape
    run = seq // 2
    tok = pl.BlockSpec((1, seq, dim), lambda b, c: (b, 0, 0))
    tok_in = pl.BlockSpec((1, seq, dim), lambda b, c: (b + lo, 0, 0))
    whole = lambda shape: pl.BlockSpec(shape, lambda b, c: (0,) * len(shape))
    specs, shapes = row_outputs(batch, run, dim, first)
    return pl.pallas_call(
        back_kernel,
        grid_spec=pltpu.PrefetchScalarGridSpec(
            num_scalar_prefetch=1,
            grid=(n,),
            in_specs=[tok] * 3 + [tok_in] * 2 + [whole((1, dim)), whole((3 * dim, dim)), whole((8, dim))] + [UNREAD] * (len(prev) + len(after)),
            out_specs=specs + [whole((8, dim))],
            scratch_shapes=[pltpu.VMEM((seq, dim), BF16)],
        ),
        out_shape=shapes + [jax.ShapeDtypeStruct((8, dim), F32)],
        input_output_aliases={9 + i: i for i in range(len(prev))},
        compiler_params=params(1),
        cost_estimate=pl.CostEstimate(flops=6 * n * seq * dim * dim, bytes_accessed=12 * n * seq * dim, transcendentals=0),
        name="back",
    )(core, dq, dk, dv, x, g, ln_g, w_t, acc, *prev, *after)


def tok_dot(a, b):
    return lax.dot_general(a, b, (((0, 1), (0, 1)), ((), ())), preferred_element_type=F32)


def solution(mesh):
    tok_spec = P('dp', 'sp', None)
    part_spec = P('dp')

    def local_step(x, g, ln_g, ln_b, w_qkv, b_qkv, w_out, b_out):
        batch, _, dim = x.shape
        _, _, heads, head = w_qkv.shape
        index = lax.axis_index('sp')
        chip, core = lax.div(index, 2), lax.rem(index, 2)
        role, side = chip.reshape(1), core.reshape(1)
        ln_g2, ln_b2, b_o = ln_g.reshape(1, dim), ln_b.reshape(1, dim), b_out.reshape(1, dim)
        w_t = jnp.transpose(w_qkv, (1, 2, 3, 0)).reshape(3 * dim, dim)
        w_o = w_out.reshape(dim, dim)
        b_all = b_qkv.reshape(1, 3 * dim)
        half_b = batch // 2
        n = half_b // CHUNKS
        half_d = dim // 2

        def send(z, perm):
            return lax.ppermute(z, 'sp', perm)

        def handed(z, lo, count):
            return send(lax.dynamic_slice_in_dim(z, (1 - core) * half_b + lo, count, 0), SWAP_CORE)

        spans = ((0, n), (n, half_b - n))
        got = [(handed(g, *span), handed(x, *span)) for span in spans]
        fronts = []
        for j, (lo, _) in enumerate(spans):
            fronts.append(front(side, x, got[j][1], g, got[j][0], ln_g2, ln_b2, w_t, b_all, w_o, lo))
        own, far = [], []
        for i in range(CHUNKS):
            group, lo = fronts[min(i, 1)], max(i - 1, 0) * n
            own.append((group, lo))
            h, qd = group[0][lo:lo + n], group[1][:, lo:lo + n]
            far.append((send(h, UP), send(qd, DOWN)))

        def halves_added(w):
            theirs = send(lax.dynamic_slice_in_dim(w, (1 - core) * half_d, half_d, 0), SWAP_CORE)
            return lax.dynamic_slice_in_dim(w, core * half_d, half_d, 0) + theirs

        att, stats = {}, {}
        dw = {}
        d_x, acc = [], jnp.zeros((8, dim), F32)

        def add_to(name, part):
            dw[name] = part if name not in dw else dw[name] + part

        def forward(i, after):
            (h, qd, k, v, xb, gb), lo = own[i]
            k_o, v_o = other_kv(role, far[i][0], w_t, b_all)
            att[i] = attend(role, qd, k, v, lo, k_o, v_o, head, after)
            stats[i] = send(att[i][6], DOWN)

        def backward(i, after, d_x, acc):
            (h, qd, k, v, xb, gb), lo = own[i]
            _, dq, dk_acc, dv_acc, dk_b, dv_b, _ = att[i]
            dk, dv = late(role, far[i][1], stats[i], k, v, lo, dk_acc, dv_acc, dk_b, dv_b, head, after)
            dwk, dwv = tok_dot(dk, h[lo:lo + n]), tok_dot(dv, h[lo:lo + n])
            add_to('k', dwk)
            add_to('v', dwv)
            after = [dwk, dwv]
            if i == CHUNKS - 1:
                after = [halves_added(dw['k']), halves_added(dw['v'])]
            *d_x, acc = back(side, dq, dk, dv, xb, gb, lo, ln_g2, w_t, acc, batch, i * n, d_x, after)
            return d_x, acc, after

        for i in range(CHUNKS - 1):
            forward(i, [])
        d_x, acc, _ = backward(0, [att[CHUNKS - 2][6]], d_x, acc)
        forward(CHUNKS - 1, [acc])
        d_x, acc, _ = backward(1, [att[CHUNKS - 1][6]], d_x, acc)
        y = []
        for i in range(CHUNKS):
            (h, qd, k, v, xb, gb), lo = own[i]
            y = post(side, att[i][0], xb, lo, w_o, b_o, batch, i * n, y)
            add_to('o', tok_dot(att[i][0], gb[lo:lo + n]))
            add_to('q', tok_dot(att[i][1], h[lo:lo + n]))
        d_x, acc, _ = backward(2, [acc, y[1]], d_x, acc)
        part_o, part_q = halves_added(dw['o']), halves_added(dw['q'])
        sum_o = part_o + send(part_o, SWAP_CHIP)
        sum_q = part_q + send(part_q, SWAP_CHIP)
        d_x, acc, (part_k, part_v) = backward(3, [acc, part_o, part_q], d_x, acc)
        sum_k = part_k + send(part_k, SWAP_CHIP)
        sum_v = part_v + send(part_v, SWAP_CHIP)

        def joined(own_rows, other_rows):
            return lax.dynamic_update_slice_in_dim(own_rows, send(other_rows, SWAP_CORE), (1 - core) * half_b, 0)

        y, d_x = joined(*y), joined(*d_x)
        acc = acc + send(acc, SWAP_CORE)
        acc = acc + send(acc, SWAP_CHIP)

        d_w_out = jnp.zeros((dim, dim), F32)
        d_w_out = lax.dynamic_update_slice(d_w_out, sum_o, (core * half_d, 0))
        d_w_out = lax.dynamic_update_slice(d_w_out, send(sum_o, SWAP_CORE), ((1 - core) * half_d, 0))
        dwt = jnp.zeros((3 * dim, dim), F32)
        for t, w in enumerate((sum_q, sum_k, sum_v)):
            dwt = lax.dynamic_update_slice(dwt, w, (t * dim + core * half_d, 0))
            dwt = lax.dynamic_update_slice(dwt, send(w, SWAP_CORE), (t * dim + (1 - core) * half_d, 0))
        d_w_qkv = jnp.transpose(dwt.reshape(3, heads, head, dim), (3, 0, 1, 2))
        return y, d_x, acc[0], acc[1], d_w_qkv, acc[2:5].reshape(3, heads, head), d_w_out.reshape(heads, head, dim), acc[5]


    return jax.shard_map(local_step, mesh=mesh, in_specs=(tok_spec, tok_spec) + (P(),) * 6, out_specs=(tok_spec, tok_spec) + (part_spec,) * 6, check_vma=False)
```

time: 720 us -> 731 us (1.015)
  Pallas kernels: 336 us -> 313 us
  starting transfers between devices: 38.4 us -> 56 us
  other arithmetic: 11.9 us -> 21.8 us
  matrix products: 47.7 us -> 56.6 us
    pallas_call x4, Pallas kernels: 107 us -> 77.5 us  [late(): pl.pallas_call(functools.partial(late_kernel, head=head, scale=head ** (-...]
    ppermute x46 -> x32, starting transfers between devices: 38.4 us -> 56 us  [send(): return lax.ppermute(z, 'sp', perm)]
    slice x0 -> x2, local copies, waits for them, and re-layouts: none -> 10.5 us  [local_step(): h, qd = (group[0][lo:lo + n], group[1][:, lo:lo + n])]
    pallas_call x4, Pallas kernels: 118 us -> 128 us  [attend(): pl.pallas_call(functools.partial(attn_kernel, head=head, scale=head ** (-...]
    dot_general x16, matrix products: 47.7 us -> 56.6 us  [tok_dot(): lax.dot_general(a, b, (((0, 1), (0, 1)), ((), ())), preferred_element_typ...]
    unnamed x138 -> x88, local copies, waits for them, and re-layouts: 18.9 us -> 10.5 us
    pallas_call x4 -> x2, Pallas kernels: 39 us -> 32.8 us  [front(): pl.pallas_call(front_kernel, grid_spec=pltpu.PrefetchScalarGridSpec(num_s...]
    dynamic_update_slice x19 -> x5, local copies, waits for them, and re-layouts: 17 us -> 12.9 us  [the longest x3 6.79 us: local_step(): lax.dynamic_update_slice(dwt, send(w, SWAP_CORE), (t * dim + (1 - core) *...]
  transfers between devices with their start and end apart: 46 -> 32, of which waited for: 8 -> 7; matrix products, arithmetic and copies ran while one was open for 12% -> 17% of each run, Pallas kernels for 47% -> 43%
where the time goes in v2:
time: 731 us; the launch traced here: 724 us
  Pallas kernels  313 us (43%)
  waiting for transfers between devices  221 us (30%)
  matrix products  56.6 us (8%)
  starting transfers between devices  56 us (8%)
  local copies, waits for them, and re-layouts  55 us (8%)
  other arithmetic  21.8 us (3%)
    ppermute x32, waiting for transfers between devices, send(): return lax.ppermute(z, 'sp', perm)  221 us
    pallas_call x4, Pallas kernels, attend(): pl.pallas_call(functools.partial(attn_kernel, head=head, scale=head ** (-...  128 us
    pallas_call x4, Pallas kernels, late(): pl.pallas_call(functools.partial(late_kernel, head=head, scale=head ** (-...  77.5 us
    dot_general x16, matrix products, tok_dot(): lax.dot_general(a, b, (((0, 1), (0, 1)), ((), ())), preferred_element_typ...  56.6 us
    ppermute x32, starting transfers between devices, send(): return lax.ppermute(z, 'sp', perm)  56 us
    pallas_call x4, Pallas kernels, back(): pl.pallas_call(back_kernel, grid_spec=pltpu.PrefetchScalarGridSpec(num_sc...  42.7 us
    pallas_call x2, Pallas kernels, front(): pl.pallas_call(front_kernel, grid_spec=pltpu.PrefetchScalarGridSpec(num_s...  32.8 us
    pallas_call x4, Pallas kernels, post(): pl.pallas_call(post_kernel, grid_spec=pltpu.PrefetchScalarGridSpec(num_sc...  17.5 us
  transfers between devices with their start and end apart: 32, of which 7 were waited for; matrix products, arithmetic and copies ran while one was open for 17% of the time, Pallas kernels for 43%

profile of v2, /device:TPU:0, one launch (start us, length us, event | category | flops | bytes accessed | tf_op | source)
XLA Modules:
  0.0 724.0 jit_solution(2846066078378076892)
XLA Ops:
  3.3 3.2 constant_dynamic-slice_fusion.6
  6.6 2.1 constant_dynamic-slice_fusion.5
  14.0 10.7 %front.3 = (bf16[2,512,768]{2,1,0:T(8,128)(2,1)}, bf16[2,2,512,768]{3,2,1,0:T(8,128)(2,1)}, bf16[2,512,768]{2,1,0:T(8,128)(2,1)}, bf16[2,512,768]{2,1,0:T(8,128)...) custom-call(s32[1]{0:T(128)} %bitcast.core_ref, bf16[16,256,768]{2,1,0:T(8,128)(2,1)} %x_ref.3, ...), custom_call_target="tpu_custom_call" | custom-call | flops 4831838208 | bytes 14155776 | tf_op jit(solution)/shard_map/front/pallas_call | solution.py:72
  24.7 5.0 collective-permute-start.5
  31.0 22.0 %front.2 = (bf16[6,512,768]{2,1,0:T(8,128)(2,1)}, bf16[2,6,512,768]{3,2,1,0:T(8,128)(2,1)}, bf16[6,512,768]{2,1,0:T(8,128)(2,1)}, bf16[6,512,768]{2,1,0:T(8,128)...) custom-call(s32[1]{0:T(128)} %bitcast.core_ref, bf16[16,256,768]{2,1,0:T(8,128)(2,1)} %x_ref.3, ...), custom_call_target="tpu_custom_call" | custom-call | flops 14495514624 | bytes 42467328 | tf_op jit(solution)/shard_map/front/pallas_call | solution.py:72
  53.0 3.8 fusion.17
  56.9 7.3 %collective-permute-start.9 = (bf16[2,512,768]{2,1,0:T(8,128)(2,1)S(1)}, bf16[2,512,768]{2,1,0:T(8,128)(2,1)}, u32[]{:S(2)}, u32[]{:S(2)}) collective-permute-start(bf16[2,512,768]{2,1,0:T(8,128)(2,1)S(1)} %get-tuple-element.174), channel_id=1, source_target_pairs={{0,2},{1,3},{4,6},{5,7}} | collective-permute-start | bytes 4718600 | tf_op jit(solution)/shard_map/ppermute | solution.py:383
  64.1 2.6 collective-permute-start.8
  67.9 3.4 other_kv.5
  71.3 31.8 %attend.4 = (bf16[2,512,768]{2,1,0:T(8,128)(2,1)}, bf16[2,512,768]{2,1,0:T(8,128)(2,1)}, f32[2,512,768]{2,1,0:T(8,128)}, f32[2,512,768]{2,1,0:T(8,128)}, bf16[2,...) custom-call(s32[1]{0:T(128)} %bitcast.1.role_ref, ...), custom_call_target="tpu_custom_call" | custom-call | flops 12884901888 | bytes 18874368 | tf_op jit(solution)/shard_map/attend/pallas_call | solution.py:198
  104.4 22.5 %collective-permute-start.2 = (bf16[2,512,768]{2,1,0:T(8,128)(2,1)}, bf16[2,512,768]{2,1,0:T(8,128)(2,1)}, u32[]{:S(2)}, u32[]{:S(2)}) collective-permute-start(bf16[2,512,768]{2,1,0:T(8,128)(2,1)} %get-tuple-element.176), channel_id=1, source_target_pairs={{0,2},{1,3},{4,6},{5,7}} | collective-permute-start | bytes 4718600 | tf_op jit(solution)/shard_map/ppermute | solution.py:383
  126.9 3.5 fusion.19
  130.4 2.8 fusion.18
  133.2 6.7 fusion.16
  141.5 3.5 other_kv.6
  144.9 32.1 %attend.5 = (bf16[2,512,768]{2,1,0:T(8,128)(2,1)}, bf16[2,512,768]{2,1,0:T(8,128)(2,1)}, f32[2,512,768]{2,1,0:T(8,128)}, f32[2,512,768]{2,1,0:T(8,128)}, bf16[2,...) custom-call(s32[1]{0:T(128)} %bitcast.1.role_ref, ...), custom_call_target="tpu_custom_call" | custom-call | flops 12884901888 | bytes 18874368 | tf_op jit(solution)/shard_map/attend/pallas_call | solution.py:198
  177.7 19.3 %late.4 = (bf16[2,512,768]{2,1,0:T(8,128)(2,1)}, bf16[2,512,768]{2,1,0:T(8,128)(2,1)}) custom-call(s32[1]{0:T(128)} %bitcast.1.role_ref, bf16[2,2,512,768]{3,2,1,0:T(8,128)(2,1)} %collective-permute-done.6.q_ref.g_ref, bf16[2,2,512,768]{3,2,1,0:T(8,128)(2,1)} %collective-permute-done.6.q_ref.g_ref, ...), custom_call_target="tpu_custom_call", output_to_operand_aliasing={{0}: (8, {}), {1}: (9, {})} | custom-call | flops 6442450944 | bytes 15728640 | tf_op jit(solution)/shard_map/late/pallas_call | solution.py:255
  197.0 4.4 convolution_bitcast_fusion.4.rest_1_
  201.4 2.8 convolution_bitcast_fusion.5.rest_0_
  204.8 10.8 %back.4 = (bf16[16,256,768]{2,1,0:T(8,128)(2,1)}, bf16[8,256,768]{2,1,0:T(8,128)(2,1)}, f32[8,768]{1,0:T(8,128)}) custom-call(s32[1]{0:T(128)} %bitcast.core_ref, bf16[2,512,768]{2,1,0:T(8,128)(2,1)} %get-tuple-element.96.dq_ref, bf16[2,512,768]{2,1,0:T(8,128)(2,1)} %get-tuple-element.105.dk_ref, bf16[2,512,768]{2,1,0:T(8,128)(2,1)} %get-tuple-element.106.dv_ref, ...), custom_call_target="tpu_custom_call" | custom-call | flops 3623878656 | bytes 9437184 | tf_op jit(solution)/shard_map/back/pallas_call | solution.py:343
  215.6 3.6 other_kv.7
  219.3 32.1 %attend.7 = (bf16[2,512,768]{2,1,0:T(8,128)(2,1)}, bf16[2,512,768]{2,1,0:T(8,128)(2,1)}, f32[2,512,768]{2,1,0:T(8,128)}, f32[2,512,768]{2,1,0:T(8,128)}, bf16[2,...) custom-call(s32[1]{0:T(128)} %bitcast.1.role_ref, ...), custom_call_target="tpu_custom_call" | custom-call | flops 12884901888 | bytes 18874368 | tf_op jit(solution)/shard_map/attend/pallas_call | solution.py:198
  251.4 4.4 fusion.3
  255.8 2.9 fusion.1
  258.6 3.4 other_kv.4
  262.1 32.2 %attend.6 = (bf16[2,512,768]{2,1,0:T(8,128)(2,1)}, bf16[2,512,768]{2,1,0:T(8,128)(2,1)}, f32[2,512,768]{2,1,0:T(8,128)}, f32[2,512,768]{2,1,0:T(8,128)}, bf16[2,...) custom-call(s32[1]{0:T(128)} %bitcast.1.role_ref, ...), custom_call_target="tpu_custom_call" | custom-call | flops 12884901888 | bytes 18874368 | tf_op jit(solution)/shard_map/attend/pallas_call | solution.py:198
  294.3 5.2 bitcast_add_fusion.5
  302.1 3.0 fusion.5
  305.1 3.0 fusion.9
  308.1 3.1 bitcast_add_fusion.2
  316.9 4.4 post.4
  321.3 4.4 post.5
  325.7 4.4 post.6
  330.1 4.4 post.7
  335.9 3.0 dynamic-slice_add_fusion.3.rest_1_
  340.3 2.4 dynamic-slice_add_fusion.2.rest_2_
  342.8 161.4 %collective-permute-done.16.st_ref = f32[2,6,4,512]{3,2,1,0:T(4,128)S(1)} collective-permute-done((f32[2,6,4,512]{3,2,1,0:T(4,128)S(1)}, f32[2,6,4,512]{3,2,1,0:T(4,128)S(1)}, u32[]{:S(2)}, u32[]{:S(2)}) %collective-permute-start.16) | collective-permute-done | bytes 98336 | tf_op jit(solution)/shard_map/ppermute | solution.py:383
  505.6 2.7 collective-permute-start.24
  508.2 19.6 %late.5 = (bf16[2,512,768]{2,1,0:T(8,128)(2,1)}, bf16[2,512,768]{2,1,0:T(8,128)(2,1)}) custom-call(s32[1]{0:T(128)} %bitcast.1.role_ref, bf16[2,2,512,768]{3,2,1,0:T(8,128)(2,1)} %collective-permute-done.15.q_ref.g_ref, bf16[2,2,512,768]{3,2,1,0:T(8,128)(2,1)} %collective-permute-done.15.q_ref.g_ref, ...), custom_call_target="tpu_custom_call", output_to_operand_aliasing={{0}: (8, {}), {1}: (9, {})} | custom-call | flops 6442450944 | bytes 15728640 | tf_op jit(solution)/shard_map/late/pallas_call | solution.py:255
  527.9 4.4 convolution_bitcast_fusion.2.rest_3_
  532.3 2.9 convolution_bitcast_fusion.3.rest_2_
  535.2 10.5 %back.5 = (bf16[16,256,768]{2,1,0:T(8,128)(2,1)}, bf16[8,256,768]{2,1,0:T(8,128)(2,1)}, f32[8,768]{1,0:T(8,128)}) custom-call(s32[1]{0:T(128)} %bitcast.core_ref, bf16[2,512,768]{2,1,0:T(8,128)(2,1)} %get-tuple-element.136.dq_ref, bf16[2,512,768]{2,1,0:T(8,128)(2,1)} %get-tuple-element.142.dk_ref, ...), custom_call_target="tpu_custom_call", output_to_operand_aliasing={{0}: (9, {}), {1}: (10, {})} | custom-call | flops 3623878656 | bytes 9437184 | tf_op jit(solution)/shard_map/back/pallas_call | solution.py:343
  546.3 19.3 %late.6 = (bf16[2,512,768]{2,1,0:T(8,128)(2,1)}, bf16[2,512,768]{2,1,0:T(8,128)(2,1)}) custom-call(s32[1]{0:T(128)} %bitcast.1.role_ref, bf16[2,2,512,768]{3,2,1,0:T(8,128)(2,1)} %collective-permute-done.13.q_ref.g_ref, bf16[2,2,512,768]{3,2,1,0:T(8,128)(2,1)} %collective-permute-done.13.q_ref.g_ref, ...), custom_call_target="tpu_custom_call", output_to_operand_aliasing={{0}: (8, {}), {1}: (9, {})} | custom-call | flops 6442450944 | bytes 15728640 | tf_op jit(solution)/shard_map/late/pallas_call | solution.py:255
  565.6 4.3 convolution_bitcast_fusion.rest_3_
  570.0 2.9 convolution_bitcast_fusion.1.rest_2_
  572.9 10.8 %back.6 = (bf16[16,256,768]{2,1,0:T(8,128)(2,1)}, bf16[8,256,768]{2,1,0:T(8,128)(2,1)}, f32[8,768]{1,0:T(8,128)}) custom-call(s32[1]{0:T(128)} %bitcast.core_ref, bf16[2,512,768]{2,1,0:T(8,128)(2,1)} %get-tuple-element.131.dq_ref, bf16[2,512,768]{2,1,0:T(8,128)(2,1)} %get-tuple-element.148.dk_ref, ...), custom_call_target="tpu_custom_call", output_to_operand_aliasing={{0}: (9, {}), {1}: (10, {})} | custom-call | flops 3623878656 | bytes 9437184 | tf_op jit(solution)/shard_map/back/pallas_call | solution.py:343
  585.4 19.3 %late.7 = (bf16[2,512,768]{2,1,0:T(8,128)(2,1)}, bf16[2,512,768]{2,1,0:T(8,128)(2,1)}) custom-call(s32[1]{0:T(128)} %bitcast.1.role_ref, bf16[2,2,512,768]{3,2,1,0:T(8,128)(2,1)} %copy-done.2, bf16[2,2,512,768]{3,2,1,0:T(8,128)(2,1)} %copy-done.2, f32[2,6,4,512]{3,2,1,0:T(4,128)} %copy-done.25, ...), custom_call_target="tpu_custom_call", output_to_operand_aliasing={{0}: (8, {}), {1}: (9, {})} | custom-call | flops 6442450944 | bytes 15728640 | tf_op jit(solution)/shard_map/late/pallas_call | solution.py:255
  604.7 5.3 bitcast_add_fusion.1
  618.5 3.3 dynamic-slice_add_fusion.1.rest_2_
  622.3 2.5 dynamic-slice_add_fusion.rest_3_
  624.7 10.5 %back.7 = (bf16[16,256,768]{2,1,0:T(8,128)(2,1)}, bf16[8,256,768]{2,1,0:T(8,128)(2,1)}, f32[8,768]{1,0:T(8,128)}) custom-call(s32[1]{0:T(128)} %bitcast.core_ref, bf16[2,512,768]{2,1,0:T(8,128)(2,1)} %get-tuple-element.125.dq_ref, bf16[2,512,768]{2,1,0:T(8,128)(2,1)} %get-tuple-element.153.dk_ref, ...), custom_call_target="tpu_custom_call", output_to_operand_aliasing={{0}: (9, {}), {1}: (10, {})} | custom-call | flops 3623878656 | bytes 9437184 | tf_op jit(solution)/shard_map/back/pallas_call | solution.py:343
  637.4 2.4 constant_dynamic-update-slice_fusion.6
  639.8 11.2 %collective-permute-done.26 = f32[384,768]{1,0:T(8,128)} collective-permute-done((f32[384,768]{1,0:T(8,128)}, f32[384,768]{1,0:T(8,128)}, u32[]{:S(2)}, u32[]{:S(2)}) %collective-permute-start.26) | collective-permute-done | bytes 1179680 | tf_op jit(solution)/shard_map/ppermute | solution.py:383
  651.0 3.2 constant_dynamic-update-slice_fusion.5
  654.2 22.1 %collective-permute-done.30 = f32[384,768]{1,0:T(8,128)} collective-permute-done((f32[384,768]{1,0:T(8,128)S(1)}, f32[384,768]{1,0:T(8,128)}, u32[]{:S(2)}, u32[]{:S(2)}) %collective-permute-start.30) | collective-permute-done | bytes 1179680 | tf_op jit(solution)/shard_map/ppermute | solution.py:383
  676.5 2.5 constant_dynamic-update-slice_fusion.1
  678.9 3.2 constant_dynamic-update-slice_fusion.4
  682.2 18.8 %collective-permute-done.28 = f32[384,768]{1,0:T(8,128)} collective-permute-done((f32[384,768]{1,0:T(8,128)S(1)}, f32[384,768]{1,0:T(8,128)}, u32[]{:S(2)}, u32[]{:S(2)}) %collective-permute-start.28) | collective-permute-done | bytes 1179680 | tf_op jit(solution)/shard_map/ppermute | solution.py:383
  701.0 3.0 constant_dynamic-update-slice_fusion.3
  704.5 2.6 collective-permute-done.22
  707.4 3.5 collective-permute-done.23
  712.2 3.9 constant_dynamic-update-slice_fusion.9
  716.1 2.4 constant_dynamic-update-slice_fusion
  718.5 2.2 constant_dynamic-update-slice_fusion.8
  (165 shorter events, 45.5 us)
Async XLA Ops:
  2.5 28.5 %collective-permute-start = (bf16[6,256,768]{2,1,0:T(8,128)(2,1)S(1)}, bf16[6,256,768]{2,1,0:T(8,128)(2,1)}, u32[]{:S(2)}, u32[]{:S(2)}) collective-permute-start(bf16[6,256,768]{2,1,0:T(8,128)(2,1)S(1)} %constant_dynamic-slice_fusion.7), channel_id=1, source_target_pairs={{0,1},{1,0},{2,3},{3,2},{4,5},{5,4},{6,7},{7,6}} | collective-permute-start | bytes 7077896 | tf_op jit(solution)/shard_map/ppermute | solution.py:383
  6.5 24.5 %collective-permute-start.1 = (bf16[6,256,768]{2,1,0:T(8,128)(2,1)}, bf16[6,256,768]{2,1,0:T(8,128)(2,1)}, u32[]{:S(2)}, u32[]{:S(2)}) collective-permute-start(bf16[6,256,768]{2,1,0:T(8,128)(2,1)} %constant_dynamic-slice_fusion.6), channel_id=1, source_target_pairs={{0,1},{1,0},{2,3},{3,2},{4,5},{5,4},{6,7},{7,6}} | collective-permute-start | bytes 7077896 | tf_op jit(solution)/shard_map/ppermute | solution.py:383
  6.6 4.7 copy-start.28
  6.6 5.4 copy-start.30
  6.6 5.9 copy-start.31
  8.7 4.4 collective-permute-start.3
  11.2 2.6 collective-permute-start.4
  24.7 42.0 %collective-permute-start.5 = (bf16[2,512,768]{2,1,0:T(8,128)(2,1)}, bf16[2,512,768]{2,1,0:T(8,128)(2,1)S(1)}, u32[]{:S(2)}, u32[]{:S(2)}) collective-permute-start(bf16[2,512,768]{2,1,0:T(8,128)(2,1)} %get-tuple-element.93), channel_id=1, source_target_pairs={{0,2},{1,3},{4,6},{5,7}} | collective-permute-start | bytes 4718600 | tf_op jit(solution)/shard_map/ppermute | solution.py:383
  29.7 147.3 %collective-permute-start.6 = (bf16[2,2,512,768]{3,2,1,0:T(8,128)(2,1)}, bf16[2,2,512,768]{3,2,1,0:T(8,128)(2,1)}, u32[]{:S(2)}, u32[]{:S(2)}) collective-permute-start(bf16[2,2,512,768]{3,2,1,0:T(8,128)(2,1)} %get-tuple-element.90.q_ref.g_ref), channel_id=1, source_target_pairs={{2,0},{3,1},{6,4},{7,5}} | collective-permute-start | bytes 9437192 | tf_op jit(solution)/shard_map/ppermute | solution.py:383
  56.9 158.8 %collective-permute-start.9 = (bf16[2,512,768]{2,1,0:T(8,128)(2,1)S(1)}, bf16[2,512,768]{2,1,0:T(8,128)(2,1)}, u32[]{:S(2)}, u32[]{:S(2)}) collective-permute-start(bf16[2,512,768]{2,1,0:T(8,128)(2,1)S(1)} %get-tuple-element.174), channel_id=1, source_target_pairs={{0,2},{1,3},{4,6},{5,7}} | collective-permute-start | bytes 4718600 | tf_op jit(solution)/shard_map/ppermute | solution.py:383
  64.1 75.8 %collective-permute-start.8 = (bf16[2,512,768]{2,1,0:T(8,128)(2,1)S(1)}, bf16[2,512,768]{2,1,0:T(8,128)(2,1)}, u32[]{:S(2)}, u32[]{:S(2)}) collective-permute-start(bf16[2,512,768]{2,1,0:T(8,128)(2,1)S(1)} %get-tuple-element.175), channel_id=1, source_target_pairs={{0,2},{1,3},{4,6},{5,7}} | collective-permute-start | bytes 4718600 | tf_op jit(solution)/shard_map/ppermute | solution.py:383
  103.1 73.9 %collective-permute-start.7 = (f32[2,6,4,512]{3,2,1,0:T(4,128)}, f32[2,6,4,512]{3,2,1,0:T(4,128)S(1)}, u32[]{:S(2)}, u32[]{:S(2)}) collective-permute-start(f32[2,6,4,512]{3,2,1,0:T(4,128)} %get-tuple-element.97), channel_id=1, source_target_pairs={{2,0},{3,1},{6,4},{7,5}} | collective-permute-start | bytes 294920 | tf_op jit(solution)/shard_map/ppermute | solution.py:383
  104.4 154.2 %collective-permute-start.2 = (bf16[2,512,768]{2,1,0:T(8,128)(2,1)}, bf16[2,512,768]{2,1,0:T(8,128)(2,1)}, u32[]{:S(2)}, u32[]{:S(2)}) collective-permute-start(bf16[2,512,768]{2,1,0:T(8,128)(2,1)} %get-tuple-element.176), channel_id=1, source_target_pairs={{0,2},{1,3},{4,6},{5,7}} | collective-permute-start | bytes 4718600 | tf_op jit(solution)/shard_map/ppermute | solution.py:383
  126.9 3.5 copy-start.21
  126.9 3.5 copy-start.37
  139.9 365.6 %collective-permute-start.15 = (bf16[2,2,512,768]{3,2,1,0:T(8,128)(2,1)}, bf16[2,2,512,768]{3,2,1,0:T(8,128)(2,1)}, u32[]{:S(2)}, u32[]{:S(2)}) collective-permute-start(bf16[2,2,512,768]{3,2,1,0:T(8,128)(2,1)} %get-tuple-element.171), channel_id=1, source_target_pairs={{2,0},{3,1},{6,4},{7,5}} | collective-permute-start | bytes 9437192 | tf_op jit(solution)/shard_map/ppermute | solution.py:383
  177.6 19.3 %copy-start.33 = (bf16[2,512,768]{2,1,0:T(8,128)(2,1)S(1)}, bf16[2,512,768]{2,1,0:T(8,128)(2,1)}, u32[]{:S(2)}) copy-start(bf16[2,512,768]{2,1,0:T(8,128)(2,1)} %get-tuple-element.93) | copy-start | bytes 4718596
  197.0 4.4 copy-start.22
  215.6 35.7 %slice-start.2 = ((s8[4718592]{0:T(1024)(128)(4,1)}), s8[4194304]{0:T(1024)(128)(4,1)S(1)}, s32[]{:S(2)}) async-start(s8[4718592]{0:T(1024)(128)(4,1)} %bitcast.82), calls=%async_computation.2 | async-start | bytes 8388608
  219.3 32.1 %slice-start.3 = ((s8[4718592]{0:T(1024)(128)(4,1)}), s8[524288]{0:T(1024)(128)(4,1)S(1)}, s32[]{:S(2)}) async-start(s8[4718592]{0:T(1024)(128)(4,1)} %bitcast.82), calls=%async_computation.3 | async-start | bytes 1048576
  251.4 4.4 copy-start.20
  299.5 5.6 copy-start.5
  300.6 33.8 %collective-permute-start.17 = (f32[384,768]{1,0:T(8,128)}, f32[384,768]{1,0:T(8,128)}, u32[]{:S(2)}, u32[]{:S(2)}) collective-permute-start(f32[384,768]{1,0:T(8,128)} %constant_dynamic-slice_fusion.3), channel_id=1, source_target_pairs={{0,1},{1,0},{2,3},{3,2},{4,5},{5,4},{6,7},{7,6}} | collective-permute-start | bytes 3538952 | tf_op jit(solution)/shard_map/ppermute | solution.py:383
  305.1 3.0 copy-start.14
  313.7 25.2 %collective-permute-start.18 = (f32[384,768]{1,0:T(8,128)}, f32[384,768]{1,0:T(8,128)}, u32[]{:S(2)}, u32[]{:S(2)}) collective-permute-start(f32[384,768]{1,0:T(8,128)} %constant_dynamic-slice_fusion.2), channel_id=1, source_target_pairs={{0,1},{1,0},{2,3},{3,2},{4,5},{5,4},{6,7},{7,6}} | collective-permute-start | bytes 3538952 | tf_op jit(solution)/shard_map/ppermute | solution.py:383
  313.7 232.0 %collective-permute-start.13 = (bf16[2,2,512,768]{3,2,1,0:T(8,128)(2,1)}, bf16[2,2,512,768]{3,2,1,0:T(8,128)(2,1)}, u32[]{:S(2)}, u32[]{:S(2)}) collective-permute-start(bf16[2,2,512,768]{3,2,1,0:T(8,128)(2,1)} %get-tuple-element.172), channel_id=1, source_target_pairs={{2,0},{3,1},{6,4},{7,5}} | collective-permute-start | bytes 9437192 | tf_op jit(solution)/shard_map/ppermute | solution.py:383
  315.6 268.1 %collective-permute-start.11 = (bf16[2,2,512,768]{3,2,1,0:T(8,128)(2,1)}, bf16[2,2,512,768]{3,2,1,0:T(8,128)(2,1)S(1)}, u32[]{:S(2)}, u32[]{:S(2)}) collective-permute-start(bf16[2,2,512,768]{3,2,1,0:T(8,128)(2,1)} %get-tuple-element.173), channel_id=1, source_target_pairs={{2,0},{3,1},{6,4},{7,5}} | collective-permute-start | bytes 9437192 | tf_op jit(solution)/shard_map/ppermute | solution.py:383
  334.5 4.4 copy-start.35
  334.5 5.9 copy-start.7
  334.5 211.2 %collective-permute-start.14 = (f32[2,6,4,512]{3,2,1,0:T(4,128)}, f32[2,6,4,512]{3,2,1,0:T(4,128)S(1)}, u32[]{:S(2)}, u32[]{:S(2)}) collective-permute-start(f32[2,6,4,512]{3,2,1,0:T(4,128)} %get-tuple-element.104.rest_0_), channel_id=1, source_target_pairs={{2,0},{3,1},{6,4},{7,5}} | collective-permute-start | bytes 294920 | tf_op jit(solution)/shard_map/ppermute | solution.py:383
  335.9 192.0 %slice-start.4 = ((s8[4718592]{0:T(1024)(128)(4,1)}), s8[4194304]{0:T(1024)(128)(4,1)S(1)}, s32[]{:S(2)}) async-start(s8[4718592]{0:T(1024)(128)(4,1)} %bitcast.84), calls=%async_computation.4 | async-start | bytes 8388608
  338.9 165.3 %copy-start.24 = (f32[2,6,4,512]{3,2,1,0:T(4,128)S(1)}, f32[2,6,4,512]{3,2,1,0:T(4,128)}, u32[]{:S(2)}) copy-start(f32[2,6,4,512]{3,2,1,0:T(4,128)} %get-tuple-element.126.rest_0_) | copy-start | bytes 294916
  338.9 165.3 %collective-permute-start.16 = (f32[2,6,4,512]{3,2,1,0:T(4,128)S(1)}, f32[2,6,4,512]{3,2,1,0:T(4,128)S(1)}, u32[]{:S(2)}, u32[]{:S(2)}) collective-permute-start(f32[2,6,4,512]{3,2,1,0:T(4,128)S(1)} %copy-done.35), channel_id=1, source_target_pairs={{2,0},{3,1},{6,4},{7,5}} | collective-permute-start | bytes 294920 | tf_op jit(solution)/shard_map/ppermute | solution.py:383
  504.2 4.0 copy-start.27
  504.3 79.5 %collective-permute-start.12 = (f32[2,6,4,512]{3,2,1,0:T(4,128)S(1)}, f32[2,6,4,512]{3,2,1,0:T(4,128)S(1)}, u32[]{:S(2)}, u32[]{:S(2)}) collective-permute-start(f32[2,6,4,512]{3,2,1,0:T(4,128)S(1)} %copy-done.24), channel_id=1, source_target_pairs={{2,0},{3,1},{6,4},{7,5}} | collective-permute-start | bytes 294920 | tf_op jit(solution)/shard_map/ppermute | solution.py:383
  505.6 110.0 %collective-permute-start.24 = (f32[384,768]{1,0:T(8,128)}, f32[384,768]{1,0:T(8,128)}, u32[]{:S(2)}, u32[]{:S(2)}) collective-permute-start(f32[384,768]{1,0:T(8,128)} %dynamic-slice_add_fusion.2.rest_2_), channel_id=1, source_target_pairs={{0,2},{1,3},{2,0},{3,1},{4,6},{5,7},{6,4},{7,5}} | collective-permute-start | bytes 3538952 | tf_op jit(solution)/shard_map/ppermute | solution.py:383
  508.2 19.7 %slice-start.5 = ((s8[4718592]{0:T(1024)(128)(4,1)}), s8[524288]{0:T(1024)(128)(4,1)S(1)}, s32[]{:S(2)}) async-start(s8[4718592]{0:T(1024)(128)(4,1)} %bitcast.84), calls=%async_computation.5 | async-start | bytes 1048576
  527.9 4.4 copy-start.16
  565.6 4.4 copy-start.15
  604.7 6.5 copy-start.10
  604.7 6.5 copy-start.11
  604.7 6.5 copy-start.12
  610.1 4.3 copy-start.8
  611.2 7.3 %collective-permute-start.19 = (f32[384,768]{1,0:T(8,128)}, f32[384,768]{1,0:T(8,128)}, u32[]{:S(2)}, u32[]{:S(2)}) collective-permute-start(f32[384,768]{1,0:T(8,128)} %constant_dynamic-slice_fusion.1), channel_id=1, source_target_pairs={{0,1},{1,0},{2,3},{3,2},{4,5},{5,4},{6,7},{7,6}} | collective-permute-start | bytes 3538952 | tf_op jit(solution)/shard_map/ppermute | solution.py:383
  615.6 6.7 collective-permute-start.20
  618.0 6.7 copy-start.13
  618.0 19.4 %collective-permute-start.25 = (f32[384,768]{1,0:T(8,128)S(1)}, f32[384,768]{1,0:T(8,128)}, u32[]{:S(2)}, u32[]{:S(2)}) collective-permute-start(f32[384,768]{1,0:T(8,128)S(1)} %get-tuple-element.170), channel_id=1, source_target_pairs={{0,1},{1,0},{2,3},{3,2},{4,5},{5,4},{6,7},{7,6}} | collective-permute-start | bytes 3538952 | tf_op jit(solution)/shard_map/ppermute | solution.py:383
  621.9 29.2 %collective-permute-start.26 = (f32[384,768]{1,0:T(8,128)}, f32[384,768]{1,0:T(8,128)}, u32[]{:S(2)}, u32[]{:S(2)}) collective-permute-start(f32[384,768]{1,0:T(8,128)} %dynamic-slice_add_fusion.1.rest_2_), channel_id=1, source_target_pairs={{0,2},{1,3},{2,0},{3,1},{4,6},{5,7},{6,4},{7,5}} | collective-permute-start | bytes 3538952 | tf_op jit(solution)/shard_map/ppermute | solution.py:383
  621.9 90.4 %collective-permute-start.10 = (bf16[8,256,768]{2,1,0:T(8,128)(2,1)}, bf16[8,256,768]{2,1,0:T(8,128)(2,1)}, u32[]{:S(2)}, u32[]{:S(2)}) collective-permute-start(bf16[8,256,768]{2,1,0:T(8,128)(2,1)} %get-tuple-element.124.rest_1_), channel_id=1, source_target_pairs={{0,1},{1,0},{2,3},{3,2},{4,5},{5,4},{6,7},{7,6}} | collective-permute-start | bytes 9437192 | tf_op jit(solution)/shard_map/ppermute | solution.py:383
  624.7 10.7 %copy-start.3 = (f32[384,768]{1,0:T(8,128)S(1)}, f32[384,768]{1,0:T(8,128)}, u32[]{:S(2)}) copy-start(f32[384,768]{1,0:T(8,128)} %dynamic-slice_add_fusion.3.rest_1_) | copy-start | bytes 3538948
  635.3 83.2 %collective-permute-start.21 = (bf16[8,256,768]{2,1,0:T(8,128)(2,1)}, bf16[8,256,768]{2,1,0:T(8,128)(2,1)}, u32[]{:S(2)}, u32[]{:S(2)}) collective-permute-start(bf16[8,256,768]{2,1,0:T(8,128)(2,1)} %get-tuple-element.158), channel_id=1, source_target_pairs={{0,1},{1,0},{2,3},{3,2},{4,5},{5,4},{6,7},{7,6}} | collective-permute-start | bytes 9437192 | tf_op jit(solution)/shard_map/ppermute | solution.py:383
  635.4 40.9 %collective-permute-start.30 = (f32[384,768]{1,0:T(8,128)S(1)}, f32[384,768]{1,0:T(8,128)}, u32[]{:S(2)}, u32[]{:S(2)}) collective-permute-start(f32[384,768]{1,0:T(8,128)S(1)} %copy-done.3), channel_id=1, source_target_pairs={{0,2},{1,3},{2,0},{3,1},{4,6},{5,7},{6,4},{7,5}} | collective-permute-start | bytes 3538952 | tf_op jit(solution)/shard_map/ppermute | solution.py:383
  639.8 14.4 %copy-start.4 = (f32[384,768]{1,0:T(8,128)S(1)}, f32[384,768]{1,0:T(8,128)}, u32[]{:S(2)}) copy-start(f32[384,768]{1,0:T(8,128)} %dynamic-slice_add_fusion.rest_3_) | copy-start | bytes 3538948
  654.2 24.7 %collective-permute-start.27 = (f32[384,768]{1,0:T(8,128)}, f32[384,768]{1,0:T(8,128)}, u32[]{:S(2)}, u32[]{:S(2)}) collective-permute-start(f32[384,768]{1,0:T(8,128)} %get-tuple-element.168), channel_id=1, source_target_pairs={{0,1},{1,0},{2,3},{3,2},{4,5},{5,4},{6,7},{7,6}} | collective-permute-start | bytes 3538952 | tf_op jit(solution)/shard_map/ppermute | solution.py:383
  654.2 46.8 %collective-permute-start.28 = (f32[384,768]{1,0:T(8,128)S(1)}, f32[384,768]{1,0:T(8,128)}, u32[]{:S(2)}, u32[]{:S(2)}) collective-permute-start(f32[384,768]{1,0:T(8,128)S(1)} %copy-done.4), channel_id=1, source_target_pairs={{0,2},{1,3},{2,0},{3,1},{4,6},{5,7},{6,4},{7,5}} | collective-permute-start | bytes 3538952 | tf_op jit(solution)/shard_map/ppermute | solution.py:383
  678.9 25.0 %copy-start.17 = (f32[768,768]{1,0:T(8,128)}, f32[768,768]{1,0:T(8,128)S(1)}, u32[]{:S(2)}) copy-start(f32[768,768]{1,0:T(8,128)S(1)} %get-tuple-element.163) | copy-start | bytes 7077892
  678.9 37.2 %collective-permute-start.31 = (f32[384,768]{1,0:T(8,128)}, f32[384,768]{1,0:T(8,128)}, u32[]{:S(2)}, u32[]{:S(2)}) collective-permute-start(f32[384,768]{1,0:T(8,128)} %get-tuple-element.164), channel_id=1, source_target_pairs={{0,1},{1,0},{2,3},{3,2},{4,5},{5,4},{6,7},{7,6}} | collective-permute-start | bytes 3538952 | tf_op jit(solution)/shard_map/ppermute | solution.py:383
  682.2 21.8 %copy-start.29 = (f32[8,768]{1,0:T(8,128)S(1)}, f32[8,768]{1,0:T(8,128)}, u32[]{:S(2)}) copy-start(f32[8,768]{1,0:T(8,128)} %get-tuple-element.159) | copy-start | bytes 73732
  701.0 17.5 %slice-start = ((s8[6291456]{0:T(1024)(128)(4,1)}), s8[2097152]{0:T(1024)(128)(4,1)S(1)}, s32[]{:S(2)}) async-start(s8[6291456]{0:T(1024)(128)(4,1)} %bitcast.80), calls=%async_computation | async-start | bytes 4194304
  704.0 16.8 %collective-permute-start.29 = (f32[384,768]{1,0:T(8,128)}, f32[384,768]{1,0:T(8,128)S(1)}, u32[]{:S(2)}, u32[]{:S(2)}) collective-permute-start(f32[384,768]{1,0:T(8,128)} %get-tuple-element.166), channel_id=1, source_target_pairs={{0,1},{1,0},{2,3},{3,2},{4,5},{5,4},{6,7},{7,6}} | collective-permute-start | bytes 3538952 | tf_op jit(solution)/shard_map/ppermute | solution.py:383
  704.0 3.1 collective-permute-start.22
  707.1 3.8 collective-permute-start.23
  712.2 6.3 slice-start.1
  720.8 3.1 copy-start
  (12 other events, 20.2 us)

commit v3 on v2

--- a/solution.py
+++ b/solution.py
@@ -40,7 +40,8 @@
 
 
 def front_kernel(core_ref, x_ref, xr_ref, g_ref, gr_ref, lng_ref, lnb_ref, w_ref, b_ref, wo_ref,
-                 h_ref, qd_ref, k_ref, v_ref, xb_ref, gb_ref):
+                 *rest):
+    hs_ref, qd_ref, k_ref, v_ref, h_ref, xb_ref, gb_ref = rest[-7:]
     dim = x_ref.shape[2]
     run = x_ref.shape[1]
     mine = pl.ds(pl.multiple_of(core_ref[0] * run, run), run)
@@ -52,6 +53,7 @@
     qd_ref[0, 0] = dot_nt(gb_ref[0], wo_ref[...]).astype(BF16)
     x_hat, _ = normed(xb_ref[0].astype(F32))
     h_ref[0] = (x_hat * lng_ref[...] + lnb_ref[...]).astype(BF16)
+    hs_ref[0] = h_ref[0]
     for t in range(3):
         cols = slice(t * dim, (t + 1) * dim)
         val = (dot_nt(h_ref[0], w_ref[cols, :]) + b_ref[:, cols]).astype(BF16)
@@ -61,56 +63,59 @@
             (k_ref if t == 1 else v_ref)[0] = val
 
 
-def front(core, x, x_r, g, g_r, ln_g, ln_b, w_t, b_qkv, w_o, lo):
+def front(core, x, x_r, g, g_r, ln_g, ln_b, w_t, b_qkv, w_o, lo, prev):
     batch, run, dim = x.shape
     n, seq = x_r.shape[0], 2 * run
     whole = lambda shape: pl.BlockSpec(shape, lambda b, c: (0,) * len(shape))
     own = pl.BlockSpec((1, run, dim), lambda b, c: (c[0] * (batch // 2) + lo + b, 0, 0))
     got = pl.BlockSpec((1, run, dim), lambda b, c: (b, 0, 0))
     tok = pl.BlockSpec((1, seq, dim), lambda b, c: (b, 0, 0))
+    row = pl.BlockSpec((1, seq, dim), lambda b, c: (lo + b, 0, 0))
     out = jax.ShapeDtypeStruct((n, seq, dim), BF16)
+    all_rows = jax.ShapeDtypeStruct((batch // 2, seq, dim), BF16)
     return pl.pallas_call(
         front_kernel,
         grid_spec=pltpu.PrefetchScalarGridSpec(
             num_scalar_prefetch=1,
             grid=(n,),
-            in_specs=[own, got, own, got, whole((1, dim)), whole((1, dim)), whole((3 * dim, dim)), whole((1, 3 * dim)), whole((dim, dim))],
-            out_specs=[tok, pl.BlockSpec((2, 1, seq, dim), lambda b, c: (0, b, 0, 0)), tok, tok, tok, tok],
-        ),
-        out_shape=[out, jax.ShapeDtypeStruct((2, n, seq, dim), BF16), out, out, out, out],
+            in_specs=[own, got, own, got, whole((1, dim)), whole((1, dim)), whole((3 * dim, dim)), whole((1, 3 * dim)), whole((dim, dim))] + [UNREAD] * len(prev),
+            out_specs=[tok, pl.BlockSpec((2, 1, seq, dim), lambda b, c: (0, b, 0, 0)), tok, tok, row, row, row],
+        ),
+        out_shape=[out, jax.ShapeDtypeStruct((2, n, seq, dim), BF16), out, out] + [all_rows] * 3,
+        input_output_aliases={10 + i: 4 + i for i in range(len(prev))},
         compiler_params=params(1),
         cost_estimate=pl.CostEstimate(flops=8 * n * seq * dim * dim, bytes_accessed=18 * n * seq * dim, transcendentals=0),
         name="front",
-    )(core, x, x_r, g, g_r, ln_g, ln_b, w_t, b_qkv, w_o)
-
-
-def kv_kernel(role_ref, h_ref, w_ref, b_ref, k_ref, v_ref):
+    )(core, x, x_r, g, g_r, ln_g, ln_b, w_t, b_qkv, w_o, *prev)
+
+
+def kv_kernel(role_ref, h_ref, wk_ref, wv_ref, b_ref, k_ref, v_ref):
     dim = h_ref.shape[2]
 
     @pl.when(role_ref[0] == 1)
     def _():
-        for t, out in enumerate((k_ref, v_ref)):
-            cols = slice((t + 1) * dim, (t + 2) * dim)
-            out[0] = (dot_nt(h_ref[0], w_ref[cols, :]) + b_ref[:, cols]).astype(BF16)
+        for t, w_ref, out in ((1, wk_ref, k_ref), (2, wv_ref, v_ref)):
+            out[0] = (dot_nt(h_ref[0], w_ref[...]) + b_ref[:, t * dim:(t + 1) * dim]).astype(BF16)
 
 
 def other_kv(role, h_o, w_t, b_qkv):
     n, seq, dim = h_o.shape
     tok = pl.BlockSpec((1, seq, dim), lambda b, r: (b * r[0], 0, 0))
+    third = lambda t: pl.BlockSpec((dim, dim), lambda b, r: (t, 0))
     out = jax.ShapeDtypeStruct((n, seq, dim), BF16)
     return pl.pallas_call(
         kv_kernel,
         grid_spec=pltpu.PrefetchScalarGridSpec(
             num_scalar_prefetch=1,
             grid=(n,),
-            in_specs=[tok, pl.BlockSpec((3 * dim, dim), lambda b, r: (0, 0)), pl.BlockSpec((1, 3 * dim), lambda b, r: (0, 0))],
+            in_specs=[tok, third(1), third(2), pl.BlockSpec((1, 3 * dim), lambda b, r: (0, 0))],
             out_specs=[tok] * 2,
         ),
         out_shape=[out] * 2,
         compiler_params=params(1),
         cost_estimate=pl.CostEstimate(flops=4 * n * seq * dim * dim, bytes_accessed=6 * n * seq * dim, transcendentals=0),
         name="other_kv",
-    )(role, h_o, w_t, b_qkv)
+    )(role, h_o, w_t, w_t, b_qkv)
 
 
 def head_only(z, h, head):
@@ -119,7 +124,7 @@
 
 
 def attn_kernel(role_ref, q_ref, g_ref, k_ref, v_ref, ko_ref, vo_ref, *rest, head, scale):
-    a_ref, dq_ref, dk_ref, dv_ref, dkb_ref, dvb_ref, st_ref = rest[-7:]
+    a_ref, dq_ref, dkb_ref, dvb_ref, dk_ref, dv_ref, st_ref = rest[-7:]
     seq, width = k_ref.shape[1:]
     blk = seq // 2
     causal = lax.broadcasted_iota(jnp.int32, (blk, blk), 0) <= lax.broadcasted_iota(jnp.int32, (blk, blk), 1)
@@ -150,11 +155,11 @@
                 dp = products(v_ref, vo_ref, gm)
                 l = functools.reduce(jnp.add, [jnp.sum(e_i, axis=0, keepdims=True) for e_i in e])
                 c = functools.reduce(jnp.add, [jnp.sum(e_i * d_i, axis=0, keepdims=True) for e_i, d_i in zip(e, dp)])
-                inv_l = 1.0 / l
-                c = c * inv_l
-                st_ref[0, 0, 2 * h, rows] = (m + jnp.log(l))[0]
+                c = c / l
+                lse = m + jnp.log(l)
+                st_ref[0, 0, 2 * h, rows] = lse[0]
                 st_ref[0, 0, 2 * h + 1, rows] = c[0]
-                p = [e_i * inv_l for e_i in e]
+                p = [jnp.exp(s_i - lse) for s_i in s]
                 ds = [(p_i * (d_i - c)).astype(BF16) for p_i, d_i in zip(p, dp)]
                 p = [p_i.astype(BF16) for p_i in p]
                 kt_h, vt_h = k_t[hrow, :near], v_t[hrow, :near]
@@ -184,30 +189,32 @@
     pl.when(role_ref[0] == 1)(lambda: run(True))
 
 
-def attend(role, qd, k, v, lo, k_o, v_o, head, after):
+def attend(role, qd, k, v, lo, k_o, v_o, head, first, batch, prev, after):
     n, seq, dim = k_o.shape
     width = 128
     pairs = dim // width
     pick = lambda t: pl.BlockSpec((1, 1, seq, width), lambda b, p, r: (t, b + lo, 0, p))
     tok_in = pl.BlockSpec((1, seq, width), lambda b, p, r: (b + lo, 0, p))
-    tok = pl.BlockSpec((1, seq, width), lambda b, p, r: (b, 0, p))
-    high = pl.BlockSpec((1, seq, width), lambda b, p, r: (b * r[0], 0, p * r[0]))
+    row = pl.BlockSpec((1, seq, width), lambda b, p, r: (first + b, 0, p))
+    high_in = pl.BlockSpec((1, seq, width), lambda b, p, r: (b * r[0], 0, p * r[0]))
+    high = pl.BlockSpec((1, seq, width), lambda b, p, r: (first + b * r[0], 0, p * r[0]))
     low = pl.BlockSpec((1, seq, width), lambda b, p, r: (b * (1 - r[0]), 0, p * (1 - r[0])))
-    narrow = jax.ShapeDtypeStruct((n, seq, dim), BF16)
+    all_rows = jax.ShapeDtypeStruct((batch, seq, dim), BF16)
     acc = jax.ShapeDtypeStruct((n, seq, dim), F32)
     return pl.pallas_call(
         functools.partial(attn_kernel, head=head, scale=head ** -0.5),
         grid_spec=pltpu.PrefetchScalarGridSpec(
             num_scalar_prefetch=1,
             grid=(n, pairs),
-            in_specs=[pick(1), pick(0), tok_in, tok_in, high, high] + [UNREAD] * len(after),
-            out_specs=[tok, tok, low, low, high, high, pl.BlockSpec((1, 1, 4, seq), lambda b, p, r: (b, p, 0, 0))],
-        ),
-        out_shape=[narrow, narrow, acc, acc, narrow, narrow, jax.ShapeDtypeStruct((n, pairs, 4, seq), F32)],
+            in_specs=[pick(1), pick(0), tok_in, tok_in, high_in, high_in] + [UNREAD] * (len(prev) + len(after)),
+            out_specs=[row, row, high, high, low, low, pl.BlockSpec((1, 1, 4, seq), lambda b, p, r: (b, p, 0, 0))],
+        ),
+        out_shape=[all_rows] * 4 + [acc, acc, jax.ShapeDtypeStruct((n, pairs, 4, seq), F32)],
+        input_output_aliases={7 + i: i for i in range(len(prev))},
         compiler_params=params(2),
         cost_estimate=pl.CostEstimate(flops=32 * n * seq * seq * dim, bytes_accessed=24 * n * seq * dim, transcendentals=0),
         name="attend",
-    )(role, qd, qd, k, v, k_o, v_o, *after)
+    )(role, qd, qd, k, v, k_o, v_o, *prev, *after)
 
 
 def late_kernel(role_ref, q_ref, g_ref, st_ref, k_ref, v_ref, dka_ref, dva_ref, dkb_ref, dvb_ref, *rest, head, scale):
@@ -243,29 +250,29 @@
         dv_ref[0] = dv.astype(BF16)
 
 
-def late(role, qd_o, stats, k, v, lo, dk_acc, dv_acc, dk_b, dv_b, head, after):
+def late(role, qd_o, stats, k, v, lo, dk_acc, dv_acc, dk_all, dv_all, head, first, after):
     n, seq, dim = dk_acc.shape
     width = 128
     pairs = dim // width
     pick = lambda t: pl.BlockSpec((1, 1, seq, width), lambda b, p, r: (t, b * (1 - r[0]), 0, p * (1 - r[0])))
     low_in = pl.BlockSpec((1, seq, width), lambda b, p, r: (lo + b * (1 - r[0]), 0, p * (1 - r[0])))
     low = pl.BlockSpec((1, seq, width), lambda b, p, r: (b * (1 - r[0]), 0, p * (1 - r[0])))
-    first = pl.BlockSpec((1, seq, width), lambda b, p, r: (0, 0, 0))
-    narrow = jax.ShapeDtypeStruct((n, seq, dim), BF16)
+    still = pl.BlockSpec((1, seq, width), lambda b, p, r: (first, 0, 0))
+    out = pl.BlockSpec((1, seq, width), lambda b, p, r: (first + b * (1 - r[0]), 0, p * (1 - r[0])))
     return pl.pallas_call(
         functools.partial(late_kernel, head=head, scale=head ** -0.5),
         grid_spec=pltpu.PrefetchScalarGridSpec(
             num_scalar_prefetch=1,
             grid=(n, pairs),
-            in_specs=[pick(1), pick(0), pl.BlockSpec((1, 1, 4, seq), lambda b, p, r: (b, p, 0, 0)), low_in, low_in, low, low, first, first] + [UNREAD] * len(after),
-            out_specs=[low] * 2,
-        ),
-        out_shape=[narrow] * 2,
+            in_specs=[pick(1), pick(0), pl.BlockSpec((1, 1, 4, seq), lambda b, p, r: (b, p, 0, 0)), low_in, low_in, low, low, still, still] + [UNREAD] * len(after),
+            out_specs=[out] * 2,
+        ),
+        out_shape=[jax.ShapeDtypeStruct(dk_all.shape, BF16)] * 2,
         input_output_aliases={8: 0, 9: 1},
         compiler_params=params(2),
         cost_estimate=pl.CostEstimate(flops=16 * n * seq * seq * dim, bytes_accessed=20 * n * seq * dim, transcendentals=0),
         name="late",
-    )(role, qd_o, qd_o, stats, k, v, dk_acc, dv_acc, dk_b, dv_b, *after)
+    )(role, qd_o, qd_o, stats, k, v, dk_acc, dv_acc, dk_all, dv_all, *after)
 
 
 def split_rows(core_ref, full_ref, own_ref, send_ref):
@@ -281,43 +288,40 @@
     split_rows(core_ref, full_ref, own_ref, send_ref)
 
 
-def row_outputs(batch, run, dim, first):
-    own = pl.BlockSpec((1, run, dim), lambda b, c: (c[0] * (batch // 2) + first + b, 0, 0))
-    other = pl.BlockSpec((1, run, dim), lambda b, c: (first + b, 0, 0))
-    return [own, other], [jax.ShapeDtypeStruct((batch, run, dim), BF16), jax.ShapeDtypeStruct((batch // 2, run, dim), BF16)]
-
-
-def post(core, a, x, lo, w_o, b_o, batch, first, prev):
+def row_outputs(n, run, dim):
+    own = pl.BlockSpec((1, run, dim), lambda b, c: (c[0] * n + b, 0, 0))
+    other = pl.BlockSpec((1, run, dim), lambda b, c: (b, 0, 0))
+    return [own, other], [jax.ShapeDtypeStruct((2 * n, run, dim), BF16), jax.ShapeDtypeStruct((n, run, dim), BF16)]
+
+
+def post(core, a, x, w_o, b_o, after):
     n, seq, dim = a.shape
-    run = seq // 2
     tok = pl.BlockSpec((1, seq, dim), lambda b, c: (b, 0, 0))
-    tok_in = pl.BlockSpec((1, seq, dim), lambda b, c: (b + lo, 0, 0))
     whole = lambda shape: pl.BlockSpec(shape, lambda b, c: (0,) * len(shape))
-    specs, shapes = row_outputs(batch, run, dim, first)
+    specs, shapes = row_outputs(n, seq // 2, dim)
     return pl.pallas_call(
         post_kernel,
         grid_spec=pltpu.PrefetchScalarGridSpec(
             num_scalar_prefetch=1,
             grid=(n,),
-            in_specs=[tok, tok_in, whole((dim, dim)), whole((1, dim))] + [UNREAD] * len(prev),
+            in_specs=[tok, tok, whole((dim, dim)), whole((1, dim))] + [UNREAD] * len(after),
             out_specs=specs,
             scratch_shapes=[pltpu.VMEM((seq, dim), BF16)],
         ),
         out_shape=shapes,
-        input_output_aliases={5 + i: i for i in range(len(prev))},
         compiler_params=params(1),
         cost_estimate=pl.CostEstimate(flops=2 * n * seq * dim * dim, bytes_accessed=6 * n * seq * dim, transcendentals=0),
         name="post",
-    )(core, a, x, w_o, b_o, *prev)
-
-
-def back_kernel(core_ref, dq_ref, dk_ref, dv_ref, x_ref, g_ref, lng_ref, w_ref, prev_ref, *rest):
+    )(core, a, x, w_o, b_o, *after)
+
+
+def back_kernel(core_ref, dq_ref, dk_ref, dv_ref, x_ref, g_ref, lng_ref, w_ref, *rest):
     own_ref, send_ref, acc_ref, full_ref = rest[-4:]
     dim = x_ref.shape[2]
 
     @pl.when(pl.program_id(0) == 0)
     def _():
-        acc_ref[...] = prev_ref[...]
+        acc_ref[...] = jnp.zeros_like(acc_ref)
 
     dh = dot_nn(dq_ref[0], w_ref[0:dim, :]) + dot_nn(dk_ref[0], w_ref[dim:2 * dim, :]) + dot_nn(dv_ref[0], w_ref[2 * dim:3 * dim, :])
     x_hat, inv_std = normed(x_ref[0].astype(F32))
@@ -333,28 +337,25 @@
     acc_ref[5:6, :] += jnp.sum(g, axis=0, keepdims=True)
 
 
-def back(core, dq, dk, dv, x, g, lo, ln_g, w_t, acc, batch, first, prev, after):
+def back(core, dq, dk, dv, x, g, ln_g, w_t, after):
     n, seq, dim = dq.shape
-    run = seq // 2
     tok = pl.BlockSpec((1, seq, dim), lambda b, c: (b, 0, 0))
-    tok_in = pl.BlockSpec((1, seq, dim), lambda b, c: (b + lo, 0, 0))
     whole = lambda shape: pl.BlockSpec(shape, lambda b, c: (0,) * len(shape))
-    specs, shapes = row_outputs(batch, run, dim, first)
+    specs, shapes = row_outputs(n, seq // 2, dim)
     return pl.pallas_call(
         back_kernel,
         grid_spec=pltpu.PrefetchScalarGridSpec(
             num_scalar_prefetch=1,
             grid=(n,),
-            in_specs=[tok] * 3 + [tok_in] * 2 + [whole((1, dim)), whole((3 * dim, dim)), whole((8, dim))] + [UNREAD] * (len(prev) + len(after)),
+            in_specs=[tok] * 5 + [whole((1, dim)), whole((3 * dim, dim))] + [UNREAD] * len(after),
             out_specs=specs + [whole((8, dim))],
             scratch_shapes=[pltpu.VMEM((seq, dim), BF16)],
         ),
         out_shape=shapes + [jax.ShapeDtypeStruct((8, dim), F32)],
-        input_output_aliases={9 + i: i for i in range(len(prev))},
         compiler_params=params(1),
         cost_estimate=pl.CostEstimate(flops=6 * n * seq * dim * dim, bytes_accessed=12 * n * seq * dim, transcendentals=0),
         name="back",
-    )(core, dq, dk, dv, x, g, ln_g, w_t, acc, *prev, *after)
+    )(core, dq, dk, dv, x, g, ln_g, w_t, *after)
 
 
 def tok_dot(a, b):
@@ -387,64 +388,54 @@
 
         spans = ((0, n), (n, half_b - n))
         got = [(handed(g, *span), handed(x, *span)) for span in spans]
-        fronts = []
+        fronts, whole = [], []
         for j, (lo, _) in enumerate(spans):
-            fronts.append(front(side, x, got[j][1], g, got[j][0], ln_g2, ln_b2, w_t, b_all, w_o, lo))
+            *group, h, xb, gb = front(side, x, got[j][1], g, got[j][0], ln_g2, ln_b2, w_t, b_all, w_o, lo, whole)
+            fronts.append(group)
+            whole = [h, xb, gb]
         own, far = [], []
         for i in range(CHUNKS):
-            group, lo = fronts[min(i, 1)], max(i - 1, 0) * n
-            own.append((group, lo))
-            h, qd = group[0][lo:lo + n], group[1][:, lo:lo + n]
-            far.append((send(h, UP), send(qd, DOWN)))
+            (hs, qd, k, v), lo = fronts[min(i, 1)], max(i - 1, 0) * n
+            own.append((qd, k, v, lo))
+            far.append((send(hs[lo:lo + n], UP), send(qd[:, lo:lo + n], DOWN)))
 
         def halves_added(w):
             theirs = send(lax.dynamic_slice_in_dim(w, (1 - core) * half_d, half_d, 0), SWAP_CORE)
             return lax.dynamic_slice_in_dim(w, core * half_d, half_d, 0) + theirs
 
-        att, stats = {}, {}
-        dw = {}
-        d_x, acc = [], jnp.zeros((8, dim), F32)
-
-        def add_to(name, part):
-            dw[name] = part if name not in dw else dw[name] + part
-
-        def forward(i, after):
-            (h, qd, k, v, xb, gb), lo = own[i]
+        accs, stats, sent = {}, {}, {}
+
+        def forward(i, chain):
             k_o, v_o = other_kv(role, far[i][0], w_t, b_all)
-            att[i] = attend(role, qd, k, v, lo, k_o, v_o, head, after)
-            stats[i] = send(att[i][6], DOWN)
-
-        def backward(i, after, d_x, acc):
-            (h, qd, k, v, xb, gb), lo = own[i]
-            _, dq, dk_acc, dv_acc, dk_b, dv_b, _ = att[i]
-            dk, dv = late(role, far[i][1], stats[i], k, v, lo, dk_acc, dv_acc, dk_b, dv_b, head, after)
-            dwk, dwv = tok_dot(dk, h[lo:lo + n]), tok_dot(dv, h[lo:lo + n])
-            add_to('k', dwk)
-            add_to('v', dwv)
-            after = [dwk, dwv]
-            if i == CHUNKS - 1:
-                after = [halves_added(dw['k']), halves_added(dw['v'])]
-            *d_x, acc = back(side, dq, dk, dv, xb, gb, lo, ln_g2, w_t, acc, batch, i * n, d_x, after)
-            return d_x, acc, after
-
-        for i in range(CHUNKS - 1):
-            forward(i, [])
-        d_x, acc, _ = backward(0, [att[CHUNKS - 2][6]], d_x, acc)
-        forward(CHUNKS - 1, [acc])
-        d_x, acc, _ = backward(1, [att[CHUNKS - 1][6]], d_x, acc)
-        y = []
-        for i in range(CHUNKS):
-            (h, qd, k, v, xb, gb), lo = own[i]
-            y = post(side, att[i][0], xb, lo, w_o, b_o, batch, i * n, y)
-            add_to('o', tok_dot(att[i][0], gb[lo:lo + n]))
-            add_to('q', tok_dot(att[i][1], h[lo:lo + n]))
-        d_x, acc, _ = backward(2, [acc, y[1]], d_x, acc)
-        part_o, part_q = halves_added(dw['o']), halves_added(dw['q'])
+            *chain, dk_acc, dv_acc, stats[i] = attend(role, *own[i], k_o, v_o, head, i * n, half_b, chain, [])
+            accs[i] = dk_acc, dv_acc
+            sent[i] = send(stats[i], DOWN)
+            return chain
+
+        def backward(i, chain, after):
+            a, dq, dk, dv = chain
+            _, k, v, lo = own[i]
+            dk, dv = late(role, far[i][1], sent[i], k, v, lo, *accs[i], dk, dv, head, i * n, after)
+            return [a, dq, dk, dv]
+
+        chain = forward(0, [])
+        chain = forward(1, chain)
+        chain = forward(2, chain)
+        chain = backward(0, chain, [])
+        chain = forward(3, chain)
+        chain = backward(1, chain, [])
+        dw_o, dw_q = tok_dot(chain[0], gb), tok_dot(chain[1], h)
+        part_o, part_q = halves_added(dw_o), halves_added(dw_q)
+        chain = backward(2, chain, [part_o, part_q])
         sum_o = part_o + send(part_o, SWAP_CHIP)
         sum_q = part_q + send(part_q, SWAP_CHIP)
-        d_x, acc, (part_k, part_v) = backward(3, [acc, part_o, part_q], d_x, acc)
+        chain = backward(3, chain, [])
+        a, dq, dk, dv = chain
+        part_k, part_v = halves_added(tok_dot(dk, h)), halves_added(tok_dot(dv, h))
         sum_k = part_k + send(part_k, SWAP_CHIP)
         sum_v = part_v + send(part_v, SWAP_CHIP)
+        y = post(side, a, xb, w_o, b_o, [part_k, part_v])
+        *d_x, acc = back(side, dq, dk, dv, xb, gb, ln_g2, w_t, [part_k, part_v])
 
         def joined(own_rows, other_rows):
             return lax.dynamic_update_slice_in_dim(own_rows, send(other_rows, SWAP_CORE), (1 - core) * half_b, 0)

time: 731 us -> 578 us (0.79)
  waiting for transfers between devices: 221 us -> 100 us
  matrix products: 56.6 us -> 33.1 us
  Pallas kernels: 313 us -> 297 us
    ppermute x32, waiting for transfers between devices: 221 us -> 100 us  [send(): return lax.ppermute(z, 'sp', perm)]
    dot_general x16 -> x4, matrix products: 56.6 us -> 33.1 us  [tok_dot(): lax.dot_general(a, b, (((0, 1), (0, 1)), ((), ())), preferred_element_typ...]
    pallas_call x4 -> x1, Pallas kernels: 42.7 us -> 30.3 us  [back(): pl.pallas_call(back_kernel, grid_spec=pltpu.PrefetchScalarGridSpec(num_sc...]
    pallas_call x4 -> x1, Pallas kernels: 17.5 us -> 12.1 us  [post(): pl.pallas_call(post_kernel, grid_spec=pltpu.PrefetchScalarGridSpec(num_sc...]
  transfers between devices with their start and end apart: 32 -> 32, of which waited for: 7 -> 6; matrix products, arithmetic and copies ran while one was open for 17% -> 17% of each run, Pallas kernels for 43% -> 52%
where the time goes in v3:
time: 578 us; the launch traced here: 571 us
  Pallas kernels  297 us (51%)
  waiting for transfers between devices  100 us (17%)
  starting transfers between devices  61.9 us (11%)
  local copies, waits for them, and re-layouts  55.2 us (10%)
  matrix products  33.1 us (6%)
  other arithmetic  21.3 us (4%)
    pallas_call x4, Pallas kernels, attend(): pl.pallas_call(functools.partial(attn_kernel, head=head, scale=head ** (-...  132 us
    ppermute x32, waiting for transfers between devices, send(): return lax.ppermute(z, 'sp', perm)  100 us
    pallas_call x4, Pallas kernels, late(): pl.pallas_call(functools.partial(late_kernel, head=head, scale=head ** (-...  77 us
    ppermute x32, starting transfers between devices, send(): return lax.ppermute(z, 'sp', perm)  61.9 us
    pallas_call x2, Pallas kernels, front(): pl.pallas_call(front_kernel, grid_spec=pltpu.PrefetchScalarGridSpec(num_s...  33.5 us
    dot_general x4, matrix products, tok_dot(): lax.dot_general(a, b, (((0, 1), (0, 1)), ((), ())), preferred_element_typ...  33.1 us
    pallas_call x1, Pallas kernels, back(): pl.pallas_call(back_kernel, grid_spec=pltpu.PrefetchScalarGridSpec(num_sc...  30.3 us
    pallas_call x4, Pallas kernels, other_kv(): pl.pallas_call(kv_kernel, grid_spec=pltpu.PrefetchScalarGridSpec(num_scal...  12.3 us
  transfers between devices with their start and end apart: 32, of which 6 were waited for; matrix products, arithmetic and copies ran while one was open for 17% of the time, Pallas kernels for 52%

profile of v3, /device:TPU:0, one launch (start us, length us, event | category | flops | bytes accessed | tf_op | source)
XLA Modules:
  0.0 570.7 jit_solution(6841719540622505028)
XLA Ops:
  0.6 1.8 constant_dynamic-slice_fusion.7
  3.4 3.2 constant_dynamic-slice_fusion.6
  6.6 2.1 constant_dynamic-slice_fusion.5
  9.2 2.1 constant_dynamic-slice_fusion.4
  14.0 11.0 %front.2 = (bf16[2,512,768]{2,1,0:T(8,128)(2,1)}, bf16[2,2,512,768]{3,2,1,0:T(8,128)(2,1)}, bf16[2,512,768]{2,1,0:T(8,128)(2,1)}, bf16[2,512,768]{2,1,0:T(8,128)...) custom-call(s32[1]{0:T(128)} %bitcast.core_ref, ...), custom_call_target="tpu_custom_call" | custom-call | flops 4831838208 | bytes 14155776 | tf_op jit(solution)/shard_map/front/pallas_call | solution.py:76
  25.0 6.1 %collective-permute-start.7 = (bf16[2,512,768]{2,1,0:T(8,128)(2,1)}, bf16[2,512,768]{2,1,0:T(8,128)(2,1)}, u32[]{:S(2)}, u32[]{:S(2)}) collective-permute-start(bf16[2,512,768]{2,1,0:T(8,128)(2,1)} %get-tuple-element.87), channel_id=1, source_target_pairs={{0,2},{1,3},{4,6},{5,7}} | collective-permute-start | bytes 4718600 | tf_op jit(solution)/shard_map/ppermute | solution.py:384
  31.0 1.3 collective-permute-start.8
  32.4 22.4 %front.3 = (bf16[6,512,768]{2,1,0:T(8,128)(2,1)}, bf16[2,6,512,768]{3,2,1,0:T(8,128)(2,1)}, bf16[6,512,768]{2,1,0:T(8,128)(2,1)}, bf16[6,512,768]{2,1,0:T(8,128)...) custom-call(s32[1]{0:T(128)} %bitcast.core_ref, ...), custom_call_target="tpu_custom_call", output_to_operand_aliasing={{4}: (10, {}), {5}: (11, {}), {6}: (12, {})} | custom-call | flops 14495514624 | bytes 42467328 | tf_op jit(solution)/shard_map/front/pallas_call | solution.py:76
  54.8 2.7 fusion.1
  57.5 5.9 %collective-permute-start.6 = (bf16[2,512,768]{2,1,0:T(8,128)(2,1)S(1)}, bf16[2,512,768]{2,1,0:T(8,128)(2,1)}, u32[]{:S(2)}, u32[]{:S(2)}) collective-permute-start(bf16[2,512,768]{2,1,0:T(8,128)(2,1)S(1)} %get-tuple-element.148), channel_id=1, source_target_pairs={{0,2},{1,3},{4,6},{5,7}} | collective-permute-start | bytes 4718600 | tf_op jit(solution)/shard_map/ppermute | solution.py:384
  63.4 2.6 collective-permute-start.5
  66.0 3.0 other_kv.7
  69.1 32.8 %attend.4 = (bf16[8,512,768]{2,1,0:T(8,128)(2,1)}, bf16[8,512,768]{2,1,0:T(8,128)(2,1)}, bf16[8,512,768]{2,1,0:T(8,128)(2,1)}, bf16[8,512,768]{2,1,0:T(8,128)(2,...) custom-call(s32[1]{0:T(128)} %bitcast.1.role_ref, ...), custom_call_target="tpu_custom_call" | custom-call | flops 12884901888 | bytes 18874368 | tf_op jit(solution)/shard_map/attend/pallas_call | solution.py:204
  101.9 1.3 collective-permute-start.9
  103.2 25.6 %collective-permute-start.4 = (bf16[2,512,768]{2,1,0:T(8,128)(2,1)S(1)}, bf16[2,512,768]{2,1,0:T(8,128)(2,1)}, u32[]{:S(2)}, u32[]{:S(2)}) collective-permute-start(bf16[2,512,768]{2,1,0:T(8,128)(2,1)S(1)} %get-tuple-element.150), channel_id=1, source_target_pairs={{0,2},{1,3},{4,6},{5,7}} | collective-permute-start | bytes 4718600 | tf_op jit(solution)/shard_map/ppermute | solution.py:384
  128.8 6.7 %fusion = (bf16[2,2,512,768]{3,2,1,0:T(8,128)(2,1)}, bf16[2,2,512,768]{3,2,1,0:T(8,128)(2,1)}, bf16[2,2,512,768]{3,2,1,0:T(8,128)(2,1)}) fusion(bf16[2,6,512,768]{3,2,1,0:T(8,128)(2,1)} %get-tuple-element.74.q_ref.g_ref), kind=kLoop, calls=%fused_computation.29 | loop fusion | bytes 18874368 | tf_op jit(solution)/shard_map/slice | solution.py:400
  135.5 1.5 collective-permute-start.14
  137.0 3.1 other_kv.6
  140.1 33.1 %attend.5 = (bf16[8,512,768]{2,1,0:T(8,128)(2,1)}, bf16[8,512,768]{2,1,0:T(8,128)(2,1)}, bf16[8,512,768]{2,1,0:T(8,128)(2,1)}, bf16[8,512,768]{2,1,0:T(8,128)(2,...) custom-call(s32[1]{0:T(128)} %bitcast.1.role_ref, ...), custom_call_target="tpu_custom_call", output_to_operand_aliasing={{0}: (7, {}), {1}: (8, {}), {2}: (9, {}), {3}: (10, {})} | custom-call | flops 12884901888 | bytes 18874368 | tf_op jit(solution)/shard_map/attend/pallas_call | solution.py:204
  173.2 1.5 collective-permute-start.12
  174.8 3.1 other_kv.5
  177.9 33.2 %attend.6 = (bf16[8,512,768]{2,1,0:T(8,128)(2,1)}, bf16[8,512,768]{2,1,0:T(8,128)(2,1)}, bf16[8,512,768]{2,1,0:T(8,128)(2,1)}, bf16[8,512,768]{2,1,0:T(8,128)(2,...) custom-call(s32[1]{0:T(128)} %bitcast.1.role_ref, ...), custom_call_target="tpu_custom_call", output_to_operand_aliasing={{0}: (7, {}), {1}: (8, {}), {2}: (9, {}), {3}: (10, {})} | custom-call | flops 12884901888 | bytes 18874368 | tf_op jit(solution)/shard_map/attend/pallas_call | solution.py:204
  211.1 1.8 collective-permute-start.10
  212.9 3.1 other_kv.4
  217.7 19.2 %late.4 = (bf16[8,512,768]{2,1,0:T(8,128)(2,1)}, bf16[8,512,768]{2,1,0:T(8,128)(2,1)}) custom-call(s32[1]{0:T(128)} %bitcast.1.role_ref, bf16[2,2,512,768]{3,2,1,0:T(8,128)(2,1)} %copy-done.2, bf16[2,2,512,768]{3,2,1,0:T(8,128)(2,1)} %copy-done.2, f32[2,6,4,512]{3,2,1,0:T(4,128)} %copy-done.15, ...), custom_call_target="tpu_custom_call", output_to_operand_aliasing={{0}: (8, {}), {1}: (9, {})} | custom-call | flops 6442450944 | bytes 15728640 | tf_op jit(solution)/shard_map/late/pallas_call | solution.py:262
  236.9 33.1 %attend.7 = (bf16[8,512,768]{2,1,0:T(8,128)(2,1)}, bf16[8,512,768]{2,1,0:T(8,128)(2,1)}, bf16[8,512,768]{2,1,0:T(8,128)(2,1)}, bf16[8,512,768]{2,1,0:T(8,128)(2,...) custom-call(s32[1]{0:T(128)} %bitcast.1.role_ref, ...), custom_call_target="tpu_custom_call", output_to_operand_aliasing={{0}: (7, {}), {1}: (8, {}), {2}: (9, {}), {3}: (10, {})} | custom-call | flops 12884901888 | bytes 18874368 | tf_op jit(solution)/shard_map/attend/pallas_call | solution.py:204
  270.0 9.2 %convolution_bitcast_fusion.3 = f32[768,768]{1,0:T(8,128)S(1)} fusion(bf16[8,512,768]{2,1,0:T(8,128)(2,1)} %get-tuple-element.107.a_ref, bf16[8,512,768]{2,1,0:T(8,128)(2,1)} %get-tuple-element.122.g_ref), kind=kOutput, calls=%fused_computation.3 | convolution fusion | flops 4831838208 | bytes 14942208 | tf_op jit(solution)/shard_map/dot_general | solution.py:362
  279.2 1.3 constant_dynamic-slice_fusion.3
  281.0 7.4 %convolution_bitcast_fusion.2 = f32[768,768]{1,0:T(8,128)S(1)} fusion(bf16[8,512,768]{2,1,0:T(8,128)(2,1)S(1)} %copy-done.1, bf16[8,512,768]{2,1,0:T(8,128)(2,1)} %get-tuple-element.124), kind=kOutput, calls=%fused_computation.2 | convolution fusion | flops 4831838208 | bytes 14942208 | tf_op jit(solution)/shard_map/dot_general | solution.py:362
  288.5 1.4 copy-done.11
  291.0 1.4 collective-permute-start.15
  292.4 2.8 dynamic-slice_add_fusion.3.rest_0_
  295.2 1.3 collective-permute-start.13
  296.5 2.4 dynamic-slice_add_fusion.2.rest_1_
  299.0 53.7 %collective-permute-done.15.st_ref = f32[2,6,4,512]{3,2,1,0:T(4,128)S(1)} collective-permute-done((f32[2,6,4,512]{3,2,1,0:T(4,128)S(1)}, f32[2,6,4,512]{3,2,1,0:T(4,128)S(1)}, u32[]{:S(2)}, u32[]{:S(2)}) %collective-permute-start.15) | collective-permute-done | bytes 98336 | tf_op jit(solution)/shard_map/ppermute | solution.py:384
  352.7 1.3 collective-permute-start.11
  354.0 3.2 collective-permute-start.24
  357.2 19.3 %late.5 = (bf16[8,512,768]{2,1,0:T(8,128)(2,1)}, bf16[8,512,768]{2,1,0:T(8,128)(2,1)}) custom-call(s32[1]{0:T(128)} %bitcast.1.role_ref, bf16[2,2,512,768]{3,2,1,0:T(8,128)(2,1)} %collective-permute-done.14.q_ref.g_ref, bf16[2,2,512,768]{3,2,1,0:T(8,128)(2,1)} %collective-permute-done.14.q_ref.g_ref, ...), custom_call_target="tpu_custom_call", output_to_operand_aliasing={{0}: (8, {}), {1}: (9, {})} | custom-call | flops 6442450944 | bytes 15728640 | tf_op jit(solution)/shard_map/late/pallas_call | solution.py:262
  378.2 19.3 %late.6 = (bf16[8,512,768]{2,1,0:T(8,128)(2,1)}, bf16[8,512,768]{2,1,0:T(8,128)(2,1)}) custom-call(s32[1]{0:T(128)} %bitcast.1.role_ref, bf16[2,2,512,768]{3,2,1,0:T(8,128)(2,1)} %copy-done.3, bf16[2,2,512,768]{3,2,1,0:T(8,128)(2,1)} %copy-done.3, f32[2,6,4,512]{3,2,1,0:T(4,128)} %copy-done.17, ...), custom_call_target="tpu_custom_call", output_to_operand_aliasing={{0}: (8, {}), {1}: (9, {})} | custom-call | flops 6442450944 | bytes 15728640 | tf_op jit(solution)/shard_map/late/pallas_call | solution.py:262
  398.1 19.2 %late.7 = (bf16[8,512,768]{2,1,0:T(8,128)(2,1)}, bf16[8,512,768]{2,1,0:T(8,128)(2,1)}) custom-call(s32[1]{0:T(128)} %bitcast.1.role_ref, bf16[2,2,512,768]{3,2,1,0:T(8,128)(2,1)} %collective-permute-done.10.q_ref.g_ref, bf16[2,2,512,768]{3,2,1,0:T(8,128)(2,1)} %collective-permute-done.10.q_ref.g_ref, ...), custom_call_target="tpu_custom_call", output_to_operand_aliasing={{0}: (8, {}), {1}: (9, {})} | custom-call | flops 6442450944 | bytes 15728640 | tf_op jit(solution)/shard_map/late/pallas_call | solution.py:262
  417.3 9.2 %convolution_bitcast_fusion.1 = f32[768,768]{1,0:T(8,128)S(1)} fusion(bf16[8,512,768]{2,1,0:T(8,128)(2,1)} %get-tuple-element.127.dk_ref, bf16[8,512,768]{2,1,0:T(8,128)(2,1)} %get-tuple-element.124), kind=kOutput, calls=%fused_computation.1 | convolution fusion | flops 4831838208 | bytes 14942208 | tf_op jit(solution)/shard_map/dot_general | solution.py:362
  427.9 7.3 %convolution_bitcast_fusion = f32[768,768]{1,0:T(8,128)S(1)} fusion(bf16[8,512,768]{2,1,0:T(8,128)(2,1)S(1)} %copy-done, bf16[8,512,768]{2,1,0:T(8,128)(2,1)} %get-tuple-element.124), kind=kOutput, calls=%fused_computation | convolution fusion | flops 4831838208 | bytes 14942208 | tf_op jit(solution)/shard_map/dot_general | solution.py:362
  437.3 3.4 broadcast_in_dim.6
  440.7 2.9 constant_dynamic-update-slice_fusion.7
  443.8 2.4 dynamic-slice_add_fusion.1.rest_0_
  446.3 2.5 dynamic-slice_add_fusion.rest_1_
  448.7 30.3 %back.1 = (bf16[16,256,768]{2,1,0:T(8,128)(2,1)}, bf16[8,256,768]{2,1,0:T(8,128)(2,1)}, f32[8,768]{1,0:T(8,128)}) custom-call(s32[1]{0:T(128)} %bitcast.core_ref, bf16[8,512,768]{2,1,0:T(8,128)(2,1)} %get-tuple-element.123.dq_ref, bf16[8,512,768]{2,1,0:T(8,128)(2,1)} %get-tuple-element.127.dk_ref, bf16[8,512,768]{2,1,0:T(8,128)(2,1)} %get-tuple-element.128.dv_ref, ...), custom_call_target="tpu_custom_call" | custom-call | flops 14495514624 | bytes 37748736 | tf_op jit(solution)/shard_map/back/pallas_call | solution.py:345
  479.4 12.1 %post.1 = (bf16[16,256,768]{2,1,0:T(8,128)(2,1)}, bf16[8,256,768]{2,1,0:T(8,128)(2,1)}) custom-call(s32[1]{0:T(128)} %bitcast.core_ref, bf16[8,512,768]{2,1,0:T(8,128)(2,1)} %get-tuple-element.107.a_ref, bf16[8,512,768]{2,1,0:T(8,128)(2,1)} %get-tuple-element.108.x_ref, bf16[768,768]{1,0:T(8,128)(2,1)} %bitcast.40, f32[1,768]{1,0:T(1,128)} %reshape.56.bo_ref, ...), custom_call_target="tpu_custom_call" | custom-call | flops 4831838208 | bytes 18874368 | tf_op jit(solution)/shard_map/post/pallas_call | solution.py:302
  491.8 1.9 collective-permute-start.30
  493.7 2.5 constant_dynamic-update-slice_fusion.6
  496.2 2.8 constant_dynamic-update-slice_fusion.5
  499.1 21.5 %collective-permute-done.30 = f32[384,768]{1,0:T(8,128)S(1)} collective-permute-done((f32[384,768]{1,0:T(8,128)S(1)}, f32[384,768]{1,0:T(8,128)S(1)}, u32[]{:S(2)}, u32[]{:S(2)}) %collective-permute-start.30) | collective-permute-done | bytes 1179680 | tf_op jit(solution)/shard_map/ppermute | solution.py:384
  520.8 1.2 constant_dynamic-update-slice_fusion.1
  522.0 1.4 copy-done.6
  523.5 2.5 constant_dynamic-update-slice_fusion.4
  526.0 19.4 %collective-permute-done.28 = f32[384,768]{1,0:T(8,128)} collective-permute-done((f32[384,768]{1,0:T(8,128)S(1)}, f32[384,768]{1,0:T(8,128)}, u32[]{:S(2)}, u32[]{:S(2)}) %collective-permute-start.28) | collective-permute-done | bytes 1179680 | tf_op jit(solution)/shard_map/ppermute | solution.py:384
  545.4 2.8 constant_dynamic-update-slice_fusion.3
  548.7 2.6 collective-permute-done.22
  551.9 1.7 collective-permute-start.23
  553.6 2.4 collective-permute-done.23
  558.1 1.5 slice_reduce_fusion
  559.6 1.3 constant_dynamic-update-slice_fusion
  561.0 4.6 constant_dynamic-update-slice_fusion.8
  565.6 3.8 constant_dynamic-update-slice_fusion.9
  (111 shorter events, 18.7 us)
Async XLA Ops:
  2.5 8.8 %copy-start.20 = (f32[3,12,64]{2,1,0:T(8,128)S(1)}, f32[3,12,64]{2,1,0:T(8,128)}, u32[]{:S(2)}) copy-start(f32[3,12,64]{2,1,0:T(8,128)} %param.13) | copy-start | bytes 27652
  2.5 9.4 %copy-start.22 = (f32[768]{0:T(1024)S(1)}, f32[768]{0:T(1024)}, u32[]{:S(2)}) copy-start(f32[768]{0:T(1024)} %param.10) | copy-start | bytes 9220
  2.5 10.0 %copy-start.23 = (f32[768]{0:T(1024)S(1)}, f32[768]{0:T(1024)}, u32[]{:S(2)}) copy-start(f32[768]{0:T(1024)} %param.11) | copy-start | bytes 9220
  2.5 29.8 %collective-permute-start = (bf16[6,256,768]{2,1,0:T(8,128)(2,1)S(1)}, bf16[6,256,768]{2,1,0:T(8,128)(2,1)}, u32[]{:S(2)}, u32[]{:S(2)}) collective-permute-start(bf16[6,256,768]{2,1,0:T(8,128)(2,1)S(1)} %constant_dynamic-slice_fusion.7), channel_id=1, source_target_pairs={{0,1},{1,0},{2,3},{3,2},{4,5},{5,4},{6,7},{7,6}} | collective-permute-start | bytes 7077896 | tf_op jit(solution)/shard_map/ppermute | solution.py:384
  6.6 25.8 %collective-permute-start.1 = (bf16[6,256,768]{2,1,0:T(8,128)(2,1)}, bf16[6,256,768]{2,1,0:T(8,128)(2,1)}, u32[]{:S(2)}, u32[]{:S(2)}) collective-permute-start(bf16[6,256,768]{2,1,0:T(8,128)(2,1)} %constant_dynamic-slice_fusion.6), channel_id=1, source_target_pairs={{0,1},{1,0},{2,3},{3,2},{4,5},{5,4},{6,7},{7,6}} | collective-permute-start | bytes 7077896 | tf_op jit(solution)/shard_map/ppermute | solution.py:384
  8.7 4.4 collective-permute-start.2
  11.2 2.6 collective-permute-start.3
  13.1 0.9 copy-start.14
  25.0 41.0 %collective-permute-start.7 = (bf16[2,512,768]{2,1,0:T(8,128)(2,1)}, bf16[2,512,768]{2,1,0:T(8,128)(2,1)}, u32[]{:S(2)}, u32[]{:S(2)}) collective-permute-start(bf16[2,512,768]{2,1,0:T(8,128)(2,1)} %get-tuple-element.87), channel_id=1, source_target_pairs={{0,2},{1,3},{4,6},{5,7}} | collective-permute-start | bytes 4718600 | tf_op jit(solution)/shard_map/ppermute | solution.py:384
  31.0 184.9 %collective-permute-start.8 = (bf16[2,2,512,768]{3,2,1,0:T(8,128)(2,1)}, bf16[2,2,512,768]{3,2,1,0:T(8,128)(2,1)S(1)}, u32[]{:S(2)}, u32[]{:S(2)}) collective-permute-start(bf16[2,2,512,768]{3,2,1,0:T(8,128)(2,1)} %get-tuple-element.84.q_ref.g_ref), channel_id=1, source_target_pairs={{2,0},{3,1},{6,4},{7,5}} | collective-permute-start | bytes 9437192 | tf_op jit(solution)/shard_map/ppermute | solution.py:384
  57.5 78.1 %collective-permute-start.6 = (bf16[2,512,768]{2,1,0:T(8,128)(2,1)S(1)}, bf16[2,512,768]{2,1,0:T(8,128)(2,1)}, u32[]{:S(2)}, u32[]{:S(2)}) collective-permute-start(bf16[2,512,768]{2,1,0:T(8,128)(2,1)S(1)} %get-tuple-element.148), channel_id=1, source_target_pairs={{0,2},{1,3},{4,6},{5,7}} | collective-permute-start | bytes 4718600 | tf_op jit(solution)/shard_map/ppermute | solution.py:384
  63.4 109.8 %collective-permute-start.5 = (bf16[2,512,768]{2,1,0:T(8,128)(2,1)S(1)}, bf16[2,512,768]{2,1,0:T(8,128)(2,1)}, u32[]{:S(2)}, u32[]{:S(2)}) collective-permute-start(bf16[2,512,768]{2,1,0:T(8,128)(2,1)S(1)} %get-tuple-element.149), channel_id=1, source_target_pairs={{0,2},{1,3},{4,6},{5,7}} | collective-permute-start | bytes 4718600 | tf_op jit(solution)/shard_map/ppermute | solution.py:384
  101.9 114.1 %collective-permute-start.9 = (f32[2,6,4,512]{3,2,1,0:T(4,128)}, f32[2,6,4,512]{3,2,1,0:T(4,128)S(1)}, u32[]{:S(2)}, u32[]{:S(2)}) collective-permute-start(f32[2,6,4,512]{3,2,1,0:T(4,128)} %get-tuple-element.100), channel_id=1, source_target_pairs={{2,0},{3,1},{6,4},{7,5}} | collective-permute-start | bytes 294920 | tf_op jit(solution)/shard_map/ppermute | solution.py:384
  103.2 107.9 %collective-permute-start.4 = (bf16[2,512,768]{2,1,0:T(8,128)(2,1)S(1)}, bf16[2,512,768]{2,1,0:T(8,128)(2,1)}, u32[]{:S(2)}, u32[]{:S(2)}) collective-permute-start(bf16[2,512,768]{2,1,0:T(8,128)(2,1)S(1)} %get-tuple-element.150), channel_id=1, source_target_pairs={{0,2},{1,3},{4,6},{5,7}} | collective-permute-start | bytes 4718600 | tf_op jit(solution)/shard_map/ppermute | solution.py:384
  135.5 218.5 %collective-permute-start.14 = (bf16[2,2,512,768]{3,2,1,0:T(8,128)(2,1)}, bf16[2,2,512,768]{3,2,1,0:T(8,128)(2,1)}, u32[]{:S(2)}, u32[]{:S(2)}) collective-permute-start(bf16[2,2,512,768]{3,2,1,0:T(8,128)(2,1)} %get-tuple-element.145), channel_id=1, source_target_pairs={{2,0},{3,1},{6,4},{7,5}} | collective-permute-start | bytes 9437192 | tf_op jit(solution)/shard_map/ppermute | solution.py:384
  173.2 203.3 %collective-permute-start.12 = (bf16[2,2,512,768]{3,2,1,0:T(8,128)(2,1)}, bf16[2,2,512,768]{3,2,1,0:T(8,128)(2,1)S(1)}, u32[]{:S(2)}, u32[]{:S(2)}) collective-permute-start(bf16[2,2,512,768]{3,2,1,0:T(8,128)(2,1)} %get-tuple-element.146), channel_id=1, source_target_pairs={{2,0},{3,1},{6,4},{7,5}} | collective-permute-start | bytes 9437192 | tf_op jit(solution)/shard_map/ppermute | solution.py:384
  211.1 186.4 %collective-permute-start.10 = (bf16[2,2,512,768]{3,2,1,0:T(8,128)(2,1)}, bf16[2,2,512,768]{3,2,1,0:T(8,128)(2,1)}, u32[]{:S(2)}, u32[]{:S(2)}) collective-permute-start(bf16[2,2,512,768]{3,2,1,0:T(8,128)(2,1)} %get-tuple-element.147), channel_id=1, source_target_pairs={{2,0},{3,1},{6,4},{7,5}} | collective-permute-start | bytes 9437192 | tf_op jit(solution)/shard_map/ppermute | solution.py:384
  215.9 0.7 copy-start.15
  215.9 1.7 copy-start.2
  270.0 11.0 %copy-start.1 = (bf16[8,512,768]{2,1,0:T(8,128)(2,1)S(1)}, bf16[8,512,768]{2,1,0:T(8,128)(2,1)}, u32[]{:S(2)}) copy-start(bf16[8,512,768]{2,1,0:T(8,128)(2,1)} %get-tuple-element.123.dq_ref) | copy-start | bytes 18874372
  279.2 1.8 copy-start.13
  280.5 10.5 %collective-permute-start.16 = (f32[384,768]{1,0:T(8,128)}, f32[384,768]{1,0:T(8,128)}, u32[]{:S(2)}, u32[]{:S(2)}) collective-permute-start(f32[384,768]{1,0:T(8,128)} %constant_dynamic-slice_fusion.3), channel_id=1, source_target_pairs={{0,1},{1,0},{2,3},{3,2},{4,5},{5,4},{6,7},{7,6}} | collective-permute-start | bytes 3538952 | tf_op jit(solution)/shard_map/ppermute | solution.py:384
  281.0 10.0 %copy-start.25 = (f32[2,6,4,512]{3,2,1,0:T(4,128)S(1)}, f32[2,6,4,512]{3,2,1,0:T(4,128)}, u32[]{:S(2)}) copy-start(f32[2,6,4,512]{3,2,1,0:T(4,128)} %get-tuple-element.115) | copy-start | bytes 294916
  288.5 1.4 copy-start.11
  289.9 5.4 copy-start.26
  290.9 4.3 collective-permute-start.17
  291.0 5.6 copy-start.12
  291.0 61.7 %copy-start.27 = (f32[2,6,4,512]{3,2,1,0:T(4,128)S(1)}, f32[2,6,4,512]{3,2,1,0:T(4,128)}, u32[]{:S(2)}) copy-start(f32[2,6,4,512]{3,2,1,0:T(4,128)} %get-tuple-element.109) | copy-start | bytes 294916
  291.0 61.7 %collective-permute-start.15 = (f32[2,6,4,512]{3,2,1,0:T(4,128)S(1)}, f32[2,6,4,512]{3,2,1,0:T(4,128)S(1)}, u32[]{:S(2)}, u32[]{:S(2)}) collective-permute-start(f32[2,6,4,512]{3,2,1,0:T(4,128)S(1)} %copy-done.25), channel_id=1, source_target_pairs={{2,0},{3,1},{6,4},{7,5}} | collective-permute-start | bytes 294920 | tf_op jit(solution)/shard_map/ppermute | solution.py:384
  295.2 81.3 %collective-permute-start.13 = (f32[2,6,4,512]{3,2,1,0:T(4,128)S(1)}, f32[2,6,4,512]{3,2,1,0:T(4,128)S(1)}, u32[]{:S(2)}, u32[]{:S(2)}) collective-permute-start(f32[2,6,4,512]{3,2,1,0:T(4,128)S(1)} %copy-done.26), channel_id=1, source_target_pairs={{2,0},{3,1},{6,4},{7,5}} | collective-permute-start | bytes 294920 | tf_op jit(solution)/shard_map/ppermute | solution.py:384
  352.7 4.5 copy-start.18
  352.7 44.8 %collective-permute-start.11 = (f32[2,6,4,512]{3,2,1,0:T(4,128)S(1)}, f32[2,6,4,512]{3,2,1,0:T(4,128)S(1)}, u32[]{:S(2)}, u32[]{:S(2)}) collective-permute-start(f32[2,6,4,512]{3,2,1,0:T(4,128)S(1)} %copy-done.27), channel_id=1, source_target_pairs={{2,0},{3,1},{6,4},{7,5}} | collective-permute-start | bytes 294920 | tf_op jit(solution)/shard_map/ppermute | solution.py:384
  354.0 83.3 %collective-permute-start.24 = (f32[384,768]{1,0:T(8,128)}, f32[384,768]{1,0:T(8,128)}, u32[]{:S(2)}, u32[]{:S(2)}) collective-permute-start(f32[384,768]{1,0:T(8,128)} %dynamic-slice_add_fusion.2.rest_1_), channel_id=1, source_target_pairs={{0,2},{1,3},{2,0},{3,1},{4,6},{5,7},{6,4},{7,5}} | collective-permute-start | bytes 3538952 | tf_op jit(solution)/shard_map/ppermute | solution.py:384
  376.5 0.6 copy-start.17
  376.5 1.6 copy-start.3
  397.5 0.6 copy-start.16
  417.3 10.6 %copy-start = (bf16[8,512,768]{2,1,0:T(8,128)(2,1)S(1)}, bf16[8,512,768]{2,1,0:T(8,128)(2,1)}, u32[]{:S(2)}) copy-start(bf16[8,512,768]{2,1,0:T(8,128)(2,1)} %get-tuple-element.128.dv_ref) | copy-start | bytes 18874372
  426.5 8.7 %copy-start.9 = (f32[768,768]{1,0:T(8,128)}, f32[768,768]{1,0:T(8,128)S(1)}, u32[]{:S(2)}) copy-start(f32[768,768]{1,0:T(8,128)S(1)} %convolution_bitcast_fusion.1) | copy-start | bytes 7077892
  427.7 16.1 %collective-permute-start.18 = (f32[384,768]{1,0:T(8,128)}, f32[384,768]{1,0:T(8,128)}, u32[]{:S(2)}, u32[]{:S(2)}) collective-permute-start(f32[384,768]{1,0:T(8,128)} %constant_dynamic-slice_fusion.1), channel_id=1, source_target_pairs={{0,1},{1,0},{2,3},{3,2},{4,5},{5,4},{6,7},{7,6}} | collective-permute-start | bytes 3538952 | tf_op jit(solution)/shard_map/ppermute | solution.py:384
  427.9 8.7 %copy-start.24 = (f32[768]{0:T(1024)S(1)}, f32[768]{0:T(1024)}, u32[]{:S(2)}) copy-start(f32[768]{0:T(1024)} %param.15) | copy-start | bytes 9220
  436.4 9.9 %collective-permute-start.19 = (f32[384,768]{1,0:T(8,128)}, f32[384,768]{1,0:T(8,128)}, u32[]{:S(2)}, u32[]{:S(2)}) collective-permute-start(f32[384,768]{1,0:T(8,128)} %constant_dynamic-slice_fusion), channel_id=1, source_target_pairs={{0,1},{1,0},{2,3},{3,2},{4,5},{5,4},{6,7},{7,6}} | collective-permute-start | bytes 3538952 | tf_op jit(solution)/shard_map/ppermute | solution.py:384
  440.7 3.1 copy-start.10
  443.6 50.1 %collective-permute-start.25 = (f32[384,768]{1,0:T(8,128)S(1)}, f32[384,768]{1,0:T(8,128)}, u32[]{:S(2)}, u32[]{:S(2)}) collective-permute-start(f32[384,768]{1,0:T(8,128)S(1)} %get-tuple-element.144), channel_id=1, source_target_pairs={{0,1},{1,0},{2,3},{3,2},{4,5},{5,4},{6,7},{7,6}} | collective-permute-start | bytes 3538952 | tf_op jit(solution)/shard_map/ppermute | solution.py:384
  446.3 49.9 %collective-permute-start.26 = (f32[384,768]{1,0:T(8,128)}, f32[384,768]{1,0:T(8,128)}, u32[]{:S(2)}, u32[]{:S(2)}) collective-permute-start(f32[384,768]{1,0:T(8,128)} %dynamic-slice_add_fusion.1.rest_0_), channel_id=1, source_target_pairs={{0,2},{1,3},{2,0},{3,1},{4,6},{5,7},{6,4},{7,5}} | collective-permute-start | bytes 3538952 | tf_op jit(solution)/shard_map/ppermute | solution.py:384
  479.0 12.8 %copy-start.4 = (f32[384,768]{1,0:T(8,128)S(1)}, f32[384,768]{1,0:T(8,128)}, u32[]{:S(2)}) copy-start(f32[384,768]{1,0:T(8,128)} %dynamic-slice_add_fusion.3.rest_0_) | copy-start | bytes 3538948
  479.0 81.9 %collective-permute-start.21 = (bf16[8,256,768]{2,1,0:T(8,128)(2,1)}, bf16[8,256,768]{2,1,0:T(8,128)(2,1)}, u32[]{:S(2)}, u32[]{:S(2)}) collective-permute-start(bf16[8,256,768]{2,1,0:T(8,128)(2,1)} %get-tuple-element.132), channel_id=1, source_target_pairs={{0,1},{1,0},{2,3},{3,2},{4,5},{5,4},{6,7},{7,6}} | collective-permute-start | bytes 9437192 | tf_op jit(solution)/shard_map/ppermute | solution.py:384
  491.5 74.1 %collective-permute-start.20 = (bf16[8,256,768]{2,1,0:T(8,128)(2,1)}, bf16[8,256,768]{2,1,0:T(8,128)(2,1)}, u32[]{:S(2)}, u32[]{:S(2)}) collective-permute-start(bf16[8,256,768]{2,1,0:T(8,128)(2,1)} %get-tuple-element.130), channel_id=1, source_target_pairs={{0,1},{1,0},{2,3},{3,2},{4,5},{5,4},{6,7},{7,6}} | collective-permute-start | bytes 9437192 | tf_op jit(solution)/shard_map/ppermute | solution.py:384
  491.8 28.8 %collective-permute-start.30 = (f32[384,768]{1,0:T(8,128)S(1)}, f32[384,768]{1,0:T(8,128)S(1)}, u32[]{:S(2)}, u32[]{:S(2)}) collective-permute-start(f32[384,768]{1,0:T(8,128)S(1)} %copy-done.4), channel_id=1, source_target_pairs={{0,2},{1,3},{2,0},{3,1},{4,6},{5,7},{6,4},{7,5}} | collective-permute-start | bytes 3538952 | tf_op jit(solution)/shard_map/ppermute | solution.py:384
  493.7 5.3 copy-start.5
  499.0 24.5 %collective-permute-start.27 = (f32[384,768]{1,0:T(8,128)S(1)}, f32[384,768]{1,0:T(8,128)}, u32[]{:S(2)}, u32[]{:S(2)}) collective-permute-start(f32[384,768]{1,0:T(8,128)S(1)} %get-tuple-element.142), channel_id=1, source_target_pairs={{0,1},{1,0},{2,3},{3,2},{4,5},{5,4},{6,7},{7,6}} | collective-permute-start | bytes 3538952 | tf_op jit(solution)/shard_map/ppermute | solution.py:384
  499.0 46.4 %collective-permute-start.28 = (f32[384,768]{1,0:T(8,128)S(1)}, f32[384,768]{1,0:T(8,128)}, u32[]{:S(2)}, u32[]{:S(2)}) collective-permute-start(f32[384,768]{1,0:T(8,128)S(1)} %copy-done.5), channel_id=1, source_target_pairs={{0,2},{1,3},{2,0},{3,1},{4,6},{5,7},{6,4},{7,5}} | collective-permute-start | bytes 3538952 | tf_op jit(solution)/shard_map/ppermute | solution.py:384
  522.0 1.4 copy-start.6
  523.4 36.1 %collective-permute-start.31 = (f32[384,768]{1,0:T(8,128)}, f32[384,768]{1,0:T(8,128)}, u32[]{:S(2)}, u32[]{:S(2)}) collective-permute-start(f32[384,768]{1,0:T(8,128)} %get-tuple-element.138), channel_id=1, source_target_pairs={{0,1},{1,0},{2,3},{3,2},{4,5},{5,4},{6,7},{7,6}} | collective-permute-start | bytes 3538952 | tf_op jit(solution)/shard_map/ppermute | solution.py:384
  523.5 24.7 %copy-start.21 = (f32[8,768]{1,0:T(8,128)S(1)}, f32[8,768]{1,0:T(8,128)}, u32[]{:S(2)}) copy-start(f32[8,768]{1,0:T(8,128)} %get-tuple-element.133) | copy-start | bytes 73732
  523.5 36.1 %copy-start.7 = (f32[768,768]{1,0:T(8,128)S(1)}, f32[768,768]{1,0:T(8,128)}, u32[]{:S(2)}) copy-start(f32[768,768]{1,0:T(8,128)} %copy-done.6) | copy-start | bytes 7077892
  548.2 21.1 %collective-permute-start.29 = (f32[384,768]{1,0:T(8,128)}, f32[384,768]{1,0:T(8,128)S(1)}, u32[]{:S(2)}, u32[]{:S(2)}) collective-permute-start(f32[384,768]{1,0:T(8,128)} %get-tuple-element.140), channel_id=1, source_target_pairs={{0,1},{1,0},{2,3},{3,2},{4,5},{5,4},{6,7},{7,6}} | collective-permute-start | bytes 3538952 | tf_op jit(solution)/shard_map/ppermute | solution.py:384
  548.2 3.1 collective-permute-start.22
  551.9 4.1 collective-permute-start.23
  556.8 0.6 copy-start.19
  560.9 9.5 %copy-start.8 = (f32[768,768]{1,0:T(8,128)}, f32[768,768]{1,0:T(8,128)S(1)}, u32[]{:S(2)}) copy-start(f32[768,768]{1,0:T(8,128)S(1)} %constant_dynamic-update-slice_fusion) | copy-start | bytes 7077892

commit v4 on v3

--- a/solution.py
+++ b/solution.py
@@ -12,6 +12,7 @@
 F32 = jnp.float32
 BF16 = jnp.bfloat16
 CHUNKS = 4
+PAIR = 128
 UP = [(0, 2), (1, 3)]
 DOWN = [(2, 0), (3, 1)]
 SWAP_CHIP = [(0, 2), (1, 3), (2, 0), (3, 1)]
@@ -123,95 +124,105 @@
     return jnp.where((lane >= h * head) & (lane < (h + 1) * head), z, jnp.zeros_like(z))
 
 
-def attn_kernel(role_ref, q_ref, g_ref, k_ref, v_ref, ko_ref, vo_ref, *rest, head, scale):
-    a_ref, dq_ref, dkb_ref, dvb_ref, dk_ref, dv_ref, st_ref = rest[-7:]
+def each_pair(body, tok_refs, st_ref):
+    def step(p, carry):
+        cols = pl.ds(pl.multiple_of(p * PAIR, PAIR), PAIR)
+        views = [r.at[:, :, cols] if len(r.shape) == 3 else r.at[:, :, :, cols] for r in tok_refs]
+        body(*views, st_ref.at[:, pl.ds(p, 1)])
+        return carry
+
+    lax.fori_loop(0, st_ref.shape[1], step, 0)
+
+
+def attn_kernel(role_ref, *refs, head, scale):
+    tok_refs, st_ref = refs[:6] + refs[-7:-1], refs[-1]
+    pl.when(role_ref[0] == 0)(lambda: each_pair(functools.partial(attn_pair, rect=False, head=head, scale=scale), tok_refs, st_ref))
+    pl.when(role_ref[0] == 1)(lambda: each_pair(functools.partial(attn_pair, rect=True, head=head, scale=scale), tok_refs, st_ref))
+
+
+def attn_pair(q_ref, g_ref, k_ref, v_ref, ko_ref, vo_ref, a_ref, dq_ref, dkb_ref, dvb_ref, dk_ref, dv_ref, st_ref, *, rect, head, scale):
     seq, width = k_ref.shape[1:]
     blk = seq // 2
     causal = lax.broadcasted_iota(jnp.int32, (blk, blk), 0) <= lax.broadcasted_iota(jnp.int32, (blk, blk), 1)
 
-    def run(rect):
-        k_t, v_t = k_ref[0].T, v_ref[0].T
-        if rect:
-            ko_t, vo_t = ko_ref[0].T, vo_ref[0].T
-        for qi in range(2):
-            rows = slice(qi * blk, (qi + 1) * blk)
-            near = (qi + 1) * blk
-            q2 = q_ref[0, 0, rows, :] * jnp.asarray(scale, BF16)
-            g2 = g_ref[0, 0, rows, :]
-            o_parts, dq_parts, p_near, ds_near, q_only, g_only = [], [], [], [], [], []
-            for h in range(width // head):
-                hrow = slice(h * head, (h + 1) * head)
-                qm, gm = head_only(q2, h, head), head_only(g2, h, head)
-
-                def products(mine, far, z):
-                    near_z = dot_nt(mine[0, :near, :], z)
-                    parts = [near_z] if qi == 0 else [near_z[:blk], near_z[blk:]]
-                    return parts + ([dot_nt(far[0], z)] if rect else [])
-
-                s = products(k_ref, ko_ref, qm)
-                s[qi] = jnp.where(causal, s[qi], -jnp.inf)
-                m = functools.reduce(jnp.maximum, [jnp.max(s_i, axis=0, keepdims=True) for s_i in s])
-                e = [jnp.exp(s_i - m) for s_i in s]
-                dp = products(v_ref, vo_ref, gm)
-                l = functools.reduce(jnp.add, [jnp.sum(e_i, axis=0, keepdims=True) for e_i in e])
-                c = functools.reduce(jnp.add, [jnp.sum(e_i * d_i, axis=0, keepdims=True) for e_i, d_i in zip(e, dp)])
-                c = c / l
-                lse = m + jnp.log(l)
-                st_ref[0, 0, 2 * h, rows] = lse[0]
-                st_ref[0, 0, 2 * h + 1, rows] = c[0]
-                p = [jnp.exp(s_i - lse) for s_i in s]
-                ds = [(p_i * (d_i - c)).astype(BF16) for p_i, d_i in zip(p, dp)]
-                p = [p_i.astype(BF16) for p_i in p]
-                kt_h, vt_h = k_t[hrow, :near], v_t[hrow, :near]
-                if rect:
-                    kt_h = jnp.concatenate([kt_h, ko_t[hrow]], axis=1)
-                    vt_h = jnp.concatenate([vt_h, vo_t[hrow]], axis=1)
-                o_parts.append(dot_nn(vt_h, jnp.concatenate(p, axis=0)))
-                dq_parts.append(dot_nn(kt_h, jnp.concatenate(ds, axis=0)))
-                p_near.append(jnp.concatenate(p[:qi + 1], axis=0))
-                ds_near.append(jnp.concatenate(ds[:qi + 1], axis=0))
-                q_only.append(qm)
-                g_only.append(gm)
-            a_ref[0, rows, :] = jnp.concatenate(o_parts, axis=0).T.astype(BF16)
-            dq_ref[0, rows, :] = (jnp.concatenate(dq_parts, axis=0).T * scale).astype(BF16)
-            for acc_ref, parts, other in ((dk_ref, ds_near, q_only), (dv_ref, p_near, g_only)):
-                val = dot_nn(jnp.concatenate(parts, axis=1), jnp.concatenate(other, axis=0))
-                if qi == 0:
-                    acc_ref[0, :blk, :] = val
-                else:
-                    acc_ref[0, :blk, :] += val[:blk]
-                    acc_ref[0, blk:, :] = val[blk:]
-        if rect:
-            dkb_ref[0] = dk_ref[0].astype(BF16)
-            dvb_ref[0] = dv_ref[0].astype(BF16)
-
-    pl.when(role_ref[0] == 0)(lambda: run(False))
-    pl.when(role_ref[0] == 1)(lambda: run(True))
+    k_t, v_t = k_ref[0].T, v_ref[0].T
+    if rect:
+        ko_t, vo_t = ko_ref[0].T, vo_ref[0].T
+    for qi in range(2):
+        rows = slice(qi * blk, (qi + 1) * blk)
+        near = (qi + 1) * blk
+        q2 = q_ref[0, 0, rows, :] * jnp.asarray(scale, BF16)
+        g2 = g_ref[0, 0, rows, :]
+        o_parts, dq_parts, p_near, ds_near, q_only, g_only = [], [], [], [], [], []
+        for h in range(width // head):
+            hrow = slice(h * head, (h + 1) * head)
+            qm, gm = head_only(q2, h, head), head_only(g2, h, head)
+
+            def products(mine, far, z):
+                near_z = dot_nt(mine[0, :near, :], z)
+                parts = [near_z] if qi == 0 else [near_z[:blk], near_z[blk:]]
+                return parts + ([dot_nt(far[0], z)] if rect else [])
+
+            s = products(k_ref, ko_ref, qm)
+            s[qi] = jnp.where(causal, s[qi], -jnp.inf)
+            m = functools.reduce(jnp.maximum, [jnp.max(s_i, axis=0, keepdims=True) for s_i in s])
+            e = [jnp.exp(s_i - m) for s_i in s]
+            dp = products(v_ref, vo_ref, gm)
+            l = functools.reduce(jnp.add, [jnp.sum(e_i, axis=0, keepdims=True) for e_i in e])
+            c = functools.reduce(jnp.add, [jnp.sum(e_i * d_i, axis=0, keepdims=True) for e_i, d_i in zip(e, dp)])
+            inv_l = 1.0 / l
+            c = c * inv_l
+            st_ref[0, 0, 2 * h, rows] = (m + jnp.log(l))[0]
+            st_ref[0, 0, 2 * h + 1, rows] = c[0]
+            p = [e_i * inv_l for e_i in e]
+            ds = [(p_i * (d_i - c)).astype(BF16) for p_i, d_i in zip(p, dp)]
+            p = [p_i.astype(BF16) for p_i in p]
+            kt_h, vt_h = k_t[hrow, :near], v_t[hrow, :near]
+            if rect:
+                kt_h = jnp.concatenate([kt_h, ko_t[hrow]], axis=1)
+                vt_h = jnp.concatenate([vt_h, vo_t[hrow]], axis=1)
+            o_parts.append(dot_nn(vt_h, jnp.concatenate(p, axis=0)))
+            dq_parts.append(dot_nn(kt_h, jnp.concatenate(ds, axis=0)))
+            p_near.append(jnp.concatenate(p[:qi + 1], axis=0))
+            ds_near.append(jnp.concatenate(ds[:qi + 1], axis=0))
+            q_only.append(qm)
+            g_only.append(gm)
+        a_ref[0, rows, :] = jnp.concatenate(o_parts, axis=0).T.astype(BF16)
+        dq_ref[0, rows, :] = (jnp.concatenate(dq_parts, axis=0).T * scale).astype(BF16)
+        for acc_ref, parts, other in ((dk_ref, ds_near, q_only), (dv_ref, p_near, g_only)):
+            val = dot_nn(jnp.concatenate(parts, axis=1), jnp.concatenate(other, axis=0))
+            if qi == 0:
+                acc_ref[0, :blk, :] = val
+            else:
+                acc_ref[0, :blk, :] += val[:blk]
+                acc_ref[0, blk:, :] = val[blk:]
+    if rect:
+        dkb_ref[0] = dk_ref[0].astype(BF16)
+        dvb_ref[0] = dv_ref[0].astype(BF16)
 
 
 def attend(role, qd, k, v, lo, k_o, v_o, head, first, batch, prev, after):
     n, seq, dim = k_o.shape
-    width = 128
-    pairs = dim // width
-    pick = lambda t: pl.BlockSpec((1, 1, seq, width), lambda b, p, r: (t, b + lo, 0, p))
-    tok_in = pl.BlockSpec((1, seq, width), lambda b, p, r: (b + lo, 0, p))
-    row = pl.BlockSpec((1, seq, width), lambda b, p, r: (first + b, 0, p))
-    high_in = pl.BlockSpec((1, seq, width), lambda b, p, r: (b * r[0], 0, p * r[0]))
-    high = pl.BlockSpec((1, seq, width), lambda b, p, r: (first + b * r[0], 0, p * r[0]))
-    low = pl.BlockSpec((1, seq, width), lambda b, p, r: (b * (1 - r[0]), 0, p * (1 - r[0])))
+    pairs = dim // PAIR
+    pick = lambda t: pl.BlockSpec((1, 1, seq, dim), lambda b, r: (t, b + lo, 0, 0))
+    tok_in = pl.BlockSpec((1, seq, dim), lambda b, r: (b + lo, 0, 0))
+    row = pl.BlockSpec((1, seq, dim), lambda b, r: (first + b, 0, 0))
+    high_in = pl.BlockSpec((1, seq, dim), lambda b, r: (b * r[0], 0, 0))
+    high = pl.BlockSpec((1, seq, dim), lambda b, r: (first + b * r[0], 0, 0))
+    low = pl.BlockSpec((1, seq, dim), lambda b, r: (b * (1 - r[0]), 0, 0))
     all_rows = jax.ShapeDtypeStruct((batch, seq, dim), BF16)
     acc = jax.ShapeDtypeStruct((n, seq, dim), F32)
     return pl.pallas_call(
         functools.partial(attn_kernel, head=head, scale=head ** -0.5),
         grid_spec=pltpu.PrefetchScalarGridSpec(
             num_scalar_prefetch=1,
-            grid=(n, pairs),
+            grid=(n,),
             in_specs=[pick(1), pick(0), tok_in, tok_in, high_in, high_in] + [UNREAD] * (len(prev) + len(after)),
-            out_specs=[row, row, high, high, low, low, pl.BlockSpec((1, 1, 4, seq), lambda b, p, r: (b, p, 0, 0))],
+            out_specs=[row, row, high, high, low, low, pl.BlockSpec((1, pairs, 4, seq), lambda b, r: (b, 0, 0, 0))],
         ),
         out_shape=[all_rows] * 4 + [acc, acc, jax.ShapeDtypeStruct((n, pairs, 4, seq), F32)],
         input_output_aliases={7 + i: i for i in range(len(prev))},
-        compiler_params=params(2),
+        compiler_params=params(1),
         cost_estimate=pl.CostEstimate(flops=32 * n * seq * seq * dim, bytes_accessed=24 * n * seq * dim, transcendentals=0),
         name="attend",
     )(role, qd, qd, k, v, k_o, v_o, *prev, *after)
@@ -219,8 +230,6 @@
 
 def late_kernel(role_ref, q_ref, g_ref, st_ref, k_ref, v_ref, dka_ref, dva_ref, dkb_ref, dvb_ref, *rest, head, scale):
     dk_ref, dv_ref = rest[-2:]
-    seq, width = k_ref.shape[1:]
-    blk = seq // 2
 
     @pl.when(role_ref[0] == 1)
     def _():
@@ -229,47 +238,54 @@
 
     @pl.when(role_ref[0] == 0)
     def _():
-        dk, dv = dka_ref[0], dva_ref[0]
-        for qi in range(2):
-            rows = slice(qi * blk, (qi + 1) * blk)
-            q2 = q_ref[0, 0, rows, :] * jnp.asarray(scale, BF16)
-            g2 = g_ref[0, 0, rows, :]
-            ps, dss, q_only, g_only = [], [], [], []
-            for h in range(width // head):
-                qm, gm = head_only(q2, h, head), head_only(g2, h, head)
-                lse = st_ref[0, 0, 2 * h, rows].reshape(1, blk)
-                c = st_ref[0, 0, 2 * h + 1, rows].reshape(1, blk)
-                p = jnp.exp(dot_nt(k_ref[0], qm) - lse)
-                dss.append((p * (dot_nt(v_ref[0], gm) - c)).astype(BF16))
-                ps.append(p.astype(BF16))
-                q_only.append(qm)
-                g_only.append(gm)
-            dv = dv + dot_nn(jnp.concatenate(ps, axis=1), jnp.concatenate(g_only, axis=0))
-            dk = dk + dot_nn(jnp.concatenate(dss, axis=1), jnp.concatenate(q_only, axis=0))
-        dk_ref[0] = dk.astype(BF16)
-        dv_ref[0] = dv.astype(BF16)
+        each_pair(functools.partial(late_pair, head=head, scale=scale), (q_ref, g_ref, k_ref, v_ref, dka_ref, dva_ref, dk_ref, dv_ref), st_ref)
+
+
+def late_pair(q_ref, g_ref, k_ref, v_ref, dka_ref, dva_ref, dk_ref, dv_ref, st_ref, *, head, scale):
+    seq, width = k_ref.shape[1:]
+    blk = seq // 2
+    k, v = k_ref[0], v_ref[0]
+    dk, dv = dka_ref[0], dva_ref[0]
+    for qi in range(2):
+        rows = slice(qi * blk, (qi + 1) * blk)
+        q2 = q_ref[0, 0, rows, :] * jnp.asarray(scale, BF16)
+        g2 = g_ref[0, 0, rows, :]
+        ps, dss, q_only, g_only = [], [], [], []
+        for h in range(width // head):
+            qm, gm = head_only(q2, h, head), head_only(g2, h, head)
+            lse = st_ref[0, 0, 2 * h, rows].reshape(1, blk)
+            c = st_ref[0, 0, 2 * h + 1, rows].reshape(1, blk)
+            p = jnp.exp(dot_nt(k, qm) - lse)
+            dss.append((p * (dot_nt(v, gm) - c)).astype(BF16))
+            ps.append(p.astype(BF16))
+            q_only.append(qm)
+            g_only.append(gm)
+        dv = dv + dot_nn(jnp.concatenate(ps, axis=1), jnp.concatenate(g_only, axis=0))
+        dk = dk + dot_nn(jnp.concatenate(dss, axis=1), jnp.concatenate(q_only, axis=0))
+    dk_ref[0] = dk.astype(BF16)
+    dv_ref[0] = dv.astype(BF16)
 
 
 def late(role, qd_o, stats, k, v, lo, dk_acc, dv_acc, dk_all, dv_all, head, first, after):
     n, seq, dim = dk_acc.shape
-    width = 128
-    pairs = dim // width
-    pick = lambda t: pl.BlockSpec((1, 1, seq, width), lambda b, p, r: (t, b * (1 - r[0]), 0, p * (1 - r[0])))
-    low_in = pl.BlockSpec((1, seq, width), lambda b, p, r: (lo + b * (1 - r[0]), 0, p * (1 - r[0])))
-    low = pl.BlockSpec((1, seq, width), lambda b, p, r: (b * (1 - r[0]), 0, p * (1 - r[0])))
-    still = pl.BlockSpec((1, seq, width), lambda b, p, r: (first, 0, 0))
-    out = pl.BlockSpec((1, seq, width), lambda b, p, r: (first + b * (1 - r[0]), 0, p * (1 - r[0])))
+    pairs = dim // PAIR
+    pick = lambda t: pl.BlockSpec((1, 1, seq, dim), lambda b, r: (t, b * (1 - r[0]), 0, 0))
+    low_in = pl.BlockSpec((1, seq, dim), lambda b, r: (lo + b * (1 - r[0]), 0, 0))
+    low = pl.BlockSpec((1, seq, dim), lambda b, r: (b * (1 - r[0]), 0, 0))
+    still = pl.BlockSpec((1, seq, dim), lambda b, r: (first, 0, 0))
+    out = pl.BlockSpec((1, seq, dim), lambda b, r: (first + b * (1 - r[0]), 0, 0))
+    stat = pl.BlockSpec((1, pairs, 4, seq), lambda b, r: (b * (1 - r[0]), 0, 0, 0))
     return pl.pallas_call(
         functools.partial(late_kernel, head=head, scale=head ** -0.5),
         grid_spec=pltpu.PrefetchScalarGridSpec(
             num_scalar_prefetch=1,
-            grid=(n, pairs),
-            in_specs=[pick(1), pick(0), pl.BlockSpec((1, 1, 4, seq), lambda b, p, r: (b, p, 0, 0)), low_in, low_in, low, low, still, still] + [UNREAD] * len(after),
+            grid=(n,),
+            in_specs=[pick(1), pick(0), stat, low_in, low_in, low, low, still, still] + [UNREAD] * len(after),
             out_specs=[out] * 2,
         ),
         out_shape=[jax.ShapeDtypeStruct(dk_all.shape, BF16)] * 2,
         input_output_aliases={8: 0, 9: 1},
-        compiler_params=params(2),
+        compiler_params=params(1),
         cost_estimate=pl.CostEstimate(flops=16 * n * seq * seq * dim, bytes_accessed=20 * n * seq * dim, transcendentals=0),
         name="late",
     )(role, qd_o, qd_o, stats, k, v, dk_acc, dv_acc, dk_all, dv_all, *after)
@@ -356,6 +372,44 @@
         cost_estimate=pl.CostEstimate(flops=6 * n * seq * dim * dim, bytes_accessed=12 * n * seq * dim, transcendentals=0),
         name="back",
     )(core, dq, dk, dv, x, g, ln_g, w_t, *after)
+
+
+def join_kernel(core_ref, *refs):
+    own, other, (three_ref, one_ref) = refs[:4], refs[4:8], refs[8:]
+
+    def put(parts):
+        for t in range(3):
+            three_ref[t, 0] = parts[t][...]
+        one_ref[0] = parts[3][...]
+
+    pl.when(pl.program_id(0) == 0)(lambda: put(own))
+    pl.when(pl.program_id(0) == 1)(lambda: put(other))
+
+
+def join(core, own, other):
+    half, dim = own[0].shape
+    rows = 128
+    steps = half // rows
+    mine = pl.BlockSpec((rows, dim), lambda j, r, c: (r * (1 - j) + (steps - 1) * j, 0))
+    theirs = pl.BlockSpec((rows, dim), lambda j, r, c: (r * j, 0))
+    side = lambda j, c: c[0] * (1 - j) + (1 - c[0]) * j
+    three, one = pl.pallas_call(
+        join_kernel,
+        grid_spec=pltpu.PrefetchScalarGridSpec(
+            num_scalar_prefetch=1,
+            grid=(2, steps),
+            in_specs=[mine] * 4 + [theirs] * 4,
+            out_specs=[
+                pl.BlockSpec((3, 1, rows, dim), lambda j, r, c: (0, side(j, c), r, 0)),
+                pl.BlockSpec((1, rows, dim), lambda j, r, c: (side(j, c), r, 0)),
+            ],
+        ),
+        out_shape=[jax.ShapeDtypeStruct((3, 2, half, dim), F32), jax.ShapeDtypeStruct((2, half, dim), F32)],
+        compiler_params=params(2),
+        cost_estimate=pl.CostEstimate(flops=8 * half * dim, bytes_accessed=64 * half * dim, transcendentals=0),
+        name="join",
+    )(core, *own, *other)
+    return three.reshape(6 * half, dim), one.reshape(2 * half, dim)
 
 
 def tok_dot(a, b):
@@ -444,13 +498,8 @@
         acc = acc + send(acc, SWAP_CORE)
         acc = acc + send(acc, SWAP_CHIP)
 
-        d_w_out = jnp.zeros((dim, dim), F32)
-        d_w_out = lax.dynamic_update_slice(d_w_out, sum_o, (core * half_d, 0))
-        d_w_out = lax.dynamic_update_slice(d_w_out, send(sum_o, SWAP_CORE), ((1 - core) * half_d, 0))
-        dwt = jnp.zeros((3 * dim, dim), F32)
-        for t, w in enumerate((sum_q, sum_k, sum_v)):
-            dwt = lax.dynamic_update_slice(dwt, w, (t * dim + core * half_d, 0))
-            dwt = lax.dynamic_update_slice(dwt, send(w, SWAP_CORE), (t * dim + (1 - core) * half_d, 0))
+        sums = (sum_q, sum_k, sum_v, sum_o)
+        dwt, d_w_out = join(side, sums, [send(w, SWAP_CORE) for w in sums])
         d_w_qkv = jnp.transpose(dwt.reshape(3, heads, head, dim), (3, 0, 1, 2))
         return y, d_x, acc[0], acc[1], d_w_qkv, acc[2:5].reshape(3, heads, head), d_w_out.reshape(heads, head, dim), acc[5]
 

time: 578 us -> 562 us (0.972)
  Pallas kernels: 297 us -> 313 us
  local copies, waits for them, and re-layouts: 55.2 us -> 42.1 us
  other arithmetic: 21.3 us -> 9.2 us
  starting transfers between devices: 61.9 us -> 55 us
    dynamic_update_slice x4 -> x0, other arithmetic: 9.8 us -> none  [the longest x3 8.56 us: local_step(): dwt = lax.dynamic_update_slice(dwt, w, (t * dim + core * half_d, 0))]
    pallas_call x0 -> x1, Pallas kernels: none -> 8.92 us  [join(): pl.pallas_call(join_kernel, grid_spec=pltpu.PrefetchScalarGridSpec(num_sc...]
    dynamic_update_slice x4 -> x0, local copies, waits for them, and re-layouts: 7.41 us -> none  [the longest x3 6.06 us: local_step(): lax.dynamic_update_slice(dwt, send(w, SWAP_CORE), (t * dim + (1 - core) *...]
    ppermute x32, starting transfers between devices: 61.9 us -> 55 us  [send(): return lax.ppermute(z, 'sp', perm)]
    pallas_call x4, Pallas kernels: 77 us -> 83.1 us  [late(): pl.pallas_call(functools.partial(late_kernel, head=head, scale=head ** (-...]
  transfers between devices with their start and end apart: 32 -> 32, of which waited for: 6 -> 6; matrix products, arithmetic and copies ran while one was open for 17% -> 11% of each run, Pallas kernels for 52% -> 53%
where the time goes in v4:
time: 562 us; the launch traced here: 556 us
  Pallas kernels  313 us (56%)
  waiting for transfers between devices  102 us (18%)
  starting transfers between devices  55 us (10%)
  local copies, waits for them, and re-layouts  42.1 us (7%)
  matrix products  33.1 us (6%)
  other arithmetic  9.2 us (2%)
    pallas_call x4, Pallas kernels, attend(): pl.pallas_call(functools.partial(attn_kernel, head=head, scale=head ** (-...  132 us
    ppermute x32, waiting for transfers between devices, send(): return lax.ppermute(z, 'sp', perm)  102 us
    pallas_call x4, Pallas kernels, late(): pl.pallas_call(functools.partial(late_kernel, head=head, scale=head ** (-...  83.1 us
    ppermute x32, starting transfers between devices, send(): return lax.ppermute(z, 'sp', perm)  55 us
    pallas_call x2, Pallas kernels, front(): pl.pallas_call(front_kernel, grid_spec=pltpu.PrefetchScalarGridSpec(num_s...  33.5 us
    dot_general x4, matrix products, tok_dot(): lax.dot_general(a, b, (((0, 1), (0, 1)), ((), ())), preferred_element_typ...  33.1 us
    pallas_call x1, Pallas kernels, back(): pl.pallas_call(back_kernel, grid_spec=pltpu.PrefetchScalarGridSpec(num_sc...  30.1 us
    pallas_call x1, Pallas kernels, post(): pl.pallas_call(post_kernel, grid_spec=pltpu.PrefetchScalarGridSpec(num_sc...  12.5 us
  transfers between devices with their start and end apart: 32, of which 6 were waited for; matrix products, arithmetic and copies ran while one was open for 11% of the time, Pallas kernels for 53%

profile of v4, /device:TPU:0, one launch (start us, length us, event | category | flops | bytes accessed | tf_op | source)
XLA Modules:
  0.0 555.7 jit_solution(18006005685259603429)
XLA Ops:
  0.6 1.8 constant_dynamic-slice_fusion.7
  2.5 0.9 collective-permute-start
  3.4 3.2 constant_dynamic-slice_fusion.6
  6.6 2.1 constant_dynamic-slice_fusion.5
  9.2 2.1 constant_dynamic-slice_fusion.4
  11.2 0.7 reshape.48.b_ref
  13.1 0.8 collective-permute-done.3.gr_ref
  14.0 11.0 %front.2 = (bf16[2,512,768]{2,1,0:T(8,128)(2,1)}, bf16[2,2,512,768]{3,2,1,0:T(8,128)(2,1)}, bf16[2,512,768]{2,1,0:T(8,128)(2,1)}, bf16[2,512,768]{2,1,0:T(8,128)...) custom-call(s32[1]{0:T(128)} %bitcast.core_ref, ...), custom_call_target="tpu_custom_call" | custom-call | flops 4831838208 | bytes 14155776 | tf_op jit(solution)/shard_map/front/pallas_call | solution.py:77
  25.0 6.1 %collective-permute-start.7 = (bf16[2,512,768]{2,1,0:T(8,128)(2,1)}, bf16[2,512,768]{2,1,0:T(8,128)(2,1)}, u32[]{:S(2)}, u32[]{:S(2)}) collective-permute-start(bf16[2,512,768]{2,1,0:T(8,128)(2,1)} %get-tuple-element.89), channel_id=1, source_target_pairs={{0,2},{1,3},{4,6},{5,7}} | collective-permute-start | bytes 4718600 | tf_op jit(solution)/shard_map/ppermute | solution.py:438
  31.1 1.3 collective-permute-start.8
  32.4 22.4 %front.3 = (bf16[6,512,768]{2,1,0:T(8,128)(2,1)}, bf16[2,6,512,768]{3,2,1,0:T(8,128)(2,1)}, bf16[6,512,768]{2,1,0:T(8,128)(2,1)}, bf16[6,512,768]{2,1,0:T(8,128)...) custom-call(s32[1]{0:T(128)} %bitcast.core_ref, ...), custom_call_target="tpu_custom_call", output_to_operand_aliasing={{4}: (10, {}), {5}: (11, {}), {6}: (12, {})} | custom-call | flops 14495514624 | bytes 42467328 | tf_op jit(solution)/shard_map/front/pallas_call | solution.py:77
  54.9 2.7 fusion.1
  57.5 6.0 %collective-permute-start.6 = (bf16[2,512,768]{2,1,0:T(8,128)(2,1)S(1)}, bf16[2,512,768]{2,1,0:T(8,128)(2,1)}, u32[]{:S(2)}, u32[]{:S(2)}) collective-permute-start(bf16[2,512,768]{2,1,0:T(8,128)(2,1)S(1)} %get-tuple-element.144), channel_id=1, source_target_pairs={{0,2},{1,3},{4,6},{5,7}} | collective-permute-start | bytes 4718600 | tf_op jit(solution)/shard_map/ppermute | solution.py:438
  63.5 2.7 collective-permute-start.5
  66.2 3.1 other_kv.7
  69.2 33.0 %attend.4 = (bf16[8,512,768]{2,1,0:T(8,128)(2,1)}, bf16[8,512,768]{2,1,0:T(8,128)(2,1)}, bf16[8,512,768]{2,1,0:T(8,128)(2,1)}, bf16[8,512,768]{2,1,0:T(8,128)(2,...) custom-call(s32[1]{0:T(128)} %bitcast.1.role_ref, ...), custom_call_target="tpu_custom_call" | custom-call | flops 12884901888 | bytes 18874368 | tf_op jit(solution)/shard_map/attend/pallas_call | solution.py:215
  102.2 1.3 collective-permute-start.9
  103.5 23.9 %collective-permute-start.4 = (bf16[2,512,768]{2,1,0:T(8,128)(2,1)S(1)}, bf16[2,512,768]{2,1,0:T(8,128)(2,1)}, u32[]{:S(2)}, u32[]{:S(2)}) collective-permute-start(bf16[2,512,768]{2,1,0:T(8,128)(2,1)S(1)} %get-tuple-element.146), channel_id=1, source_target_pairs={{0,2},{1,3},{4,6},{5,7}} | collective-permute-start | bytes 4718600 | tf_op jit(solution)/shard_map/ppermute | solution.py:438
  127.4 6.7 %fusion = (bf16[2,2,512,768]{3,2,1,0:T(8,128)(2,1)}, bf16[2,2,512,768]{3,2,1,0:T(8,128)(2,1)}, bf16[2,2,512,768]{3,2,1,0:T(8,128)(2,1)}) fusion(bf16[2,6,512,768]{3,2,1,0:T(8,128)(2,1)} %get-tuple-element.76.refs_0_.refs_1_), kind=kLoop, calls=%fused_computation.21 | loop fusion | bytes 18874368 | tf_op jit(solution)/shard_map/slice | solution.py:454
  134.1 1.5 collective-permute-start.14
  135.6 3.1 other_kv.6
  138.7 33.1 %attend.5 = (bf16[8,512,768]{2,1,0:T(8,128)(2,1)}, bf16[8,512,768]{2,1,0:T(8,128)(2,1)}, bf16[8,512,768]{2,1,0:T(8,128)(2,1)}, bf16[8,512,768]{2,1,0:T(8,128)(2,...) custom-call(s32[1]{0:T(128)} %bitcast.1.role_ref, ...), custom_call_target="tpu_custom_call", output_to_operand_aliasing={{0}: (7, {}), {1}: (8, {}), {2}: (9, {}), {3}: (10, {})} | custom-call | flops 12884901888 | bytes 18874368 | tf_op jit(solution)/shard_map/attend/pallas_call | solution.py:215
  171.8 1.5 collective-permute-start.12
  173.4 3.1 other_kv.5
  176.4 33.1 %attend.6 = (bf16[8,512,768]{2,1,0:T(8,128)(2,1)}, bf16[8,512,768]{2,1,0:T(8,128)(2,1)}, bf16[8,512,768]{2,1,0:T(8,128)(2,1)}, bf16[8,512,768]{2,1,0:T(8,128)(2,...) custom-call(s32[1]{0:T(128)} %bitcast.1.role_ref, ...), custom_call_target="tpu_custom_call", output_to_operand_aliasing={{0}: (7, {}), {1}: (8, {}), {2}: (9, {}), {3}: (10, {})} | custom-call | flops 12884901888 | bytes 18874368 | tf_op jit(solution)/shard_map/attend/pallas_call | solution.py:215
  209.5 1.8 collective-permute-start.10
  211.3 3.1 other_kv.4
  215.0 1.1 copy-done.2
  216.1 20.7 %late.4 = (bf16[8,512,768]{2,1,0:T(8,128)(2,1)}, bf16[8,512,768]{2,1,0:T(8,128)(2,1)}) custom-call(s32[1]{0:T(128)} %bitcast.1.role_ref, bf16[2,2,512,768]{3,2,1,0:T(8,128)(2,1)} %copy-done.2, bf16[2,2,512,768]{3,2,1,0:T(8,128)(2,1)} %copy-done.2, f32[2,6,4,512]{3,2,1,0:T(4,128)} %copy-done.17, ...), custom_call_target="tpu_custom_call", output_to_operand_aliasing={{0}: (8, {}), {1}: (9, {})} | custom-call | flops 6442450944 | bytes 15728640 | tf_op jit(solution)/shard_map/late/pallas_call | solution.py:278
  236.7 33.1 %attend.7 = (bf16[8,512,768]{2,1,0:T(8,128)(2,1)}, bf16[8,512,768]{2,1,0:T(8,128)(2,1)}, bf16[8,512,768]{2,1,0:T(8,128)(2,1)}, bf16[8,512,768]{2,1,0:T(8,128)(2,...) custom-call(s32[1]{0:T(128)} %bitcast.1.role_ref, ...), custom_call_target="tpu_custom_call", output_to_operand_aliasing={{0}: (7, {}), {1}: (8, {}), {2}: (9, {}), {3}: (10, {})} | custom-call | flops 12884901888 | bytes 18874368 | tf_op jit(solution)/shard_map/attend/pallas_call | solution.py:215
  269.8 9.2 %convolution_bitcast_fusion.3 = f32[768,768]{1,0:T(8,128)S(1)} fusion(bf16[8,512,768]{2,1,0:T(8,128)(2,1)} %get-tuple-element.109.a_ref, bf16[8,512,768]{2,1,0:T(8,128)(2,1)} %get-tuple-element.124.g_ref), kind=kOutput, calls=%fused_computation.3 | convolution fusion | flops 4831838208 | bytes 14942208 | tf_op jit(solution)/shard_map/dot_general | solution.py:416
  279.0 1.2 constant_dynamic-slice_fusion.3
  280.8 7.3 %convolution_bitcast_fusion.2 = f32[768,768]{1,0:T(8,128)S(1)} fusion(bf16[8,512,768]{2,1,0:T(8,128)(2,1)S(1)} %copy-done.1, bf16[8,512,768]{2,1,0:T(8,128)(2,1)} %get-tuple-element.126), kind=kOutput, calls=%fused_computation.2 | convolution fusion | flops 4831838208 | bytes 14942208 | tf_op jit(solution)/shard_map/dot_general | solution.py:416
  288.2 1.4 copy-done.11
  289.6 1.1 constant_dynamic-slice_fusion.2
  290.7 1.4 collective-permute-start.15
  292.1 2.8 dynamic-slice_add_fusion.3.rest_0_
  294.9 1.3 collective-permute-start.13
  296.2 2.4 dynamic-slice_add_fusion.2.rest_1_
  298.6 44.9 %collective-permute-done.15.st_ref = f32[2,6,4,512]{3,2,1,0:T(4,128)S(1)} collective-permute-done((f32[2,6,4,512]{3,2,1,0:T(4,128)S(1)}, f32[2,6,4,512]{3,2,1,0:T(4,128)S(1)}, u32[]{:S(2)}, u32[]{:S(2)}) %collective-permute-start.15) | collective-permute-done | bytes 98336 | tf_op jit(solution)/shard_map/ppermute | solution.py:438
  343.6 1.3 collective-permute-start.11
  344.9 21.0 %late.5 = (bf16[8,512,768]{2,1,0:T(8,128)(2,1)}, bf16[8,512,768]{2,1,0:T(8,128)(2,1)}) custom-call(s32[1]{0:T(128)} %bitcast.1.role_ref, bf16[2,2,512,768]{3,2,1,0:T(8,128)(2,1)} %collective-permute-done.14.q_ref.g_ref, bf16[2,2,512,768]{3,2,1,0:T(8,128)(2,1)} %collective-permute-done.14.q_ref.g_ref, ...), custom_call_target="tpu_custom_call", output_to_operand_aliasing={{0}: (8, {}), {1}: (9, {})} | custom-call | flops 6442450944 | bytes 15728640 | tf_op jit(solution)/shard_map/late/pallas_call | solution.py:278
  366.5 1.1 copy-done.3
  367.6 20.7 %late.6 = (bf16[8,512,768]{2,1,0:T(8,128)(2,1)}, bf16[8,512,768]{2,1,0:T(8,128)(2,1)}) custom-call(s32[1]{0:T(128)} %bitcast.1.role_ref, bf16[2,2,512,768]{3,2,1,0:T(8,128)(2,1)} %copy-done.3, bf16[2,2,512,768]{3,2,1,0:T(8,128)(2,1)} %copy-done.3, f32[2,6,4,512]{3,2,1,0:T(4,128)} %copy-done.19, ...), custom_call_target="tpu_custom_call", output_to_operand_aliasing={{0}: (8, {}), {1}: (9, {})} | custom-call | flops 6442450944 | bytes 15728640 | tf_op jit(solution)/shard_map/late/pallas_call | solution.py:278
  389.0 20.7 %late.7 = (bf16[8,512,768]{2,1,0:T(8,128)(2,1)}, bf16[8,512,768]{2,1,0:T(8,128)(2,1)}) custom-call(s32[1]{0:T(128)} %bitcast.1.role_ref, bf16[2,2,512,768]{3,2,1,0:T(8,128)(2,1)} %collective-permute-done.10.q_ref.g_ref, bf16[2,2,512,768]{3,2,1,0:T(8,128)(2,1)} %collective-permute-done.10.q_ref.g_ref, ...), custom_call_target="tpu_custom_call", output_to_operand_aliasing={{0}: (8, {}), {1}: (9, {})} | custom-call | flops 6442450944 | bytes 15728640 | tf_op jit(solution)/shard_map/late/pallas_call | solution.py:278
  409.7 9.2 %convolution_bitcast_fusion = f32[768,768]{1,0:T(8,128)S(1)} fusion(bf16[8,512,768]{2,1,0:T(8,128)(2,1)} %get-tuple-element.130.dv_ref, bf16[8,512,768]{2,1,0:T(8,128)(2,1)} %get-tuple-element.126), kind=kOutput, calls=%fused_computation | convolution fusion | flops 4831838208 | bytes 14942208 | tf_op jit(solution)/shard_map/dot_general | solution.py:416
  419.1 7.4 %convolution_bitcast_fusion.1 = f32[768,768]{1,0:T(8,128)S(1)} fusion(bf16[8,512,768]{2,1,0:T(8,128)(2,1)S(1)} %copy-done, bf16[8,512,768]{2,1,0:T(8,128)(2,1)} %get-tuple-element.126), kind=kOutput, calls=%fused_computation.1 | convolution fusion | flops 4831838208 | bytes 14942208 | tf_op jit(solution)/shard_map/dot_general | solution.py:416
  427.7 2.0 collective-permute-start.24
  429.8 1.1 dynamic-slice_add_fusion.rest_1_
  430.9 1.2 dynamic-slice_add_fusion.1.rest_0_
  432.1 30.1 %back.1 = (bf16[16,256,768]{2,1,0:T(8,128)(2,1)}, bf16[8,256,768]{2,1,0:T(8,128)(2,1)}, f32[8,768]{1,0:T(8,128)}) custom-call(s32[1]{0:T(128)} %bitcast.core_ref, bf16[8,512,768]{2,1,0:T(8,128)(2,1)} %get-tuple-element.125.dq_ref, bf16[8,512,768]{2,1,0:T(8,128)(2,1)} %get-tuple-element.129.dk_ref, bf16[8,512,768]{2,1,0:T(8,128)(2,1)} %get-tuple-element.130.dv_ref, ...), custom_call_target="tpu_custom_call" | custom-call | flops 14495514624 | bytes 37748736 | tf_op jit(solution)/shard_map/back/pallas_call | solution.py:361
  462.2 12.5 %post.1 = (bf16[16,256,768]{2,1,0:T(8,128)(2,1)}, bf16[8,256,768]{2,1,0:T(8,128)(2,1)}) custom-call(s32[1]{0:T(128)} %bitcast.core_ref, bf16[8,512,768]{2,1,0:T(8,128)(2,1)} %get-tuple-element.109.a_ref, bf16[8,512,768]{2,1,0:T(8,128)(2,1)} %get-tuple-element.110.x_ref, bf16[768,768]{1,0:T(8,128)(2,1)} %bitcast.39, f32[1,768]{1,0:T(1,128)} %reshape.50.bo_ref, ...), custom_call_target="tpu_custom_call" | custom-call | flops 4831838208 | bytes 18874368 | tf_op jit(solution)/shard_map/post/pallas_call | solution.py:318
  475.3 6.5 %collective-permute-done.24 = f32[384,768]{1,0:T(8,128)S(1)} collective-permute-done((f32[384,768]{1,0:T(8,128)S(1)}, f32[384,768]{1,0:T(8,128)S(1)}, u32[]{:S(2)}, u32[]{:S(2)}) %collective-permute-start.24) | collective-permute-done | bytes 1179680 | tf_op jit(solution)/shard_map/ppermute | solution.py:438
  482.1 25.1 %collective-permute-done.26 = f32[384,768]{1,0:T(8,128)S(1)} collective-permute-done((f32[384,768]{1,0:T(8,128)S(1)}, f32[384,768]{1,0:T(8,128)S(1)}, u32[]{:S(2)}, u32[]{:S(2)}) %collective-permute-start.26) | collective-permute-done | bytes 1179680 | tf_op jit(solution)/shard_map/ppermute | solution.py:438
  507.5 24.3 %collective-permute-done.25 = f32[384,768]{1,0:T(8,128)S(1)} collective-permute-done((f32[384,768]{1,0:T(8,128)S(1)}, f32[384,768]{1,0:T(8,128)S(1)}, u32[]{:S(2)}, u32[]{:S(2)}) %collective-permute-start.25) | collective-permute-done | bytes 1179680 | tf_op jit(solution)/shard_map/ppermute | solution.py:438
  531.8 1.2 add.70.refs_1_
  533.5 1.0 copy-done.14
  535.1 0.7 reshape.51
  535.8 1.5 slice_reduce_fusion
  537.3 0.7 collective-permute-done.29.refs_5_
  538.0 1.0 copy-done.15
  539.0 8.9 %join.1 = (f32[3,2,384,768]{3,2,1,0:T(8,128)}, f32[2,384,768]{2,1,0:T(8,128)}) custom-call(s32[1]{0:T(128)} %bitcast.core_ref, f32[384,768]{1,0:T(8,128)} %copy-done.7, f32[384,768]{1,0:T(8,128)} %add.70.refs_1_, f32[384,768]{1,0:T(8,128)} %copy-done.8, f32[384,768]{1,0:T(8,128)} %copy-done.6, f32[384,768]{1,0:T(8,128)} %collective-permute-done.28.refs_4_, ...), custom_call_target="tpu_custom_call" | custom-call | flops 2359296 | bytes 18874368 | tf_op jit(solution)/shard_map/join/pallas_call | solution.py:396
  547.9 3.8 constant_dynamic-update-slice_fusion
  551.7 3.8 constant_dynamic-update-slice_fusion.1
  (110 shorter events, 7.9 us)
Async XLA Ops:
  2.5 8.8 %copy-start.22 = (f32[3,12,64]{2,1,0:T(8,128)S(1)}, f32[3,12,64]{2,1,0:T(8,128)}, u32[]{:S(2)}) copy-start(f32[3,12,64]{2,1,0:T(8,128)} %param.13) | copy-start | bytes 27652
  2.5 9.4 %copy-start.24 = (f32[768]{0:T(1024)S(1)}, f32[768]{0:T(1024)}, u32[]{:S(2)}) copy-start(f32[768]{0:T(1024)} %param.10) | copy-start | bytes 9220
  2.5 10.0 %copy-start.25 = (f32[768]{0:T(1024)S(1)}, f32[768]{0:T(1024)}, u32[]{:S(2)}) copy-start(f32[768]{0:T(1024)} %param.11) | copy-start | bytes 9220
  2.5 29.9 %collective-permute-start = (bf16[6,256,768]{2,1,0:T(8,128)(2,1)S(1)}, bf16[6,256,768]{2,1,0:T(8,128)(2,1)}, u32[]{:S(2)}, u32[]{:S(2)}) collective-permute-start(bf16[6,256,768]{2,1,0:T(8,128)(2,1)S(1)} %constant_dynamic-slice_fusion.7), channel_id=1, source_target_pairs={{0,1},{1,0},{2,3},{3,2},{4,5},{5,4},{6,7},{7,6}} | collective-permute-start | bytes 7077896 | tf_op jit(solution)/shard_map/ppermute | solution.py:438
  6.6 25.8 %collective-permute-start.1 = (bf16[6,256,768]{2,1,0:T(8,128)(2,1)}, bf16[6,256,768]{2,1,0:T(8,128)(2,1)}, u32[]{:S(2)}, u32[]{:S(2)}) collective-permute-start(bf16[6,256,768]{2,1,0:T(8,128)(2,1)} %constant_dynamic-slice_fusion.6), channel_id=1, source_target_pairs={{0,1},{1,0},{2,3},{3,2},{4,5},{5,4},{6,7},{7,6}} | collective-permute-start | bytes 7077896 | tf_op jit(solution)/shard_map/ppermute | solution.py:438
  8.7 4.4 collective-permute-start.2
  11.2 2.6 collective-permute-start.3
  13.1 0.9 copy-start.16
  25.0 41.2 %collective-permute-start.7 = (bf16[2,512,768]{2,1,0:T(8,128)(2,1)}, bf16[2,512,768]{2,1,0:T(8,128)(2,1)}, u32[]{:S(2)}, u32[]{:S(2)}) collective-permute-start(bf16[2,512,768]{2,1,0:T(8,128)(2,1)} %get-tuple-element.89), channel_id=1, source_target_pairs={{0,2},{1,3},{4,6},{5,7}} | collective-permute-start | bytes 4718600 | tf_op jit(solution)/shard_map/ppermute | solution.py:438
  31.1 183.2 %collective-permute-start.8 = (bf16[2,2,512,768]{3,2,1,0:T(8,128)(2,1)}, bf16[2,2,512,768]{3,2,1,0:T(8,128)(2,1)S(1)}, u32[]{:S(2)}, u32[]{:S(2)}) collective-permute-start(bf16[2,2,512,768]{3,2,1,0:T(8,128)(2,1)} %get-tuple-element.86.refs_0_.refs_1_), channel_id=1, source_target_pairs={{2,0},{3,1},{6,4},{7,5}} | collective-permute-start | bytes 9437192 | tf_op jit(solution)/shard_map/ppermute | solution.py:438
  57.5 76.6 %collective-permute-start.6 = (bf16[2,512,768]{2,1,0:T(8,128)(2,1)S(1)}, bf16[2,512,768]{2,1,0:T(8,128)(2,1)}, u32[]{:S(2)}, u32[]{:S(2)}) collective-permute-start(bf16[2,512,768]{2,1,0:T(8,128)(2,1)S(1)} %get-tuple-element.144), channel_id=1, source_target_pairs={{0,2},{1,3},{4,6},{5,7}} | collective-permute-start | bytes 4718600 | tf_op jit(solution)/shard_map/ppermute | solution.py:438
  63.5 108.3 %collective-permute-start.5 = (bf16[2,512,768]{2,1,0:T(8,128)(2,1)S(1)}, bf16[2,512,768]{2,1,0:T(8,128)(2,1)}, u32[]{:S(2)}, u32[]{:S(2)}) collective-permute-start(bf16[2,512,768]{2,1,0:T(8,128)(2,1)S(1)} %get-tuple-element.145), channel_id=1, source_target_pairs={{0,2},{1,3},{4,6},{5,7}} | collective-permute-start | bytes 4718600 | tf_op jit(solution)/shard_map/ppermute | solution.py:438
  102.2 112.1 %collective-permute-start.9 = (f32[2,6,4,512]{3,2,1,0:T(4,128)}, f32[2,6,4,512]{3,2,1,0:T(4,128)S(1)}, u32[]{:S(2)}, u32[]{:S(2)}) collective-permute-start(f32[2,6,4,512]{3,2,1,0:T(4,128)} %get-tuple-element.102), channel_id=1, source_target_pairs={{2,0},{3,1},{6,4},{7,5}} | collective-permute-start | bytes 294920 | tf_op jit(solution)/shard_map/ppermute | solution.py:438
  103.5 106.0 %collective-permute-start.4 = (bf16[2,512,768]{2,1,0:T(8,128)(2,1)S(1)}, bf16[2,512,768]{2,1,0:T(8,128)(2,1)}, u32[]{:S(2)}, u32[]{:S(2)}) collective-permute-start(bf16[2,512,768]{2,1,0:T(8,128)(2,1)S(1)} %get-tuple-element.146), channel_id=1, source_target_pairs={{0,2},{1,3},{4,6},{5,7}} | collective-permute-start | bytes 4718600 | tf_op jit(solution)/shard_map/ppermute | solution.py:438
  134.1 210.8 %collective-permute-start.14 = (bf16[2,2,512,768]{3,2,1,0:T(8,128)(2,1)}, bf16[2,2,512,768]{3,2,1,0:T(8,128)(2,1)}, u32[]{:S(2)}, u32[]{:S(2)}) collective-permute-start(bf16[2,2,512,768]{3,2,1,0:T(8,128)(2,1)} %get-tuple-element.141), channel_id=1, source_target_pairs={{2,0},{3,1},{6,4},{7,5}} | collective-permute-start | bytes 9437192 | tf_op jit(solution)/shard_map/ppermute | solution.py:438
  171.8 194.1 %collective-permute-start.12 = (bf16[2,2,512,768]{3,2,1,0:T(8,128)(2,1)}, bf16[2,2,512,768]{3,2,1,0:T(8,128)(2,1)S(1)}, u32[]{:S(2)}, u32[]{:S(2)}) collective-permute-start(bf16[2,2,512,768]{3,2,1,0:T(8,128)(2,1)} %get-tuple-element.142), channel_id=1, source_target_pairs={{2,0},{3,1},{6,4},{7,5}} | collective-permute-start | bytes 9437192 | tf_op jit(solution)/shard_map/ppermute | solution.py:438
  209.5 178.9 %collective-permute-start.10 = (bf16[2,2,512,768]{3,2,1,0:T(8,128)(2,1)}, bf16[2,2,512,768]{3,2,1,0:T(8,128)(2,1)}, u32[]{:S(2)}, u32[]{:S(2)}) collective-permute-start(bf16[2,2,512,768]{3,2,1,0:T(8,128)(2,1)} %get-tuple-element.143), channel_id=1, source_target_pairs={{2,0},{3,1},{6,4},{7,5}} | collective-permute-start | bytes 9437192 | tf_op jit(solution)/shard_map/ppermute | solution.py:438
  214.3 0.6 copy-start.17
  214.3 1.7 copy-start.2
  269.8 11.0 %copy-start.1 = (bf16[8,512,768]{2,1,0:T(8,128)(2,1)S(1)}, bf16[8,512,768]{2,1,0:T(8,128)(2,1)}, u32[]{:S(2)}) copy-start(bf16[8,512,768]{2,1,0:T(8,128)(2,1)} %get-tuple-element.125.dq_ref) | copy-start | bytes 18874372
  279.0 1.8 copy-start.13
  280.2 10.4 %collective-permute-start.16 = (f32[384,768]{1,0:T(8,128)}, f32[384,768]{1,0:T(8,128)}, u32[]{:S(2)}, u32[]{:S(2)}) collective-permute-start(f32[384,768]{1,0:T(8,128)} %constant_dynamic-slice_fusion.3), channel_id=1, source_target_pairs={{0,1},{1,0},{2,3},{3,2},{4,5},{5,4},{6,7},{7,6}} | collective-permute-start | bytes 3538952 | tf_op jit(solution)/shard_map/ppermute | solution.py:438
  280.8 9.8 %copy-start.27 = (f32[2,6,4,512]{3,2,1,0:T(4,128)S(1)}, f32[2,6,4,512]{3,2,1,0:T(4,128)}, u32[]{:S(2)}) copy-start(f32[2,6,4,512]{3,2,1,0:T(4,128)} %get-tuple-element.117) | copy-start | bytes 294916
  288.2 1.4 copy-start.11
  289.6 5.3 copy-start.28
  290.7 4.2 collective-permute-start.17
  290.7 5.5 copy-start.12
  290.7 52.9 %copy-start.29 = (f32[2,6,4,512]{3,2,1,0:T(4,128)S(1)}, f32[2,6,4,512]{3,2,1,0:T(4,128)}, u32[]{:S(2)}) copy-start(f32[2,6,4,512]{3,2,1,0:T(4,128)} %get-tuple-element.111) | copy-start | bytes 294916
  290.7 52.9 %collective-permute-start.15 = (f32[2,6,4,512]{3,2,1,0:T(4,128)S(1)}, f32[2,6,4,512]{3,2,1,0:T(4,128)S(1)}, u32[]{:S(2)}, u32[]{:S(2)}) collective-permute-start(f32[2,6,4,512]{3,2,1,0:T(4,128)S(1)} %copy-done.27), channel_id=1, source_target_pairs={{2,0},{3,1},{6,4},{7,5}} | collective-permute-start | bytes 294920 | tf_op jit(solution)/shard_map/ppermute | solution.py:438
  294.9 71.0 %collective-permute-start.13 = (f32[2,6,4,512]{3,2,1,0:T(4,128)S(1)}, f32[2,6,4,512]{3,2,1,0:T(4,128)S(1)}, u32[]{:S(2)}, u32[]{:S(2)}) collective-permute-start(f32[2,6,4,512]{3,2,1,0:T(4,128)S(1)} %copy-done.28), channel_id=1, source_target_pairs={{2,0},{3,1},{6,4},{7,5}} | collective-permute-start | bytes 294920 | tf_op jit(solution)/shard_map/ppermute | solution.py:438
  343.6 1.3 copy-start.20
  343.6 44.7 %collective-permute-start.11 = (f32[2,6,4,512]{3,2,1,0:T(4,128)S(1)}, f32[2,6,4,512]{3,2,1,0:T(4,128)S(1)}, u32[]{:S(2)}, u32[]{:S(2)}) collective-permute-start(f32[2,6,4,512]{3,2,1,0:T(4,128)S(1)} %copy-done.29), channel_id=1, source_target_pairs={{2,0},{3,1},{6,4},{7,5}} | collective-permute-start | bytes 294920 | tf_op jit(solution)/shard_map/ppermute | solution.py:438
  365.9 0.6 copy-start.19
  365.9 1.7 copy-start.3
  388.4 0.6 copy-start.18
  409.7 9.3 %copy-start = (bf16[8,512,768]{2,1,0:T(8,128)(2,1)S(1)}, bf16[8,512,768]{2,1,0:T(8,128)(2,1)}, u32[]{:S(2)}) copy-start(bf16[8,512,768]{2,1,0:T(8,128)(2,1)} %get-tuple-element.129.dk_ref) | copy-start | bytes 18874372
  419.0 10.7 %collective-permute-start.19 = (f32[384,768]{1,0:T(8,128)S(1)}, f32[384,768]{1,0:T(8,128)S(1)}, u32[]{:S(2)}, u32[]{:S(2)}) collective-permute-start(f32[384,768]{1,0:T(8,128)S(1)} %constant_dynamic-slice_fusion), channel_id=1, source_target_pairs={{0,1},{1,0},{2,3},{3,2},{4,5},{5,4},{6,7},{7,6}} | collective-permute-start | bytes 3538952 | tf_op jit(solution)/shard_map/ppermute | solution.py:438
  419.1 8.1 %copy-start.26 = (f32[768]{0:T(1024)S(1)}, f32[768]{0:T(1024)}, u32[]{:S(2)}) copy-start(f32[768]{0:T(1024)} %param.15) | copy-start | bytes 9220
  419.1 8.6 %copy-start.5 = (f32[384,768]{1,0:T(8,128)S(1)}, f32[384,768]{1,0:T(8,128)}, u32[]{:S(2)}) copy-start(f32[384,768]{1,0:T(8,128)} %dynamic-slice_add_fusion.3.rest_0_) | copy-start | bytes 3538948
  419.1 8.6 %copy-start.4 = (f32[384,768]{1,0:T(8,128)S(1)}, f32[384,768]{1,0:T(8,128)}, u32[]{:S(2)}) copy-start(f32[384,768]{1,0:T(8,128)} %dynamic-slice_add_fusion.2.rest_1_) | copy-start | bytes 3538948
  426.7 4.2 collective-permute-start.18
  427.7 47.4 %collective-permute-start.27 = (f32[384,768]{1,0:T(8,128)S(1)}, f32[384,768]{1,0:T(8,128)S(1)}, u32[]{:S(2)}, u32[]{:S(2)}) collective-permute-start(f32[384,768]{1,0:T(8,128)S(1)} %copy-done.5), channel_id=1, source_target_pairs={{0,2},{1,3},{2,0},{3,1},{4,6},{5,7},{6,4},{7,5}} | collective-permute-start | bytes 3538952 | tf_op jit(solution)/shard_map/ppermute | solution.py:438
  427.7 54.1 %collective-permute-start.24 = (f32[384,768]{1,0:T(8,128)S(1)}, f32[384,768]{1,0:T(8,128)S(1)}, u32[]{:S(2)}, u32[]{:S(2)}) collective-permute-start(f32[384,768]{1,0:T(8,128)S(1)} %copy-done.4), channel_id=1, source_target_pairs={{0,2},{1,3},{2,0},{3,1},{4,6},{5,7},{6,4},{7,5}} | collective-permute-start | bytes 3538952 | tf_op jit(solution)/shard_map/ppermute | solution.py:438
  462.2 12.9 %copy-start.10 = (f32[384,768]{1,0:T(8,128)S(1)}, f32[384,768]{1,0:T(8,128)}, u32[]{:S(2)}) copy-start(f32[384,768]{1,0:T(8,128)} %dynamic-slice_add_fusion.rest_1_) | copy-start | bytes 3538948
  462.2 12.9 %copy-start.23 = (f32[8,768]{1,0:T(8,128)S(1)}, f32[8,768]{1,0:T(8,128)}, u32[]{:S(2)}) copy-start(f32[8,768]{1,0:T(8,128)} %get-tuple-element.135) | copy-start | bytes 73732
  462.2 19.7 %copy-start.9 = (f32[384,768]{1,0:T(8,128)S(1)}, f32[384,768]{1,0:T(8,128)}, u32[]{:S(2)}) copy-start(f32[384,768]{1,0:T(8,128)} %dynamic-slice_add_fusion.1.rest_0_) | copy-start | bytes 3538948
  462.2 85.7 %collective-permute-start.21 = (bf16[8,256,768]{2,1,0:T(8,128)(2,1)}, bf16[8,256,768]{2,1,0:T(8,128)(2,1)}, u32[]{:S(2)}, u32[]{:S(2)}) collective-permute-start(bf16[8,256,768]{2,1,0:T(8,128)(2,1)} %get-tuple-element.134), channel_id=1, source_target_pairs={{0,1},{1,0},{2,3},{3,2},{4,5},{5,4},{6,7},{7,6}} | collective-permute-start | bytes 9437192 | tf_op jit(solution)/shard_map/ppermute | solution.py:438
  474.7 76.9 %collective-permute-start.20 = (bf16[8,256,768]{2,1,0:T(8,128)(2,1)}, bf16[8,256,768]{2,1,0:T(8,128)(2,1)}, u32[]{:S(2)}, u32[]{:S(2)}) collective-permute-start(bf16[8,256,768]{2,1,0:T(8,128)(2,1)} %get-tuple-element.132), channel_id=1, source_target_pairs={{0,1},{1,0},{2,3},{3,2},{4,5},{5,4},{6,7},{7,6}} | collective-permute-start | bytes 9437192 | tf_op jit(solution)/shard_map/ppermute | solution.py:438
  475.1 32.1 %collective-permute-start.26 = (f32[384,768]{1,0:T(8,128)S(1)}, f32[384,768]{1,0:T(8,128)S(1)}, u32[]{:S(2)}, u32[]{:S(2)}) collective-permute-start(f32[384,768]{1,0:T(8,128)S(1)} %copy-done.10), channel_id=1, source_target_pairs={{0,2},{1,3},{2,0},{3,1},{4,6},{5,7},{6,4},{7,5}} | collective-permute-start | bytes 3538952 | tf_op jit(solution)/shard_map/ppermute | solution.py:438
  475.1 6.9 %collective-permute-start.22 = (f32[8,768]{1,0:T(8,128)S(1)}, f32[8,768]{1,0:T(8,128)S(1)}, u32[]{:S(2)}, u32[]{:S(2)}) collective-permute-start(f32[8,768]{1,0:T(8,128)S(1)} %copy-done.23), channel_id=1, source_target_pairs={{0,1},{1,0},{2,3},{3,2},{4,5},{5,4},{6,7},{7,6}} | collective-permute-start | bytes 73736 | tf_op jit(solution)/shard_map/ppermute | solution.py:438
  481.8 49.9 %collective-permute-start.25 = (f32[384,768]{1,0:T(8,128)S(1)}, f32[384,768]{1,0:T(8,128)S(1)}, u32[]{:S(2)}, u32[]{:S(2)}) collective-permute-start(f32[384,768]{1,0:T(8,128)S(1)} %copy-done.9), channel_id=1, source_target_pairs={{0,2},{1,3},{2,0},{3,1},{4,6},{5,7},{6,4},{7,5}} | collective-permute-start | bytes 3538952 | tf_op jit(solution)/shard_map/ppermute | solution.py:438
  482.0 25.4 %copy-start.6 = (f32[384,768]{1,0:T(8,128)}, f32[384,768]{1,0:T(8,128)S(1)}, u32[]{:S(2)}) copy-start(f32[384,768]{1,0:T(8,128)S(1)} %add.72.refs_3_) | copy-start | bytes 3538948
  482.0 51.5 %collective-permute-start.31 = (f32[384,768]{1,0:T(8,128)S(1)}, f32[384,768]{1,0:T(8,128)S(1)}, u32[]{:S(2)}, u32[]{:S(2)}) collective-permute-start(f32[384,768]{1,0:T(8,128)S(1)} %add.72.refs_3_), channel_id=1, source_target_pairs={{0,1},{1,0},{2,3},{3,2},{4,5},{5,4},{6,7},{7,6}} | collective-permute-start | bytes 3538952 | tf_op jit(solution)/shard_map/ppermute | solution.py:438
  507.1 25.8 %collective-permute-start.23 = (f32[8,768]{1,0:T(8,128)S(1)}, f32[8,768]{1,0:T(8,128)S(1)}, u32[]{:S(2)}, u32[]{:S(2)}) collective-permute-start(f32[8,768]{1,0:T(8,128)S(1)} %add.67), channel_id=1, source_target_pairs={{0,2},{1,3},{2,0},{3,1},{4,6},{5,7},{6,4},{7,5}} | collective-permute-start | bytes 73736 | tf_op jit(solution)/shard_map/ppermute | solution.py:438
  507.3 25.7 %copy-start.7 = (f32[384,768]{1,0:T(8,128)}, f32[384,768]{1,0:T(8,128)S(1)}, u32[]{:S(2)}) copy-start(f32[384,768]{1,0:T(8,128)S(1)} %add.69.refs_0_) | copy-start | bytes 3538948
  507.5 30.5 %copy-start.8 = (f32[384,768]{1,0:T(8,128)}, f32[384,768]{1,0:T(8,128)S(1)}, u32[]{:S(2)}) copy-start(f32[384,768]{1,0:T(8,128)S(1)} %add.71.refs_2_) | copy-start | bytes 3538948
  531.7 5.6 %collective-permute-start.28 = (f32[384,768]{1,0:T(8,128)S(1)}, f32[384,768]{1,0:T(8,128)}, u32[]{:S(2)}, u32[]{:S(2)}) collective-permute-start(f32[384,768]{1,0:T(8,128)S(1)} %add.69.refs_0_), channel_id=1, source_target_pairs={{0,1},{1,0},{2,3},{3,2},{4,5},{5,4},{6,7},{7,6}} | collective-permute-start | bytes 3538952 | tf_op jit(solution)/shard_map/ppermute | solution.py:438
  533.0 4.4 collective-permute-start.30
  533.5 1.0 copy-start.14
  534.5 3.5 collective-permute-start.29
  534.5 0.6 copy-start.21
  538.0 1.0 copy-start.15

commit v5 on v4

--- a/solution.py
+++ b/solution.py
@@ -477,14 +477,16 @@
         chain = forward(2, chain)
         chain = backward(0, chain, [])
         chain = forward(3, chain)
-        chain = backward(1, chain, [])
-        dw_o, dw_q = tok_dot(chain[0], gb), tok_dot(chain[1], h)
-        part_o, part_q = halves_added(dw_o), halves_added(dw_q)
-        chain = backward(2, chain, [part_o, part_q])
+
+        dw_o = tok_dot(chain[0], gb)
+        part_o = halves_added(dw_o)
+        chain = backward(1, chain, [dw_o])
+        chain = backward(2, chain, [])
+        chain = backward(3, chain, [part_o])
+        a, dq, dk, dv = chain
         sum_o = part_o + send(part_o, SWAP_CHIP)
+        part_q = halves_added(tok_dot(dq, h))
         sum_q = part_q + send(part_q, SWAP_CHIP)
-        chain = backward(3, chain, [])
-        a, dq, dk, dv = chain
         part_k, part_v = halves_added(tok_dot(dk, h)), halves_added(tok_dot(dv, h))
         sum_k = part_k + send(part_k, SWAP_CHIP)
         sum_v = part_v + send(part_v, SWAP_CHIP)
@@ -492,7 +494,8 @@
         *d_x, acc = back(side, dq, dk, dv, xb, gb, ln_g2, w_t, [part_k, part_v])
 
         def joined(own_rows, other_rows):
-            return lax.dynamic_update_slice_in_dim(own_rows, send(other_rows, SWAP_CORE), (1 - core) * half_b, 0)
+            other_rows = send(other_rows, SWAP_CORE)
+            return lax.dynamic_update_slice_in_dim(own_rows, other_rows, (1 - core) * half_b, 0)
 
         y, d_x = joined(*y), joined(*d_x)
         acc = acc + send(acc, SWAP_CORE)

time: 562 us -> 560 us (level)
  transfers between devices with their start and end apart: 32 -> 32, of which waited for: 6 -> 7; matrix products, arithmetic and copies ran while one was open for 11% -> 12% of each run, Pallas kernels for 53% -> 56%
where the time goes in v5:
time: 560 us; the launch traced here: 554 us
  Pallas kernels  312 us (56%)
  waiting for transfers between devices  107 us (19%)
  starting transfers between devices  54.4 us (10%)
  local copies, waits for them, and re-layouts  41.3 us (7%)
  matrix products  31.2 us (6%)
  other arithmetic  6.57 us (1%)
    pallas_call x4, Pallas kernels, attend(): pl.pallas_call(functools.partial(attn_kernel, head=head, scale=head ** (-...  132 us
    ppermute x32, waiting for transfers between devices, send(): return lax.ppermute(z, 'sp', perm)  107 us
    pallas_call x4, Pallas kernels, late(): pl.pallas_call(functools.partial(late_kernel, head=head, scale=head ** (-...  83.1 us
    ppermute x32, starting transfers between devices, send(): return lax.ppermute(z, 'sp', perm)  54.4 us
    pallas_call x2, Pallas kernels, front(): pl.pallas_call(front_kernel, grid_spec=pltpu.PrefetchScalarGridSpec(num_s...  33.5 us
    dot_general x4, matrix products, tok_dot(): lax.dot_general(a, b, (((0, 1), (0, 1)), ((), ())), preferred_element_typ...  31.2 us
    pallas_call x1, Pallas kernels, back(): pl.pallas_call(back_kernel, grid_spec=pltpu.PrefetchScalarGridSpec(num_sc...  30.3 us
    pallas_call x1, Pallas kernels, post(): pl.pallas_call(post_kernel, grid_spec=pltpu.PrefetchScalarGridSpec(num_sc...  12.3 us
  transfers between devices with their start and end apart: 32, of which 7 were waited for; matrix products, arithmetic and copies ran while one was open for 12% of the time, Pallas kernels for 56%

profile of v5, /device:TPU:0, one launch (start us, length us, event | category | flops | bytes accessed | tf_op | source)
XLA Modules:
  0.0 554.2 jit_solution(15535042978626870842)
XLA Ops:
  0.6 1.8 constant_dynamic-slice_fusion.7
  2.5 0.9 collective-permute-start
  3.4 3.2 constant_dynamic-slice_fusion.6
  6.6 2.1 constant_dynamic-slice_fusion.5
  9.2 2.1 constant_dynamic-slice_fusion.4
  11.2 0.7 reshape.48.b_ref
  13.1 0.8 collective-permute-done.3.gr_ref
  14.0 11.0 %front.2 = (bf16[2,512,768]{2,1,0:T(8,128)(2,1)}, bf16[2,2,512,768]{3,2,1,0:T(8,128)(2,1)}, bf16[2,512,768]{2,1,0:T(8,128)(2,1)}, bf16[2,512,768]{2,1,0:T(8,128)...) custom-call(s32[1]{0:T(128)} %bitcast.core_ref, ...), custom_call_target="tpu_custom_call" | custom-call | flops 4831838208 | bytes 14155776 | tf_op jit(solution)/shard_map/front/pallas_call | solution.py:77
  25.0 6.1 %collective-permute-start.7 = (bf16[2,512,768]{2,1,0:T(8,128)(2,1)}, bf16[2,512,768]{2,1,0:T(8,128)(2,1)}, u32[]{:S(2)}, u32[]{:S(2)}) collective-permute-start(bf16[2,512,768]{2,1,0:T(8,128)(2,1)} %get-tuple-element.89), channel_id=1, source_target_pairs={{0,2},{1,3},{4,6},{5,7}} | collective-permute-start | bytes 4718600 | tf_op jit(solution)/shard_map/ppermute | solution.py:438
  31.1 1.3 collective-permute-start.8
  32.4 22.4 %front.3 = (bf16[6,512,768]{2,1,0:T(8,128)(2,1)}, bf16[2,6,512,768]{3,2,1,0:T(8,128)(2,1)}, bf16[6,512,768]{2,1,0:T(8,128)(2,1)}, bf16[6,512,768]{2,1,0:T(8,128)...) custom-call(s32[1]{0:T(128)} %bitcast.core_ref, ...), custom_call_target="tpu_custom_call", output_to_operand_aliasing={{4}: (10, {}), {5}: (11, {}), {6}: (12, {})} | custom-call | flops 14495514624 | bytes 42467328 | tf_op jit(solution)/shard_map/front/pallas_call | solution.py:77
  54.8 3.8 fusion.1
  58.6 4.8 collective-permute-start.6
  63.5 2.6 collective-permute-start.5
  66.1 3.0 other_kv.7
  69.2 32.9 %attend.4 = (bf16[8,512,768]{2,1,0:T(8,128)(2,1)}, bf16[8,512,768]{2,1,0:T(8,128)(2,1)}, bf16[8,512,768]{2,1,0:T(8,128)(2,1)}, bf16[8,512,768]{2,1,0:T(8,128)(2,...) custom-call(s32[1]{0:T(128)} %bitcast.1.role_ref, ...), custom_call_target="tpu_custom_call" | custom-call | flops 12884901888 | bytes 18874368 | tf_op jit(solution)/shard_map/attend/pallas_call | solution.py:215
  102.1 1.3 collective-permute-start.9
  103.4 23.9 %collective-permute-start.4 = (bf16[2,512,768]{2,1,0:T(8,128)(2,1)S(1)}, bf16[2,512,768]{2,1,0:T(8,128)(2,1)}, u32[]{:S(2)}, u32[]{:S(2)}) collective-permute-start(bf16[2,512,768]{2,1,0:T(8,128)(2,1)S(1)} %get-tuple-element.146), channel_id=1, source_target_pairs={{0,2},{1,3},{4,6},{5,7}} | collective-permute-start | bytes 4718600 | tf_op jit(solution)/shard_map/ppermute | solution.py:438
  127.3 6.8 %fusion = (bf16[2,2,512,768]{3,2,1,0:T(8,128)(2,1)}, bf16[2,2,512,768]{3,2,1,0:T(8,128)(2,1)}, bf16[2,2,512,768]{3,2,1,0:T(8,128)(2,1)}) fusion(bf16[2,6,512,768]{3,2,1,0:T(8,128)(2,1)} %get-tuple-element.76.refs_0_.refs_1_), kind=kLoop, calls=%fused_computation.21 | loop fusion | bytes 18874368 | tf_op jit(solution)/shard_map/slice | solution.py:454
  134.1 1.1 copy-done.26
  135.2 1.5 collective-permute-start.14
  136.7 3.0 other_kv.6
  139.8 33.2 %attend.5 = (bf16[8,512,768]{2,1,0:T(8,128)(2,1)}, bf16[8,512,768]{2,1,0:T(8,128)(2,1)}, bf16[8,512,768]{2,1,0:T(8,128)(2,1)}, bf16[8,512,768]{2,1,0:T(8,128)(2,...) custom-call(s32[1]{0:T(128)} %bitcast.1.role_ref, ...), custom_call_target="tpu_custom_call", output_to_operand_aliasing={{0}: (7, {}), {1}: (8, {}), {2}: (9, {}), {3}: (10, {})} | custom-call | flops 12884901888 | bytes 18874368 | tf_op jit(solution)/shard_map/attend/pallas_call | solution.py:215
  173.0 1.5 collective-permute-start.12
  174.5 3.1 other_kv.5
  177.6 33.0 %attend.6 = (bf16[8,512,768]{2,1,0:T(8,128)(2,1)}, bf16[8,512,768]{2,1,0:T(8,128)(2,1)}, bf16[8,512,768]{2,1,0:T(8,128)(2,1)}, bf16[8,512,768]{2,1,0:T(8,128)(2,...) custom-call(s32[1]{0:T(128)} %bitcast.1.role_ref, ...), custom_call_target="tpu_custom_call", output_to_operand_aliasing={{0}: (7, {}), {1}: (8, {}), {2}: (9, {}), {3}: (10, {})} | custom-call | flops 12884901888 | bytes 18874368 | tf_op jit(solution)/shard_map/attend/pallas_call | solution.py:215
  210.7 1.8 collective-permute-start.10
  212.4 3.1 other_kv.4
  216.1 1.0 copy-done.2
  217.2 20.7 %late.4 = (bf16[8,512,768]{2,1,0:T(8,128)(2,1)}, bf16[8,512,768]{2,1,0:T(8,128)(2,1)}) custom-call(s32[1]{0:T(128)} %bitcast.1.role_ref, bf16[2,2,512,768]{3,2,1,0:T(8,128)(2,1)} %copy-done.2, bf16[2,2,512,768]{3,2,1,0:T(8,128)(2,1)} %copy-done.2, f32[2,6,4,512]{3,2,1,0:T(4,128)} %copy-done.16, ...), custom_call_target="tpu_custom_call", output_to_operand_aliasing={{0}: (8, {}), {1}: (9, {})} | custom-call | flops 6442450944 | bytes 15728640 | tf_op jit(solution)/shard_map/late/pallas_call | solution.py:278
  237.8 33.0 %attend.7 = (bf16[8,512,768]{2,1,0:T(8,128)(2,1)}, bf16[8,512,768]{2,1,0:T(8,128)(2,1)}, bf16[8,512,768]{2,1,0:T(8,128)(2,1)}, bf16[8,512,768]{2,1,0:T(8,128)(2,...) custom-call(s32[1]{0:T(128)} %bitcast.1.role_ref, ...), custom_call_target="tpu_custom_call", output_to_operand_aliasing={{0}: (7, {}), {1}: (8, {}), {2}: (9, {}), {3}: (10, {})} | custom-call | flops 12884901888 | bytes 18874368 | tf_op jit(solution)/shard_map/attend/pallas_call | solution.py:215
  270.8 9.2 %convolution_bitcast_fusion.3.rest_0_ = f32[768,768]{1,0:T(8,128)S(1)} fusion(bf16[8,512,768]{2,1,0:T(8,128)(2,1)} %get-tuple-element.109.a_ref, bf16[8,512,768]{2,1,0:T(8,128)(2,1)} %get-tuple-element.122.g_ref), kind=kOutput, calls=%fused_computation.3 | convolution fusion | flops 4831838208 | bytes 14942208 | tf_op jit(solution)/shard_map/dot_general | solution.py:416
  280.2 1.5 collective-permute-start.15
  281.7 7.3 %convolution_bitcast_fusion = f32[768,768]{1,0:T(8,128)S(1)} fusion(bf16[8,512,768]{2,1,0:T(8,128)(2,1)S(1)} %copy-done.1, bf16[8,512,768]{2,1,0:T(8,128)(2,1)} %get-tuple-element.128), kind=kOutput, calls=%fused_computation | convolution fusion | flops 4831838208 | bytes 14942208 | tf_op jit(solution)/shard_map/dot_general | solution.py:416
  289.1 1.4 collective-permute-start.13
  290.6 1.2 dynamic-slice_add_fusion.3.rest_0_
  291.7 51.6 %collective-permute-done.15.st_ref = f32[2,6,4,512]{3,2,1,0:T(4,128)S(1)} collective-permute-done((f32[2,6,4,512]{3,2,1,0:T(4,128)S(1)}, f32[2,6,4,512]{3,2,1,0:T(4,128)S(1)}, u32[]{:S(2)}, u32[]{:S(2)}) %collective-permute-start.15) | collective-permute-done | bytes 98336 | tf_op jit(solution)/shard_map/ppermute | solution.py:438
  343.3 1.3 collective-permute-start.11
  344.7 1.7 copy-done.3
  346.4 20.8 %late.5 = (bf16[8,512,768]{2,1,0:T(8,128)(2,1)}, bf16[8,512,768]{2,1,0:T(8,128)(2,1)}) custom-call(s32[1]{0:T(128)} %bitcast.1.role_ref, bf16[2,2,512,768]{3,2,1,0:T(8,128)(2,1)} %copy-done.3, bf16[2,2,512,768]{3,2,1,0:T(8,128)(2,1)} %copy-done.3, f32[2,6,4,512]{3,2,1,0:T(4,128)} %copy-done.19, ...), custom_call_target="tpu_custom_call", output_to_operand_aliasing={{0}: (8, {}), {1}: (9, {})} | custom-call | flops 6442450944 | bytes 15728640 | tf_op jit(solution)/shard_map/late/pallas_call | solution.py:278
  367.1 0.6 copy-done.18
  367.8 20.9 %late.6 = (bf16[8,512,768]{2,1,0:T(8,128)(2,1)}, bf16[8,512,768]{2,1,0:T(8,128)(2,1)}) custom-call(s32[1]{0:T(128)} %bitcast.1.role_ref, bf16[2,2,512,768]{3,2,1,0:T(8,128)(2,1)} %collective-permute-done.12.q_ref.g_ref, bf16[2,2,512,768]{3,2,1,0:T(8,128)(2,1)} %collective-permute-done.12.q_ref.g_ref, ...), custom_call_target="tpu_custom_call", output_to_operand_aliasing={{0}: (8, {}), {1}: (9, {})} | custom-call | flops 6442450944 | bytes 15728640 | tf_op jit(solution)/shard_map/late/pallas_call | solution.py:278
  389.3 20.8 %late.7 = (bf16[8,512,768]{2,1,0:T(8,128)(2,1)}, bf16[8,512,768]{2,1,0:T(8,128)(2,1)}) custom-call(s32[1]{0:T(128)} %bitcast.1.role_ref, bf16[2,2,512,768]{3,2,1,0:T(8,128)(2,1)} %collective-permute-done.10.q_ref.g_ref, bf16[2,2,512,768]{3,2,1,0:T(8,128)(2,1)} %collective-permute-done.10.q_ref.g_ref, ...), custom_call_target="tpu_custom_call", output_to_operand_aliasing={{0}: (8, {}), {1}: (9, {})} | custom-call | flops 6442450944 | bytes 15728640 | tf_op jit(solution)/shard_map/late/pallas_call | solution.py:278
  410.1 7.3 %convolution_bitcast_fusion.1 = f32[768,768]{1,0:T(8,128)S(1)} fusion(bf16[8,512,768]{2,1,0:T(8,128)(2,1)} %get-tuple-element.129.dv_ref, bf16[8,512,768]{2,1,0:T(8,128)(2,1)S(1)} %bitcast.42), kind=kOutput, calls=%fused_computation.1 | convolution fusion | flops 4831838208 | bytes 14942208 | tf_op jit(solution)/shard_map/dot_general | solution.py:416
  417.7 7.4 %convolution_bitcast_fusion.2 = f32[768,768]{1,0:T(8,128)S(1)} fusion(bf16[8,512,768]{2,1,0:T(8,128)(2,1)S(1)} %copy-done, bf16[8,512,768]{2,1,0:T(8,128)(2,1)} %get-tuple-element.128), kind=kOutput, calls=%fused_computation.2 | convolution fusion | flops 4831838208 | bytes 14942208 | tf_op jit(solution)/shard_map/dot_general | solution.py:416
  426.7 1.4 dynamic-slice_add_fusion
  428.1 1.6 collective-permute-start.24
  429.7 1.2 dynamic-slice_add_fusion.1.rest_1_
  430.9 1.2 dynamic-slice_add_fusion.2.rest_0_
  432.0 30.3 %back.1 = (bf16[16,256,768]{2,1,0:T(8,128)(2,1)}, bf16[8,256,768]{2,1,0:T(8,128)(2,1)}, f32[8,768]{1,0:T(8,128)}) custom-call(s32[1]{0:T(128)} %bitcast.core_ref, bf16[8,512,768]{2,1,0:T(8,128)(2,1)} %get-tuple-element.132.dq_ref, bf16[8,512,768]{2,1,0:T(8,128)(2,1)} %get-tuple-element.127.dk_ref, bf16[8,512,768]{2,1,0:T(8,128)(2,1)} %get-tuple-element.129.dv_ref, ...), custom_call_target="tpu_custom_call" | custom-call | flops 14495514624 | bytes 37748736 | tf_op jit(solution)/shard_map/back/pallas_call | solution.py:361
  462.4 12.3 %post.1 = (bf16[16,256,768]{2,1,0:T(8,128)(2,1)}, bf16[8,256,768]{2,1,0:T(8,128)(2,1)}) custom-call(s32[1]{0:T(128)} %bitcast.core_ref, bf16[8,512,768]{2,1,0:T(8,128)(2,1)} %get-tuple-element.109.a_ref, bf16[8,512,768]{2,1,0:T(8,128)(2,1)} %get-tuple-element.110.x_ref, bf16[768,768]{1,0:T(8,128)(2,1)} %bitcast.39, f32[1,768]{1,0:T(1,128)} %reshape.50.bo_ref, ...), custom_call_target="tpu_custom_call" | custom-call | flops 4831838208 | bytes 18874368 | tf_op jit(solution)/shard_map/post/pallas_call | solution.py:318
  475.0 0.7 collective-permute-start.26
  475.7 4.7 collective-permute-done.24
  481.0 24.6 %collective-permute-done.26 = f32[384,768]{1,0:T(8,128)S(1)} collective-permute-done((f32[384,768]{1,0:T(8,128)S(1)}, f32[384,768]{1,0:T(8,128)S(1)}, u32[]{:S(2)}, u32[]{:S(2)}) %collective-permute-start.26) | collective-permute-done | bytes 1179680 | tf_op jit(solution)/shard_map/ppermute | solution.py:438
  506.0 24.3 %collective-permute-done.25 = f32[384,768]{1,0:T(8,128)S(1)} collective-permute-done((f32[384,768]{1,0:T(8,128)S(1)}, f32[384,768]{1,0:T(8,128)S(1)}, u32[]{:S(2)}, u32[]{:S(2)}) %collective-permute-start.25) | collective-permute-done | bytes 1179680 | tf_op jit(solution)/shard_map/ppermute | solution.py:438
  530.3 1.2 add.70.refs_1_
  532.0 1.0 copy-done.13
  533.6 0.7 reshape.51
  534.3 1.5 slice_reduce_fusion
  535.8 0.7 collective-permute-done.29.refs_5_
  536.5 1.0 copy-done.14
  537.5 8.9 %join.1 = (f32[3,2,384,768]{3,2,1,0:T(8,128)}, f32[2,384,768]{2,1,0:T(8,128)}) custom-call(s32[1]{0:T(128)} %bitcast.core_ref, f32[384,768]{1,0:T(8,128)} %copy-done.7, f32[384,768]{1,0:T(8,128)} %add.70.refs_1_, f32[384,768]{1,0:T(8,128)} %copy-done.8, f32[384,768]{1,0:T(8,128)} %copy-done.6, f32[384,768]{1,0:T(8,128)} %collective-permute-done.28.refs_4_, ...), custom_call_target="tpu_custom_call" | custom-call | flops 2359296 | bytes 18874368 | tf_op jit(solution)/shard_map/join/pallas_call | solution.py:396
  546.4 3.8 constant_dynamic-update-slice_fusion
  550.2 3.8 constant_dynamic-update-slice_fusion.1
  (115 shorter events, 7.7 us)
Async XLA Ops:
  2.5 8.8 %copy-start.21 = (f32[3,12,64]{2,1,0:T(8,128)S(1)}, f32[3,12,64]{2,1,0:T(8,128)}, u32[]{:S(2)}) copy-start(f32[3,12,64]{2,1,0:T(8,128)} %param.13) | copy-start | bytes 27652
  2.5 9.4 %copy-start.23 = (f32[768]{0:T(1024)S(1)}, f32[768]{0:T(1024)}, u32[]{:S(2)}) copy-start(f32[768]{0:T(1024)} %param.10) | copy-start | bytes 9220
  2.5 10.0 %copy-start.24 = (f32[768]{0:T(1024)S(1)}, f32[768]{0:T(1024)}, u32[]{:S(2)}) copy-start(f32[768]{0:T(1024)} %param.11) | copy-start | bytes 9220
  2.5 29.9 %collective-permute-start = (bf16[6,256,768]{2,1,0:T(8,128)(2,1)S(1)}, bf16[6,256,768]{2,1,0:T(8,128)(2,1)}, u32[]{:S(2)}, u32[]{:S(2)}) collective-permute-start(bf16[6,256,768]{2,1,0:T(8,128)(2,1)S(1)} %constant_dynamic-slice_fusion.7), channel_id=1, source_target_pairs={{0,1},{1,0},{2,3},{3,2},{4,5},{5,4},{6,7},{7,6}} | collective-permute-start | bytes 7077896 | tf_op jit(solution)/shard_map/ppermute | solution.py:438
  6.6 25.8 %collective-permute-start.1 = (bf16[6,256,768]{2,1,0:T(8,128)(2,1)}, bf16[6,256,768]{2,1,0:T(8,128)(2,1)}, u32[]{:S(2)}, u32[]{:S(2)}) collective-permute-start(bf16[6,256,768]{2,1,0:T(8,128)(2,1)} %constant_dynamic-slice_fusion.6), channel_id=1, source_target_pairs={{0,1},{1,0},{2,3},{3,2},{4,5},{5,4},{6,7},{7,6}} | collective-permute-start | bytes 7077896 | tf_op jit(solution)/shard_map/ppermute | solution.py:438
  8.7 4.4 collective-permute-start.2
  11.2 2.6 collective-permute-start.3
  13.1 0.9 copy-start.15
  25.0 41.1 %collective-permute-start.7 = (bf16[2,512,768]{2,1,0:T(8,128)(2,1)}, bf16[2,512,768]{2,1,0:T(8,128)(2,1)}, u32[]{:S(2)}, u32[]{:S(2)}) collective-permute-start(bf16[2,512,768]{2,1,0:T(8,128)(2,1)} %get-tuple-element.89), channel_id=1, source_target_pairs={{0,2},{1,3},{4,6},{5,7}} | collective-permute-start | bytes 4718600 | tf_op jit(solution)/shard_map/ppermute | solution.py:438
  31.1 184.4 %collective-permute-start.8 = (bf16[2,2,512,768]{3,2,1,0:T(8,128)(2,1)}, bf16[2,2,512,768]{3,2,1,0:T(8,128)(2,1)S(1)}, u32[]{:S(2)}, u32[]{:S(2)}) collective-permute-start(bf16[2,2,512,768]{3,2,1,0:T(8,128)(2,1)} %get-tuple-element.86.refs_0_.refs_1_), channel_id=1, source_target_pairs={{2,0},{3,1},{6,4},{7,5}} | collective-permute-start | bytes 9437192 | tf_op jit(solution)/shard_map/ppermute | solution.py:438
  58.6 75.5 %collective-permute-start.6 = (bf16[2,512,768]{2,1,0:T(8,128)(2,1)S(1)}, bf16[2,512,768]{2,1,0:T(8,128)(2,1)S(1)}, u32[]{:S(2)}, u32[]{:S(2)}) collective-permute-start(bf16[2,512,768]{2,1,0:T(8,128)(2,1)S(1)} %get-tuple-element.144), channel_id=1, source_target_pairs={{0,2},{1,3},{4,6},{5,7}} | collective-permute-start | bytes 4718600 | tf_op jit(solution)/shard_map/ppermute | solution.py:438
  63.5 109.5 %collective-permute-start.5 = (bf16[2,512,768]{2,1,0:T(8,128)(2,1)}, bf16[2,512,768]{2,1,0:T(8,128)(2,1)}, u32[]{:S(2)}, u32[]{:S(2)}) collective-permute-start(bf16[2,512,768]{2,1,0:T(8,128)(2,1)} %get-tuple-element.145), channel_id=1, source_target_pairs={{0,2},{1,3},{4,6},{5,7}} | collective-permute-start | bytes 4718600 | tf_op jit(solution)/shard_map/ppermute | solution.py:438
  102.1 113.4 %collective-permute-start.9 = (f32[2,6,4,512]{3,2,1,0:T(4,128)}, f32[2,6,4,512]{3,2,1,0:T(4,128)S(1)}, u32[]{:S(2)}, u32[]{:S(2)}) collective-permute-start(f32[2,6,4,512]{3,2,1,0:T(4,128)} %get-tuple-element.102), channel_id=1, source_target_pairs={{2,0},{3,1},{6,4},{7,5}} | collective-permute-start | bytes 294920 | tf_op jit(solution)/shard_map/ppermute | solution.py:438
  103.4 107.2 %collective-permute-start.4 = (bf16[2,512,768]{2,1,0:T(8,128)(2,1)S(1)}, bf16[2,512,768]{2,1,0:T(8,128)(2,1)}, u32[]{:S(2)}, u32[]{:S(2)}) collective-permute-start(bf16[2,512,768]{2,1,0:T(8,128)(2,1)S(1)} %get-tuple-element.146), channel_id=1, source_target_pairs={{0,2},{1,3},{4,6},{5,7}} | collective-permute-start | bytes 4718600 | tf_op jit(solution)/shard_map/ppermute | solution.py:438
  134.1 1.1 copy-start.26
  135.2 209.3 %collective-permute-start.14 = (bf16[2,2,512,768]{3,2,1,0:T(8,128)(2,1)}, bf16[2,2,512,768]{3,2,1,0:T(8,128)(2,1)S(1)}, u32[]{:S(2)}, u32[]{:S(2)}) collective-permute-start(bf16[2,2,512,768]{3,2,1,0:T(8,128)(2,1)} %get-tuple-element.141), channel_id=1, source_target_pairs={{2,0},{3,1},{6,4},{7,5}} | collective-permute-start | bytes 9437192 | tf_op jit(solution)/shard_map/ppermute | solution.py:438
  173.0 194.2 %collective-permute-start.12 = (bf16[2,2,512,768]{3,2,1,0:T(8,128)(2,1)}, bf16[2,2,512,768]{3,2,1,0:T(8,128)(2,1)}, u32[]{:S(2)}, u32[]{:S(2)}) collective-permute-start(bf16[2,2,512,768]{3,2,1,0:T(8,128)(2,1)} %get-tuple-element.142), channel_id=1, source_target_pairs={{2,0},{3,1},{6,4},{7,5}} | collective-permute-start | bytes 9437192 | tf_op jit(solution)/shard_map/ppermute | solution.py:438
  210.7 178.0 %collective-permute-start.10 = (bf16[2,2,512,768]{3,2,1,0:T(8,128)(2,1)}, bf16[2,2,512,768]{3,2,1,0:T(8,128)(2,1)}, u32[]{:S(2)}, u32[]{:S(2)}) collective-permute-start(bf16[2,2,512,768]{3,2,1,0:T(8,128)(2,1)} %get-tuple-element.143), channel_id=1, source_target_pairs={{2,0},{3,1},{6,4},{7,5}} | collective-permute-start | bytes 9437192 | tf_op jit(solution)/shard_map/ppermute | solution.py:438
  215.5 0.6 copy-start.16
  215.5 1.6 copy-start.2
  270.8 9.4 %copy-start.27 = (f32[2,6,4,512]{3,2,1,0:T(4,128)S(1)}, f32[2,6,4,512]{3,2,1,0:T(4,128)}, u32[]{:S(2)}) copy-start(f32[2,6,4,512]{3,2,1,0:T(4,128)} %get-tuple-element.117) | copy-start | bytes 294916
  270.8 10.8 %copy-start.1 = (bf16[8,512,768]{2,1,0:T(8,128)(2,1)S(1)}, bf16[8,512,768]{2,1,0:T(8,128)(2,1)}, u32[]{:S(2)}) copy-start(bf16[8,512,768]{2,1,0:T(8,128)(2,1)} %get-tuple-element.132.dq_ref) | copy-start | bytes 18874372
  280.0 10.5 %copy-start.5 = (f32[768,768]{1,0:T(8,128)}, f32[768,768]{1,0:T(8,128)S(1)}, u32[]{:S(2)}) copy-start(f32[768,768]{1,0:T(8,128)S(1)} %convolution_bitcast_fusion.3.rest_0_) | copy-start | bytes 7077892
  280.1 9.0 %collective-permute-start.16 = (f32[384,768]{1,0:T(8,128)S(1)}, f32[384,768]{1,0:T(8,128)S(1)}, u32[]{:S(2)}, u32[]{:S(2)}) collective-permute-start(f32[384,768]{1,0:T(8,128)S(1)} %constant_dynamic-slice_fusion.3), channel_id=1, source_target_pairs={{0,1},{1,0},{2,3},{3,2},{4,5},{5,4},{6,7},{7,6}} | collective-permute-start | bytes 3538952 | tf_op jit(solution)/shard_map/ppermute | solution.py:438
  280.2 63.1 %collective-permute-start.15 = (f32[2,6,4,512]{3,2,1,0:T(4,128)S(1)}, f32[2,6,4,512]{3,2,1,0:T(4,128)S(1)}, u32[]{:S(2)}, u32[]{:S(2)}) collective-permute-start(f32[2,6,4,512]{3,2,1,0:T(4,128)S(1)} %copy-done.27), channel_id=1, source_target_pairs={{2,0},{3,1},{6,4},{7,5}} | collective-permute-start | bytes 294920 | tf_op jit(solution)/shard_map/ppermute | solution.py:438
  281.6 7.5 %copy-start.28 = (f32[2,6,4,512]{3,2,1,0:T(4,128)S(1)}, f32[2,6,4,512]{3,2,1,0:T(4,128)}, u32[]{:S(2)}) copy-start(f32[2,6,4,512]{3,2,1,0:T(4,128)} %get-tuple-element.114) | copy-start | bytes 294916
  289.0 55.6 %copy-start.11 = (f32[768,768]{1,0:T(8,128)}, f32[768,768]{1,0:T(8,128)S(1)}, u32[]{:S(2)}) copy-start(f32[768,768]{1,0:T(8,128)S(1)} %convolution_bitcast_fusion) | copy-start | bytes 7077892
  289.0 54.3 %copy-start.29 = (f32[2,6,4,512]{3,2,1,0:T(4,128)S(1)}, f32[2,6,4,512]{3,2,1,0:T(4,128)}, u32[]{:S(2)}) copy-start(f32[2,6,4,512]{3,2,1,0:T(4,128)} %get-tuple-element.111) | copy-start | bytes 294916
  289.1 78.0 %collective-permute-start.13 = (f32[2,6,4,512]{3,2,1,0:T(4,128)S(1)}, f32[2,6,4,512]{3,2,1,0:T(4,128)S(1)}, u32[]{:S(2)}, u32[]{:S(2)}) collective-permute-start(f32[2,6,4,512]{3,2,1,0:T(4,128)S(1)} %copy-done.28), channel_id=1, source_target_pairs={{2,0},{3,1},{6,4},{7,5}} | collective-permute-start | bytes 294920 | tf_op jit(solution)/shard_map/ppermute | solution.py:438
  343.3 1.4 copy-start.19
  343.3 45.3 %collective-permute-start.11 = (f32[2,6,4,512]{3,2,1,0:T(4,128)S(1)}, f32[2,6,4,512]{3,2,1,0:T(4,128)S(1)}, u32[]{:S(2)}, u32[]{:S(2)}) collective-permute-start(f32[2,6,4,512]{3,2,1,0:T(4,128)S(1)} %copy-done.29), channel_id=1, source_target_pairs={{2,0},{3,1},{6,4},{7,5}} | collective-permute-start | bytes 294920 | tf_op jit(solution)/shard_map/ppermute | solution.py:438
  344.6 1.7 copy-start.3
  344.6 81.6 %collective-permute-start.23 = (f32[384,768]{1,0:T(8,128)S(1)}, f32[384,768]{1,0:T(8,128)}, u32[]{:S(2)}, u32[]{:S(2)}) collective-permute-start(f32[384,768]{1,0:T(8,128)S(1)} %constant_dynamic-slice_fusion), channel_id=1, source_target_pairs={{0,1},{1,0},{2,3},{3,2},{4,5},{5,4},{6,7},{7,6}} | collective-permute-start | bytes 3538952 | tf_op jit(solution)/shard_map/ppermute | solution.py:438
  367.1 0.6 copy-start.18
  367.8 42.4 %slice-start = ((s8[6291456]{0:T(1024)(128)(4,1)}), s8[4194304]{0:T(1024)(128)(4,1)S(1)}, s32[]{:S(2)}) async-start(s8[6291456]{0:T(1024)(128)(4,1)} %bitcast.41), calls=%async_computation | async-start | bytes 8388608
  388.6 0.6 copy-start.17
  389.3 20.9 %slice-start.1 = ((s8[6291456]{0:T(1024)(128)(4,1)}), s8[2097152]{0:T(1024)(128)(4,1)S(1)}, s32[]{:S(2)}) async-start(s8[6291456]{0:T(1024)(128)(4,1)} %bitcast.41), calls=%async_computation.1 | async-start | bytes 4194304
  410.1 7.5 %copy-start = (bf16[8,512,768]{2,1,0:T(8,128)(2,1)S(1)}, bf16[8,512,768]{2,1,0:T(8,128)(2,1)}, u32[]{:S(2)}) copy-start(bf16[8,512,768]{2,1,0:T(8,128)(2,1)} %get-tuple-element.127.dk_ref) | copy-start | bytes 18874372
  417.6 12.1 %collective-permute-start.18 = (f32[384,768]{1,0:T(8,128)S(1)}, f32[384,768]{1,0:T(8,128)S(1)}, u32[]{:S(2)}, u32[]{:S(2)}) collective-permute-start(f32[384,768]{1,0:T(8,128)S(1)} %constant_dynamic-slice_fusion.1), channel_id=1, source_target_pairs={{0,1},{1,0},{2,3},{3,2},{4,5},{5,4},{6,7},{7,6}} | collective-permute-start | bytes 3538952 | tf_op jit(solution)/shard_map/ppermute | solution.py:438
  417.6 8.0 %copy-start.25 = (f32[768]{0:T(1024)S(1)}, f32[768]{0:T(1024)}, u32[]{:S(2)}) copy-start(f32[768]{0:T(1024)} %param.15) | copy-start | bytes 9220
  417.6 8.6 %copy-start.4 = (f32[384,768]{1,0:T(8,128)S(1)}, f32[384,768]{1,0:T(8,128)}, u32[]{:S(2)}) copy-start(f32[384,768]{1,0:T(8,128)} %dynamic-slice_add_fusion.3.rest_0_) | copy-start | bytes 3538948
  425.1 1.7 copy-start.12
  425.2 5.7 %collective-permute-start.17 = (f32[384,768]{1,0:T(8,128)S(1)}, f32[384,768]{1,0:T(8,128)S(1)}, u32[]{:S(2)}, u32[]{:S(2)}) collective-permute-start(f32[384,768]{1,0:T(8,128)S(1)} %constant_dynamic-slice_fusion.2), channel_id=1, source_target_pairs={{0,1},{1,0},{2,3},{3,2},{4,5},{5,4},{6,7},{7,6}} | collective-permute-start | bytes 3538952 | tf_op jit(solution)/shard_map/ppermute | solution.py:438
  426.2 49.5 %collective-permute-start.27 = (f32[384,768]{1,0:T(8,128)S(1)}, f32[384,768]{1,0:T(8,128)S(1)}, u32[]{:S(2)}, u32[]{:S(2)}) collective-permute-start(f32[384,768]{1,0:T(8,128)S(1)} %copy-done.4), channel_id=1, source_target_pairs={{0,2},{1,3},{2,0},{3,1},{4,6},{5,7},{6,4},{7,5}} | collective-permute-start | bytes 3538952 | tf_op jit(solution)/shard_map/ppermute | solution.py:438
  428.1 52.2 %collective-permute-start.24 = (f32[384,768]{1,0:T(8,128)S(1)}, f32[384,768]{1,0:T(8,128)S(1)}, u32[]{:S(2)}, u32[]{:S(2)}) collective-permute-start(f32[384,768]{1,0:T(8,128)S(1)} %dynamic-slice_add_fusion), channel_id=1, source_target_pairs={{0,2},{1,3},{2,0},{3,1},{4,6},{5,7},{6,4},{7,5}} | collective-permute-start | bytes 3538952 | tf_op jit(solution)/shard_map/ppermute | solution.py:438
  462.3 12.7 %copy-start.10 = (f32[384,768]{1,0:T(8,128)S(1)}, f32[384,768]{1,0:T(8,128)}, u32[]{:S(2)}) copy-start(f32[384,768]{1,0:T(8,128)} %dynamic-slice_add_fusion.1.rest_1_) | copy-start | bytes 3538948
  462.3 13.4 %copy-start.22 = (f32[8,768]{1,0:T(8,128)S(1)}, f32[8,768]{1,0:T(8,128)}, u32[]{:S(2)}) copy-start(f32[8,768]{1,0:T(8,128)} %get-tuple-element.135) | copy-start | bytes 73732
  462.3 18.0 %copy-start.9 = (f32[384,768]{1,0:T(8,128)S(1)}, f32[384,768]{1,0:T(8,128)}, u32[]{:S(2)}) copy-start(f32[384,768]{1,0:T(8,128)} %dynamic-slice_add_fusion.2.rest_0_) | copy-start | bytes 3538948
  462.4 84.1 %collective-permute-start.20 = (bf16[8,256,768]{2,1,0:T(8,128)(2,1)}, bf16[8,256,768]{2,1,0:T(8,128)(2,1)}, u32[]{:S(2)}, u32[]{:S(2)}) collective-permute-start(bf16[8,256,768]{2,1,0:T(8,128)(2,1)} %get-tuple-element.134), channel_id=1, source_target_pairs={{0,1},{1,0},{2,3},{3,2},{4,5},{5,4},{6,7},{7,6}} | collective-permute-start | bytes 9437192 | tf_op jit(solution)/shard_map/ppermute | solution.py:438
  474.7 75.5 %collective-permute-start.19 = (bf16[8,256,768]{2,1,0:T(8,128)(2,1)}, bf16[8,256,768]{2,1,0:T(8,128)(2,1)}, u32[]{:S(2)}, u32[]{:S(2)}) collective-permute-start(bf16[8,256,768]{2,1,0:T(8,128)(2,1)} %get-tuple-element.131), channel_id=1, source_target_pairs={{0,1},{1,0},{2,3},{3,2},{4,5},{5,4},{6,7},{7,6}} | collective-permute-start | bytes 9437192 | tf_op jit(solution)/shard_map/ppermute | solution.py:438
  475.0 30.6 %collective-permute-start.26 = (f32[384,768]{1,0:T(8,128)S(1)}, f32[384,768]{1,0:T(8,128)S(1)}, u32[]{:S(2)}, u32[]{:S(2)}) collective-permute-start(f32[384,768]{1,0:T(8,128)S(1)} %copy-done.10), channel_id=1, source_target_pairs={{0,2},{1,3},{2,0},{3,1},{4,6},{5,7},{6,4},{7,5}} | collective-permute-start | bytes 3538952 | tf_op jit(solution)/shard_map/ppermute | solution.py:438
  475.7 5.0 collective-permute-start.21
  480.3 49.9 %collective-permute-start.25 = (f32[384,768]{1,0:T(8,128)S(1)}, f32[384,768]{1,0:T(8,128)S(1)}, u32[]{:S(2)}, u32[]{:S(2)}) collective-permute-start(f32[384,768]{1,0:T(8,128)S(1)} %copy-done.9), channel_id=1, source_target_pairs={{0,2},{1,3},{2,0},{3,1},{4,6},{5,7},{6,4},{7,5}} | collective-permute-start | bytes 3538952 | tf_op jit(solution)/shard_map/ppermute | solution.py:438
  480.5 25.4 %copy-start.6 = (f32[384,768]{1,0:T(8,128)}, f32[384,768]{1,0:T(8,128)S(1)}, u32[]{:S(2)}) copy-start(f32[384,768]{1,0:T(8,128)S(1)} %add.72.refs_3_) | copy-start | bytes 3538948
  480.7 51.3 %collective-permute-start.31 = (f32[384,768]{1,0:T(8,128)S(1)}, f32[384,768]{1,0:T(8,128)S(1)}, u32[]{:S(2)}, u32[]{:S(2)}) collective-permute-start(f32[384,768]{1,0:T(8,128)S(1)} %add.72.refs_3_), channel_id=1, source_target_pairs={{0,1},{1,0},{2,3},{3,2},{4,5},{5,4},{6,7},{7,6}} | collective-permute-start | bytes 3538952 | tf_op jit(solution)/shard_map/ppermute | solution.py:438
  505.6 25.8 %collective-permute-start.22 = (f32[8,768]{1,0:T(8,128)S(1)}, f32[8,768]{1,0:T(8,128)S(1)}, u32[]{:S(2)}, u32[]{:S(2)}) collective-permute-start(f32[8,768]{1,0:T(8,128)S(1)} %add.66), channel_id=1, source_target_pairs={{0,2},{1,3},{2,0},{3,1},{4,6},{5,7},{6,4},{7,5}} | collective-permute-start | bytes 73736 | tf_op jit(solution)/shard_map/ppermute | solution.py:438
  505.8 25.7 %copy-start.7 = (f32[384,768]{1,0:T(8,128)}, f32[384,768]{1,0:T(8,128)S(1)}, u32[]{:S(2)}) copy-start(f32[384,768]{1,0:T(8,128)S(1)} %add.69.refs_0_) | copy-start | bytes 3538948
  506.0 30.5 %copy-start.8 = (f32[384,768]{1,0:T(8,128)}, f32[384,768]{1,0:T(8,128)S(1)}, u32[]{:S(2)}) copy-start(f32[384,768]{1,0:T(8,128)S(1)} %add.71.refs_2_) | copy-start | bytes 3538948
  530.2 5.6 %collective-permute-start.28 = (f32[384,768]{1,0:T(8,128)S(1)}, f32[384,768]{1,0:T(8,128)}, u32[]{:S(2)}, u32[]{:S(2)}) collective-permute-start(f32[384,768]{1,0:T(8,128)S(1)} %add.69.refs_0_), channel_id=1, source_target_pairs={{0,1},{1,0},{2,3},{3,2},{4,5},{5,4},{6,7},{7,6}} | collective-permute-start | bytes 3538952 | tf_op jit(solution)/shard_map/ppermute | solution.py:438
  531.5 4.4 collective-permute-start.30
  532.0 1.0 copy-start.13
  533.0 3.5 collective-permute-start.29
  533.0 0.6 copy-start.20
  536.5 1.0 copy-start.14
